TPU v7x, 32 devices: a whole 2x2x4 slice. The times are simulated.
32 devices in a mesh: dp: 16 (over z, y, core), tp: 2 (over x).
Axes of the slice: x: 2, y: 2, z: 4, core: 2. Of those that a mesh axis runs over, the one named last changes fastest.
Arguments:
- activations: bfloat16 [2048, 2304], P('dp'), may hold values from -6 to 6
- out_grads: bfloat16 [2048, 2048], P('dp', 'tp'), may hold values from -6 to 6
- right_prev: float32 [2048, 128], P('tp'), may hold values from -6 to 6
Outputs:
- update: float32 [2304, 2048], P('dp', 'tp')
- residual: bfloat16 [36864, 2048], P('dp', 'tp')
All inputs are finite; a program needn't handle non-finite values.
Results may differ from a plain program's by a relative error of at most 0.001.
Values sent between devices are 32-bit elements; how exact they have to be, the bound alone decides.
No kernel may reach another device: no remote copies, remote signals or barrier semaphores. Data moves between devices by JAX's collectives and lax.ppermute only.
A program may use at most 64 MiB of HBM per device.

v0:
```python
import functools

import jax
import jax.numpy as jnp
from jax import lax
from jax.experimental import pallas as pl
from jax.experimental.pallas import tpu as pltpu
from jax.sharding import PartitionSpec as P

HI = lax.Precision.HIGHEST


def factors_of(count):
    found, divisor = [], 2
    while count > 1:
        while count % divisor == 0:
            found.append(divisor)
            count //= divisor
        divisor += 1
    return found


def stages_of(axis):
    radices = []
    for factor in factors_of(lax.axis_size(axis)):
        if len(radices) > 1 and radices[-1] * factor <= 4:
            radices[-1] *= factor
        else:
            radices.append(factor)
    stages, stride = [], 1
    for radix in radices:
        stages.append((radix, stride))
        stride *= radix
    return stages


def partner(digit, step, radix):
    return digit ^ step if radix & (radix - 1) == 0 else (digit + step) % radix


def source(digit, step, radix):
    return digit ^ step if radix & (radix - 1) == 0 else (digit + radix - step) % radix


def shifted(value, axis, radix, stride, step):
    pairs = []
    for index in range(lax.axis_size(axis)):
        digit = index // stride % radix
        pairs.append((index, index + (partner(digit, step, radix) - digit) * stride))
    return lax.ppermute(value, axis, pairs)


def scatter_sum(value, axis):
    position = lax.axis_index(axis)
    for radix, stride in stages_of(axis):
        digit = position // stride % radix
        rows = value.shape[0] // radix
        received = []
        for step in range(1, radix):
            block = lax.dynamic_slice_in_dim(value, partner(digit, step, radix) * rows, rows, 0)
            received.append(shifted(block, axis, radix, stride, step))
        value = lax.dynamic_slice_in_dim(value, digit * rows, rows, 0)
        for block in received:
            value = value + block
    return value


def gather_rows(value, axis):
    position = lax.axis_index(axis)
    for radix, stride in reversed(stages_of(axis)):
        digit = position // stride % radix
        rows = value.shape[0]
        whole = jnp.zeros((radix * rows, value.shape[1]), value.dtype)
        received = [shifted(value, axis, radix, stride, step) for step in range(1, radix)]
        whole = lax.dynamic_update_slice_in_dim(whole, value, digit * rows, 0)
        for step, block in enumerate(received, 1):
            whole = lax.dynamic_update_slice_in_dim(whole, block, source(digit, step, radix) * rows, 0)
        value = whole
    return value


def padded_rows(value, multiple):
    extra = -value.shape[0] % multiple
    return jnp.pad(value, ((0, extra), (0, 0))) if extra else value


def inverse_factor_body(first, last, width, state_ref, out_ref):
    size = state_ref.shape[0]
    row = lax.broadcasted_iota(jnp.int32, (size, size), 0)
    column = lax.broadcasted_iota(jnp.int32, (size, size), 1)
    state = state_ref[...]
    if first == 0:
        diagonal = jnp.where(row == column, state, 0.0)
        ridge = 1e-06 * jnp.sum(diagonal) / size
        state = state + jnp.where(row == column, ridge, 0.0)
    out_ref[...] = state
    sub = lax.broadcasted_iota(jnp.int32, (width, size), 0)
    lane = lax.broadcasted_iota(jnp.int32, (width, size), 1)

    def spread(block, index):
        return jnp.broadcast_to(block[index : index + 1, :], (width, size))

    for start in range(first, last, width):
        stop = start + width
        block = out_ref[start:stop, :]
        columns = [
            jnp.broadcast_to(block[:, start + k : start + k + 1], (width, size)) for k in range(width)
        ]
        pivots = jnp.ones((width, size), jnp.float32)
        for j in range(width):
            pivot = spread(columns[j], j)
            pivots = jnp.where(sub == j, pivot, pivots)
            ratio = jnp.where(sub > j, columns[j] / pivot, 0.0)
            for k in range(width):
                if k != j:
                    columns[k] = columns[k] - ratio * spread(columns[k], j)
            columns[j] = jnp.where(sub == j, 1.0, -ratio)
        scale = 1.0 / jnp.sqrt(pivots)
        inside = (lane >= start) & (lane < stop)
        lead = jnp.where(inside, jnp.where(lane - start == sub, 1.0, 0.0), block)
        rows = columns[0] * spread(lead, 0)
        for k in range(1, width):
            rows = rows + columns[k] * spread(lead, k)
        rows = rows * scale
        out_ref[start:stop, :] = rows
        if stop < size:
            trail = jnp.where(lane >= stop, rows, 0.0)
            change = lax.dot_general(trail, rows, (((0,), (0,)), ((), ())), precision=HI, preferred_element_type=jnp.float32)
            rest = out_ref[stop:, :]
            hit = (column[stop:] >= start) & (column[stop:] < stop)
            out_ref[stop:, :] = jnp.where(hit, 0.0, rest) - change[stop:]
    if last == size:
        out_ref[...] = jnp.where(row >= column, out_ref[...], 0.0)


def inverse_factor(gram, pieces=2, width=16):
    size = gram.shape[0]
    state = gram
    for piece in range(pieces):
        first, last = size * piece // pieces, size * (piece + 1) // pieces
        call = pl.pallas_call(
            functools.partial(inverse_factor_body, first, last, width),
            out_shape=jax.ShapeDtypeStruct(gram.shape, jnp.float32),
            in_specs=[pl.BlockSpec(memory_space=pltpu.VMEM)],
            out_specs=pl.BlockSpec(memory_space=pltpu.VMEM),
            compiler_params=grant(4),
            cost_estimate=cost(3),
        )
        state = call(state)
    return state


def vmem(count):
    return [pl.BlockSpec(memory_space=pltpu.VMEM)] * count


SMEM = pl.BlockSpec(memory_space=pltpu.SMEM)


def grant(mebibytes, **more):
    return pltpu.CompilerParams(vmem_limit_bytes=mebibytes << 20, **more)


def cost(microseconds):
    return pl.CostEstimate(flops=int(microseconds * 1e9), bytes_accessed=1 << 17, transcendentals=0)


def terms_in_kernel(value, count):
    terms = []
    for _ in range(count):
        top = value.astype(jnp.bfloat16)
        terms.append(top)
        value = value - top.astype(jnp.float32)
    return terms


def exact_dot(narrow, wide, contract):
    dims = ((contract[:1], contract[1:]), ((), ()))
    total = None
    for term in reversed(terms_in_kernel(wide, 3)):
        part = lax.dot_general(narrow, term, dims, preferred_element_type=jnp.float32)
        total = part if total is None else total + part
    return total


def nt_dot(left, right):
    dims = (((1,), (1,)), ((), ()))
    return lax.dot_general(left, right, dims, precision=HI, preferred_element_type=jnp.float32)


def project_body(grads_ref, right_ref, out_ref):
    out_ref[...] = exact_dot(grads_ref[...], right_ref[...], (1, 0))


def project(out_grads, right_prev):
    return pl.pallas_call(
        project_body,
        out_shape=jax.ShapeDtypeStruct((out_grads.shape[0], right_prev.shape[1]), jnp.float32),
        in_specs=vmem(2),
        out_specs=vmem(1)[0],
        compiler_params=grant(12),
        name="project",
    )(out_grads, right_prev)


def apply_body(place_ref, tall_ref, *refs):
    total = refs[0][...]
    for ref in refs[1:-1]:
        total = total + ref[...]
    rows = refs[-1].shape[0]
    mine = pl.ds(pl.multiple_of(place_ref[0] * rows, rows), rows)
    refs[-1][...] = exact_dot(tall_ref[mine, :], total, (1, 0))


def apply(place, tall, rows, parts):
    return pl.pallas_call(
        apply_body,
        out_shape=jax.ShapeDtypeStruct((rows, parts[0].shape[1]), jnp.float32),
        in_specs=[SMEM] + vmem(1 + len(parts)),
        out_specs=vmem(1)[0],
        compiler_params=grant(12),
        name="apply",
    )(place, tall, *parts)


def weigh_body(place_ref, tall_ref, left_ref, out_ref):
    rows = left_ref.shape[0]
    mine = pl.ds(pl.multiple_of(place_ref[0] * rows, rows), rows)
    out_ref[...] = exact_dot(tall_ref[mine, :], left_ref[...], (0, 0))


def weigh(place, tall, left):
    return pl.pallas_call(
        weigh_body,
        out_shape=jax.ShapeDtypeStruct((tall.shape[1], left.shape[1]), jnp.float32),
        in_specs=[SMEM] + vmem(2),
        out_specs=vmem(1)[0],
        compiler_params=grant(12),
        name="weigh",
    )(place, tall, left)


def basis_body(place_ref, inverse_ref, acts_ref, *refs):
    out_ref, rank = refs[-1], inverse_ref.shape[0]
    tokens = acts_ref.shape[1]
    out_ref[:, :tokens] = acts_ref[...]
    for part, ref in enumerate(refs[:-1]):
        rows = ref.shape[0]
        top, low = terms_in_kernel(-nt_dot(ref[...], inverse_ref[...]), 2)
        where = pl.ds(pl.multiple_of(place_ref[part] * rows, rows), rows)
        for index, term in enumerate((top, low, top)):
            out_ref[where, tokens + index * rank : tokens + (index + 1) * rank] = term


def basis(places, inverse, acts, parts):
    columns = acts.shape[1] + 3 * inverse.shape[0]
    return pl.pallas_call(
        basis_body,
        out_shape=jax.ShapeDtypeStruct((acts.shape[0], columns), jnp.bfloat16),
        in_specs=[SMEM] + vmem(2 + len(parts)),
        out_specs=vmem(1)[0],
        compiler_params=grant(16),
        cost_estimate=cost(2),
        name="basis",
    )(places, inverse, acts, *parts)


def finish_body(replicas, mine_ref, tall_ref, grads_ref, sum_ref, inverse_ref, update_ref, residual_ref, wide):
    step, tile = pl.program_id(0), residual_ref.shape[0]
    tokens, rank = grads_ref.shape[0], inverse_ref.shape[0]

    @pl.when(step == 0)
    def _():
        right = nt_dot(inverse_ref[...], sum_ref[...]) * (1.0 / replicas)
        top, low = terms_in_kernel(right, 2)
        wide[:tokens, :] = grads_ref[...]
        for index, term in enumerate((top, top, low)):
            wide[tokens + index * rank : tokens + (index + 1) * rank, :] = term
        update_ref[...] = -jnp.dot(mine_ref[:, tokens:], wide[tokens:, :], preferred_element_type=jnp.float32)

    rows = pl.ds(pl.multiple_of(step * tile, tile), tile)
    residual = jnp.dot(tall_ref[rows, :], wide[...], preferred_element_type=jnp.float32)
    residual_ref[...] = residual.astype(jnp.bfloat16)


def finish(replicas, mine, tall, out_grads, right_sum, inverse):
    rows, columns = tall.shape[0], out_grads.shape[1]
    my_rows = mine.shape[0]
    tile = next(size for size in (384, 256, 192, 128, 96, 64, 32, 16, 8) if rows % size == 0)
    return pl.pallas_call(
        functools.partial(finish_body, replicas),
        grid=(rows // tile,),
        out_shape=(
            jax.ShapeDtypeStruct((my_rows, columns), jnp.float32),
            jax.ShapeDtypeStruct((rows, columns), jnp.bfloat16),
        ),
        in_specs=vmem(5),
        out_specs=(
            pl.BlockSpec((my_rows, columns), lambda i: (0, 0)),
            pl.BlockSpec((tile, columns), lambda i: (i, 0)),
        ),
        scratch_shapes=[pltpu.VMEM((tall.shape[1], columns), jnp.bfloat16)],
        compiler_params=grant(24, dimension_semantics=("arbitrary",)),
        name="finish",
    )(mine, tall, out_grads, right_sum, inverse)


def sent_all(value, axis):
    size, me = lax.axis_size(axis), lax.axis_index(axis)
    values, places = [value], [me]
    for step in range(1, size):
        values.append(shifted(value, axis, size, 1, step))
        places.append(source(me, step, size))
    return values, jnp.stack(places).astype(jnp.int32)


def per_device(activations, out_grads, right_prev):
    replicas, columns = lax.axis_size("dp"), lax.axis_size("tp")
    rows, my_columns = activations.shape[1], out_grads.shape[1]
    my_rows = rows // columns
    place = lax.axis_index("tp").astype(jnp.int32).reshape(1)
    origin = jnp.zeros((1,), jnp.int32)
    acts, grads = lax.optimization_barrier((activations.T, out_grads.T))

    projected, _ = sent_all(project(out_grads, right_prev), "tp")
    left_part = padded_rows(apply(place, acts, my_rows, projected), replicas)
    left_own = gather_rows(scatter_sum(left_part, "dp"), "dp")[:my_rows]

    weighted_own, left_own = lax.optimization_barrier((weigh(place, acts, left_own), left_own))
    weighted, _ = sent_all(weighted_own, "tp")
    gram = jnp.dot(left_own.T, left_own, precision=HI)
    grams, _ = sent_all(gram, "tp")
    gram = sum(grams[1:], grams[0])
    left_own, weighted[0] = lax.optimization_barrier((left_own, weighted[0]))
    right_part = padded_rows(apply(origin, grads, my_columns, weighted), replicas)
    right_sum = gather_rows(scatter_sum(right_part, "dp"), "dp")[:my_columns]

    parts, places = sent_all(left_own, "tp")
    inverse = inverse_factor(gram)
    tall = basis(places, inverse, acts, parts)
    rows_dev = rows // replicas
    mine = lax.dynamic_slice_in_dim(tall, lax.axis_index("dp") * rows_dev, rows_dev, 0)
    return finish(replicas, mine, tall, out_grads, right_sum, inverse)


def solution(mesh):
    in_specs = (P("dp", None), P("dp", "tp"), P("tp", None))
    out_specs = (P("dp", "tp"), P("dp", "tp"))
    return jax.shard_map(per_device, mesh=mesh, in_specs=in_specs, out_specs=out_specs, check_vma=False)
```

profile of v0, /device:TPU:0, one launch (start us, length us, event | category | flops | bytes accessed | tf_op | source)
XLA Modules:
  0.0 77.9 jit_solution(4732698000501474421)
XLA Ops:
  0.6 0.0 copy-start
  0.6 0.9 %copy-done = bf16[128,1024]{1,0:T(8,128)(2,1)S(1)} copy-done((bf16[128,1024]{1,0:T(8,128)(2,1)S(1)}, bf16[128,1024]{1,0:T(8,128)(2,1)}, u32[]{:S(2)}) %copy-start) | copy-done | bytes 262168
  1.6 1.0 %copy-done.2 = f32[1024,128]{1,0:T(8,128)S(1)} copy-done((f32[1024,128]{1,0:T(8,128)S(1)}, f32[1024,128]{1,0:T(8,128)}, u32[]{:S(2)}) %copy-start.2) | copy-done | bytes 524312
  2.6 0.4 project.1.refs_0_
  3.0 3.0 %collective-permute-start = (f32[128,128]{1,0:T(8,128)S(1)}, f32[128,128]{1,0:T(8,128)S(1)}, u32[]{:S(2)}, u32[]{:S(2)}) collective-permute-start(f32[128,128]{1,0:T(8,128)S(1)} %project.1.refs_0_), channel_id=1, source_target_pairs={{0,1},{1,0},{2,3},{3,2},{4,5},{5,4},{6,7},{7,6},{8,9},{9,8},{10,11... | collective-permute-start | bytes 196616 | tf_op jit(solution)/shard_map/ppermute | solution.py:50
  6.0 1.1 %copy.6 = bf16[128,1024]{0,1:T(8,128)(2,1)S(1)} copy(bf16[128,1024]{1,0:T(8,128)(2,1)} %grads_ref.3) | data formatting | bytes 524288 | tf_op args[1]
  7.2 1.4 %copy.5 = bf16[128,2304]{0,1:T(8,128)(2,1)S(1)} copy(bf16[128,2304]{1,0:T(8,128)(2,1)} %param.3) | data formatting | bytes 1179648 | tf_op args[0]
  8.6 0.0 collective-permute-done.refs_1_
  8.6 0.4 apply.2
  9.0 0.1 collective-permute-start.1
  9.1 1.5 %collective-permute-done.1 = f32[576,128]{1,0:T(8,128)S(1)} collective-permute-done((f32[576,128]{1,0:T(8,128)S(1)}, f32[576,128]{1,0:T(8,128)S(1)}, u32[]{:S(2)}, u32[]{:S(2)}) %collective-permute-start.1) | collective-permute-done | bytes 294944 | tf_op jit(solution)/shard_map/ppermute | solution.py:50
  10.7 1.8 %collective-permute-start.2 = (f32[144,128]{1,0:T(8,128)S(1)}, f32[144,128]{1,0:T(8,128)S(1)}, u32[]{:S(2)}, u32[]{:S(2)}) collective-permute-start(f32[144,128]{1,0:T(8,128)S(1)} %get-tuple-element.18), channel_id=1, source_target_pairs={{0,4},{2,6},{4,0},{6,2},{8,12},{10,14},{12,8},{14,10},{16,20},{18,... | collective-permute-start | bytes 221192 | tf_op jit(solution)/shard_map/ppermute | solution.py:50
  12.5 1.5 %collective-permute-start.4 = (f32[144,128]{1,0:T(8,128)S(1)}, f32[144,128]{1,0:T(8,128)S(1)}, u32[]{:S(2)}, u32[]{:S(2)}) collective-permute-start(f32[144,128]{1,0:T(8,128)S(1)} %get-tuple-element.19), channel_id=1, source_target_pairs={{0,12},{2,14},{4,8},{6,10},{8,4},{10,6},{12,0},{14,2},{16,28},{18,... | collective-permute-start | bytes 221192 | tf_op jit(solution)/shard_map/ppermute | solution.py:50
  14.1 0.2 collective-permute-start.3
  14.3 1.6 %collective-permute-done.2 = f32[144,128]{1,0:T(8,128)S(1)} collective-permute-done((f32[144,128]{1,0:T(8,128)S(1)}, f32[144,128]{1,0:T(8,128)S(1)}, u32[]{:S(2)}, u32[]{:S(2)}) %collective-permute-start.2) | collective-permute-done | bytes 73760 | tf_op jit(solution)/shard_map/ppermute | solution.py:50
  15.9 2.5 %collective-permute-done.4 = f32[144,128]{1,0:T(8,128)S(1)} collective-permute-done((f32[144,128]{1,0:T(8,128)S(1)}, f32[144,128]{1,0:T(8,128)S(1)}, u32[]{:S(2)}, u32[]{:S(2)}) %collective-permute-start.4) | collective-permute-done | bytes 73760 | tf_op jit(solution)/shard_map/ppermute | solution.py:50
  18.4 0.0 collective-permute-done.3
  18.5 2.7 %collective-permute-start.5 = (f32[72,128]{1,0:T(8,128)S(1)}, f32[72,128]{1,0:T(8,128)S(1)}, u32[]{:S(2)}, u32[]{:S(2)}) collective-permute-start(f32[72,128]{1,0:T(8,128)S(1)} %constant_dynamic-slice_fusion.6), channel_id=1, source_target_pairs={{0,16},{2,18},{4,20},{6,22},{8,24},{10,26},{12,28},{14,30},{16,0},... | collective-permute-start | bytes 110600 | tf_op jit(solution)/shard_map/ppermute | solution.py:50
  21.1 2.3 %collective-permute-done.5 = f32[72,128]{1,0:T(8,128)S(1)} collective-permute-done((f32[72,128]{1,0:T(8,128)S(1)}, f32[72,128]{1,0:T(8,128)S(1)}, u32[]{:S(2)}, u32[]{:S(2)}) %collective-permute-start.5) | collective-permute-done | bytes 36896 | tf_op jit(solution)/shard_map/ppermute | solution.py:50
  23.4 2.8 %collective-permute-start.6 = (f32[72,128]{1,0:T(8,128)S(1)}, f32[72,128]{1,0:T(8,128)S(1)}, u32[]{:S(2)}, u32[]{:S(2)}) collective-permute-start(f32[72,128]{1,0:T(8,128)S(1)} %get-tuple-element.17), channel_id=1, source_target_pairs={{0,16},{2,18},{4,20},{6,22},{8,24},{10,26},{12,28},{14,30},{16,0},... | collective-permute-start | bytes 110600 | tf_op jit(solution)/shard_map/ppermute | solution.py:50
  26.2 2.2 %collective-permute-done.6 = f32[72,128]{1,0:T(8,128)S(1)} collective-permute-done((f32[72,128]{1,0:T(8,128)S(1)}, f32[72,128]{1,0:T(8,128)S(1)}, u32[]{:S(2)}, u32[]{:S(2)}) %collective-permute-start.6) | collective-permute-done | bytes 36896 | tf_op jit(solution)/shard_map/ppermute | solution.py:50
  28.3 2.3 %collective-permute-start.9 = (f32[144,128]{1,0:T(8,128)S(1)}, f32[144,128]{1,0:T(8,128)S(1)}, u32[]{:S(2)}, u32[]{:S(2)}) collective-permute-start(f32[144,128]{1,0:T(8,128)S(1)} %constant_dynamic-update-slice_fusion.14), channel_id=1, source_target_pairs={{0,12},{2,14},{4,8},{6,10},{8,4},{10,6},{12,0},{14,2},{16,28},{18,... | collective-permute-start | bytes 221192 | tf_op jit(solution)/shard_map/ppermute | solution.py:50
  30.6 0.7 collective-permute-start.8
  31.3 0.5 collective-permute-start.7
  31.9 3.8 %collective-permute-done.7 = f32[144,128]{1,0:T(8,128)S(1)} collective-permute-done((f32[144,128]{1,0:T(8,128)S(1)}, f32[144,128]{1,0:T(8,128)S(1)}, u32[]{:S(2)}, u32[]{:S(2)}) %collective-permute-start.7) | collective-permute-done | bytes 73760 | tf_op jit(solution)/shard_map/ppermute | solution.py:50
  35.7 0.0 collective-permute-done.8
  35.7 0.0 collective-permute-done.9
  35.7 0.1 collective-permute-start.10
  35.9 1.5 %collective-permute-done.10 = f32[576,128]{1,0:T(8,128)S(1)} collective-permute-done((f32[576,128]{1,0:T(8,128)S(1)}, f32[576,128]{1,0:T(8,128)S(1)}, u32[]{:S(2)}, u32[]{:S(2)}) %collective-permute-start.10) | collective-permute-done | bytes 294944 | tf_op jit(solution)/shard_map/ppermute | solution.py:50
  37.4 0.4 weigh.1.refs_0_
  37.9 1.6 %collective-permute-start.13 = (f32[128,128]{1,0:T(8,128)S(1)}, f32[128,128]{1,0:T(8,128)S(1)}, u32[]{:S(2)}, u32[]{:S(2)}) collective-permute-start(f32[128,128]{1,0:T(8,128)S(1)} %weigh.1.refs_0_), channel_id=1, source_target_pairs={{0,1},{1,0},{2,3},{3,2},{4,5},{5,4},{6,7},{7,6},{8,9},{9,8},{10,11... | collective-permute-start | bytes 196616 | tf_op jit(solution)/shard_map/ppermute | solution.py:50
  39.4 2.8 %collective-permute-done.13.refs_1_ = f32[128,128]{1,0:T(8,128)S(1)} collective-permute-done((f32[128,128]{1,0:T(8,128)S(1)}, f32[128,128]{1,0:T(8,128)S(1)}, u32[]{:S(2)}, u32[]{:S(2)}) %collective-permute-start.13) | collective-permute-done | bytes 65568 | tf_op jit(solution)/shard_map/ppermute | solution.py:50
  42.2 0.4 apply.3
  42.6 0.1 collective-permute-start.14
  42.7 1.1 %fusion = f32[128,128]{1,0:T(8,128)S(1)} fusion(f32[1152,128]{1,0:T(8,128)S(1)} %constant_dynamic-update-slice_fusion.8.left_ref.refs_0_), kind=kOutput, calls=%fused_computation.34 | convolution fusion | flops 226492416 | bytes 655360 | tf_op jit(solution)/shard_map/dot_general | solution.py:331
  43.8 1.6 %collective-permute-start.11 = (f32[128,128]{1,0:T(8,128)S(1)}, f32[128,128]{1,0:T(8,128)S(1)}, u32[]{:S(2)}, u32[]{:S(2)}) collective-permute-start(f32[128,128]{1,0:T(8,128)S(1)} %fusion), channel_id=1, source_target_pairs={{0,1},{1,0},{2,3},{3,2},{4,5},{5,4},{6,7},{7,6},{8,9},{9,8},{10,11... | collective-permute-start | bytes 196616 | tf_op jit(solution)/shard_map/ppermute | solution.py:50
  45.4 0.0 collective-permute-done.14
  45.5 0.6 collective-permute-start.15
  46.0 2.3 %collective-permute-start.17 = (f32[128,128]{1,0:T(8,128)S(1)}, f32[128,128]{1,0:T(8,128)S(1)}, u32[]{:S(2)}, u32[]{:S(2)}) collective-permute-start(f32[128,128]{1,0:T(8,128)S(1)} %get-tuple-element.22), channel_id=1, source_target_pairs={{0,12},{2,14},{4,8},{6,10},{8,4},{10,6},{12,0},{14,2},{16,28},{18,... | collective-permute-start | bytes 196616 | tf_op jit(solution)/shard_map/ppermute | solution.py:50
  48.3 0.7 collective-permute-start.16
  49.0 0.1 pad_add_fusion.place_ref
  49.1 0.5 collective-permute-start.12
  49.6 0.0 collective-permute-done.11
  49.6 0.9 %collective-permute-done.15 = f32[128,128]{1,0:T(8,128)S(1)} collective-permute-done((f32[128,128]{1,0:T(8,128)S(1)}, f32[128,128]{1,0:T(8,128)S(1)}, u32[]{:S(2)}, u32[]{:S(2)}) %collective-permute-start.15) | collective-permute-done | bytes 65568 | tf_op jit(solution)/shard_map/ppermute | solution.py:50
  50.5 1.3 %collective-permute-done.17 = f32[128,128]{1,0:T(8,128)S(1)} collective-permute-done((f32[128,128]{1,0:T(8,128)S(1)}, f32[128,128]{1,0:T(8,128)S(1)}, u32[]{:S(2)}, u32[]{:S(2)}) %collective-permute-start.17) | collective-permute-done | bytes 65568 | tf_op jit(solution)/shard_map/ppermute | solution.py:50
  51.8 0.8 %collective-permute-done.16 = f32[128,128]{1,0:T(8,128)S(1)} collective-permute-done((f32[128,128]{1,0:T(8,128)S(1)}, f32[128,128]{1,0:T(8,128)S(1)}, u32[]{:S(2)}, u32[]{:S(2)}) %collective-permute-start.16) | collective-permute-done | bytes 65568 | tf_op jit(solution)/shard_map/ppermute | solution.py:50
  52.7 3.4 %collective-permute-start.18 = (f32[64,128]{1,0:T(8,128)S(1)}, f32[64,128]{1,0:T(8,128)S(1)}, u32[]{:S(2)}, u32[]{:S(2)}) collective-permute-start(f32[64,128]{1,0:T(8,128)S(1)} %constant_dynamic-slice_fusion), channel_id=1, source_target_pairs={{0,16},{2,18},{4,20},{6,22},{8,24},{10,26},{12,28},{14,30},{16,0},... | collective-permute-start | bytes 98312 | tf_op jit(solution)/shard_map/ppermute | solution.py:50
  56.0 2.6 %shard_map.50.state_ref = f32[128,128]{1,0:T(8,128)S(1)} custom-call(f32[128,128]{1,0:T(8,128)S(1)} %add.138.state_ref), custom_call_target="tpu_custom_call" | custom-call | flops 3000000000 | bytes 131072 | tf_op jit(solution)/shard_map/pallas_call | solution.py:149
  58.7 0.0 collective-permute-done.18
  58.7 2.2 %collective-permute-start.19 = (f32[64,128]{1,0:T(8,128)S(1)}, f32[64,128]{1,0:T(8,128)S(1)}, u32[]{:S(2)}, u32[]{:S(2)}) collective-permute-start(f32[64,128]{1,0:T(8,128)S(1)} %get-tuple-element.15), channel_id=1, source_target_pairs={{0,16},{2,18},{4,20},{6,22},{8,24},{10,26},{12,28},{14,30},{16,0},... | collective-permute-start | bytes 98312 | tf_op jit(solution)/shard_map/ppermute | solution.py:50
  60.9 2.2 %shard_map.51.inverse_ref = f32[128,128]{1,0:T(8,128)S(1)} custom-call(f32[128,128]{1,0:T(8,128)S(1)} %shard_map.50.state_ref), custom_call_target="tpu_custom_call" | custom-call | flops 3000000000 | bytes 131072 | tf_op jit(solution)/shard_map/pallas_call | solution.py:149
  63.1 0.5 collective-permute-done.19
  63.6 1.2 %collective-permute-start.22 = (f32[128,128]{1,0:T(8,128)S(1)}, f32[128,128]{1,0:T(8,128)S(1)}, u32[]{:S(2)}, u32[]{:S(2)}) collective-permute-start(f32[128,128]{1,0:T(8,128)S(1)} %constant_dynamic-update-slice_fusion.6), channel_id=1, source_target_pairs={{0,12},{2,14},{4,8},{6,10},{8,4},{10,6},{12,0},{14,2},{16,28},{18,... | collective-permute-start | bytes 196616 | tf_op jit(solution)/shard_map/ppermute | solution.py:50
  64.8 0.8 %collective-permute-start.21 = (f32[128,128]{1,0:T(8,128)S(1)}, f32[128,128]{1,0:T(8,128)S(1)}, u32[]{:S(2)}, u32[]{:S(2)}) collective-permute-start(f32[128,128]{1,0:T(8,128)S(1)} %constant_dynamic-update-slice_fusion.6), channel_id=1, source_target_pairs={{0,8},{2,10},{4,12},{6,14},{8,0},{10,2},{12,4},{14,6},{16,24},{18,... | collective-permute-start | bytes 196616 | tf_op jit(solution)/shard_map/ppermute | solution.py:50
  65.6 1.5 %collective-permute-start.20 = (f32[128,128]{1,0:T(8,128)S(1)}, f32[128,128]{1,0:T(8,128)S(1)}, u32[]{:S(2)}, u32[]{:S(2)}) collective-permute-start(f32[128,128]{1,0:T(8,128)S(1)} %constant_dynamic-update-slice_fusion.6), channel_id=1, source_target_pairs={{0,4},{2,6},{4,0},{6,2},{8,12},{10,14},{12,8},{14,10},{16,20},{18,... | collective-permute-start | bytes 196616 | tf_op jit(solution)/shard_map/ppermute | solution.py:50
  67.1 2.8 %collective-permute-done.20 = f32[128,128]{1,0:T(8,128)S(1)} collective-permute-done((f32[128,128]{1,0:T(8,128)S(1)}, f32[128,128]{1,0:T(8,128)S(1)}, u32[]{:S(2)}, u32[]{:S(2)}) %collective-permute-start.20) | collective-permute-done | bytes 65568 | tf_op jit(solution)/shard_map/ppermute | solution.py:50
  69.9 0.0 collective-permute-done.21
  69.9 0.0 collective-permute-done.22
  70.0 0.1 collective-permute-start.23
  70.1 0.0 copy-start.1
  70.1 0.0 collective-permute-done.12.refs_1_
  70.1 1.9 %basis.1.tall_ref = bf16[2304,512]{1,0:T(8,128)(2,1)S(1)} custom-call(s32[2]{0:T(128)S(1)} %pad_add_fusion.place_ref, f32[128,128]{1,0:T(8,128)S(1)} %shard_map.51.inverse_ref, bf16[2304,128]{1,0:T(8,128)(2,1)S(1)} %bitcast.8, f32[1152,128]{1,0:T(8,128)S(1)} %constant_dynamic-update-slice_fusion.8.left_ref.refs_0_, ...), custom_call_target="tpu_custom_call" | custom-call | flops 2000000000 | bytes 131072 | tf_op jit(solution)/shard_map/basis/pallas_call | solution.py:257
  72.1 0.0 collective-permute-done.23
  72.1 5.8 %finish.1 = (f32[144,1024]{1,0:T(8,128)}, bf16[2304,1024]{1,0:T(8,128)(2,1)}) custom-call(bf16[144,512]{1,0:T(8,128)(2,1)S(1)} %constant_dynamic-slice_fusion.5.mine_ref, bf16[2304,512]{1,0:T(8,128)(2,1)S(1)} %basis.1.tall_ref, bf16[128,1024]{1,0:T(8,128)(2,1)S(1)} %copy-done.1, f32[1024,128]{1,0:T(8,128)S(1)} %constant_dynamic-update-slice_fusion.sum_ref, ...), custom_call_target="tpu_custom_call" | custom-call | tf_op jit(solution)/shard_map/finish/pallas_call | solution.py:290
  (36 shorter events, 0.6 us)
Async XLA Ops:
  0.6 1.0 %copy-start = (bf16[128,1024]{1,0:T(8,128)(2,1)S(1)}, bf16[128,1024]{1,0:T(8,128)(2,1)}, u32[]{:S(2)}) copy-start(bf16[128,1024]{1,0:T(8,128)(2,1)} %grads_ref.3) | copy-start | bytes 786436
  1.6 1.0 %copy-start.2 = (f32[1024,128]{1,0:T(8,128)S(1)}, f32[1024,128]{1,0:T(8,128)}, u32[]{:S(2)}) copy-start(f32[1024,128]{1,0:T(8,128)} %right_ref.1) | copy-start | bytes 1572868
  3.0 5.6 %collective-permute-start = (f32[128,128]{1,0:T(8,128)S(1)}, f32[128,128]{1,0:T(8,128)S(1)}, u32[]{:S(2)}, u32[]{:S(2)}) collective-permute-start(f32[128,128]{1,0:T(8,128)S(1)} %project.1.refs_0_), channel_id=1, source_target_pairs={{0,1},{1,0},{2,3},{3,2},{4,5},{5,4},{6,7},{7,6},{8,9},{9,8},{10,11... | collective-permute-start | bytes 196616 | tf_op jit(solution)/shard_map/ppermute | solution.py:50
  9.0 1.6 %collective-permute-start.1 = (f32[576,128]{1,0:T(8,128)S(1)}, f32[576,128]{1,0:T(8,128)S(1)}, u32[]{:S(2)}, u32[]{:S(2)}) collective-permute-start(f32[576,128]{1,0:T(8,128)S(1)} %constant_dynamic-slice_fusion.10), channel_id=1, source_target_pairs={{0,2},{2,0},{4,6},{6,4},{8,10},{10,8},{12,14},{14,12},{16,18},{18,... | collective-permute-start | bytes 884744 | tf_op jit(solution)/shard_map/ppermute | solution.py:50
  10.7 5.2 %collective-permute-start.2 = (f32[144,128]{1,0:T(8,128)S(1)}, f32[144,128]{1,0:T(8,128)S(1)}, u32[]{:S(2)}, u32[]{:S(2)}) collective-permute-start(f32[144,128]{1,0:T(8,128)S(1)} %get-tuple-element.18), channel_id=1, source_target_pairs={{0,4},{2,6},{4,0},{6,2},{8,12},{10,14},{12,8},{14,10},{16,20},{18,... | collective-permute-start | bytes 221192 | tf_op jit(solution)/shard_map/ppermute | solution.py:50
  12.5 5.9 %collective-permute-start.4 = (f32[144,128]{1,0:T(8,128)S(1)}, f32[144,128]{1,0:T(8,128)S(1)}, u32[]{:S(2)}, u32[]{:S(2)}) collective-permute-start(f32[144,128]{1,0:T(8,128)S(1)} %get-tuple-element.19), channel_id=1, source_target_pairs={{0,12},{2,14},{4,8},{6,10},{8,4},{10,6},{12,0},{14,2},{16,28},{18,... | collective-permute-start | bytes 221192 | tf_op jit(solution)/shard_map/ppermute | solution.py:50
  14.1 4.4 %collective-permute-start.3 = (f32[144,128]{1,0:T(8,128)S(1)}, f32[144,128]{1,0:T(8,128)S(1)}, u32[]{:S(2)}, u32[]{:S(2)}) collective-permute-start(f32[144,128]{1,0:T(8,128)S(1)} %get-tuple-element.20), channel_id=1, source_target_pairs={{0,8},{2,10},{4,12},{6,14},{8,0},{10,2},{12,4},{14,6},{16,24},{18,... | collective-permute-start | bytes 221192 | tf_op jit(solution)/shard_map/ppermute | solution.py:50
  18.5 4.9 %collective-permute-start.5 = (f32[72,128]{1,0:T(8,128)S(1)}, f32[72,128]{1,0:T(8,128)S(1)}, u32[]{:S(2)}, u32[]{:S(2)}) collective-permute-start(f32[72,128]{1,0:T(8,128)S(1)} %constant_dynamic-slice_fusion.6), channel_id=1, source_target_pairs={{0,16},{2,18},{4,20},{6,22},{8,24},{10,26},{12,28},{14,30},{16,0},... | collective-permute-start | bytes 110600 | tf_op jit(solution)/shard_map/ppermute | solution.py:50
  23.4 4.9 %collective-permute-start.6 = (f32[72,128]{1,0:T(8,128)S(1)}, f32[72,128]{1,0:T(8,128)S(1)}, u32[]{:S(2)}, u32[]{:S(2)}) collective-permute-start(f32[72,128]{1,0:T(8,128)S(1)} %get-tuple-element.17), channel_id=1, source_target_pairs={{0,16},{2,18},{4,20},{6,22},{8,24},{10,26},{12,28},{14,30},{16,0},... | collective-permute-start | bytes 110600 | tf_op jit(solution)/shard_map/ppermute | solution.py:50
  28.3 7.4 %collective-permute-start.9 = (f32[144,128]{1,0:T(8,128)S(1)}, f32[144,128]{1,0:T(8,128)S(1)}, u32[]{:S(2)}, u32[]{:S(2)}) collective-permute-start(f32[144,128]{1,0:T(8,128)S(1)} %constant_dynamic-update-slice_fusion.14), channel_id=1, source_target_pairs={{0,12},{2,14},{4,8},{6,10},{8,4},{10,6},{12,0},{14,2},{16,28},{18,... | collective-permute-start | bytes 221192 | tf_op jit(solution)/shard_map/ppermute | solution.py:50
  30.6 5.1 %collective-permute-start.8 = (f32[144,128]{1,0:T(8,128)S(1)}, f32[144,128]{1,0:T(8,128)S(1)}, u32[]{:S(2)}, u32[]{:S(2)}) collective-permute-start(f32[144,128]{1,0:T(8,128)S(1)} %constant_dynamic-update-slice_fusion.14), channel_id=1, source_target_pairs={{0,8},{2,10},{4,12},{6,14},{8,0},{10,2},{12,4},{14,6},{16,24},{18,... | collective-permute-start | bytes 221192 | tf_op jit(solution)/shard_map/ppermute | solution.py:50
  31.3 4.4 %collective-permute-start.7 = (f32[144,128]{1,0:T(8,128)S(1)}, f32[144,128]{1,0:T(8,128)S(1)}, u32[]{:S(2)}, u32[]{:S(2)}) collective-permute-start(f32[144,128]{1,0:T(8,128)S(1)} %constant_dynamic-update-slice_fusion.14), channel_id=1, source_target_pairs={{0,4},{2,6},{4,0},{6,2},{8,12},{10,14},{12,8},{14,10},{16,20},{18,... | collective-permute-start | bytes 221192 | tf_op jit(solution)/shard_map/ppermute | solution.py:50
  35.7 1.6 %collective-permute-start.10 = (f32[576,128]{1,0:T(8,128)S(1)}, f32[576,128]{1,0:T(8,128)S(1)}, u32[]{:S(2)}, u32[]{:S(2)}) collective-permute-start(f32[576,128]{1,0:T(8,128)S(1)} %constant_dynamic-update-slice_fusion.10), channel_id=1, source_target_pairs={{0,2},{2,0},{4,6},{6,4},{8,10},{10,8},{12,14},{14,12},{16,18},{18,... | collective-permute-start | bytes 884744 | tf_op jit(solution)/shard_map/ppermute | solution.py:50
  37.9 4.3 %collective-permute-start.13 = (f32[128,128]{1,0:T(8,128)S(1)}, f32[128,128]{1,0:T(8,128)S(1)}, u32[]{:S(2)}, u32[]{:S(2)}) collective-permute-start(f32[128,128]{1,0:T(8,128)S(1)} %weigh.1.refs_0_), channel_id=1, source_target_pairs={{0,1},{1,0},{2,3},{3,2},{4,5},{5,4},{6,7},{7,6},{8,9},{9,8},{10,11... | collective-permute-start | bytes 196616 | tf_op jit(solution)/shard_map/ppermute | solution.py:50
  42.6 2.8 %collective-permute-start.14 = (f32[512,128]{1,0:T(8,128)S(1)}, f32[512,128]{1,0:T(8,128)S(1)}, u32[]{:S(2)}, u32[]{:S(2)}) collective-permute-start(f32[512,128]{1,0:T(8,128)S(1)} %constant_dynamic-slice_fusion.4), channel_id=1, source_target_pairs={{0,2},{2,0},{4,6},{6,4},{8,10},{10,8},{12,14},{14,12},{16,18},{18,... | collective-permute-start | bytes 786440 | tf_op jit(solution)/shard_map/ppermute | solution.py:50
  43.8 5.8 %collective-permute-start.11 = (f32[128,128]{1,0:T(8,128)S(1)}, f32[128,128]{1,0:T(8,128)S(1)}, u32[]{:S(2)}, u32[]{:S(2)}) collective-permute-start(f32[128,128]{1,0:T(8,128)S(1)} %fusion), channel_id=1, source_target_pairs={{0,1},{1,0},{2,3},{3,2},{4,5},{5,4},{6,7},{7,6},{8,9},{9,8},{10,11... | collective-permute-start | bytes 196616 | tf_op jit(solution)/shard_map/ppermute | solution.py:50
  45.5 5.0 %collective-permute-start.15 = (f32[128,128]{1,0:T(8,128)S(1)}, f32[128,128]{1,0:T(8,128)S(1)}, u32[]{:S(2)}, u32[]{:S(2)}) collective-permute-start(f32[128,128]{1,0:T(8,128)S(1)} %get-tuple-element.21), channel_id=1, source_target_pairs={{0,4},{2,6},{4,0},{6,2},{8,12},{10,14},{12,8},{14,10},{16,20},{18,... | collective-permute-start | bytes 196616 | tf_op jit(solution)/shard_map/ppermute | solution.py:50
  46.0 5.7 %collective-permute-start.17 = (f32[128,128]{1,0:T(8,128)S(1)}, f32[128,128]{1,0:T(8,128)S(1)}, u32[]{:S(2)}, u32[]{:S(2)}) collective-permute-start(f32[128,128]{1,0:T(8,128)S(1)} %get-tuple-element.22), channel_id=1, source_target_pairs={{0,12},{2,14},{4,8},{6,10},{8,4},{10,6},{12,0},{14,2},{16,28},{18,... | collective-permute-start | bytes 196616 | tf_op jit(solution)/shard_map/ppermute | solution.py:50
  48.3 4.3 %collective-permute-start.16 = (f32[128,128]{1,0:T(8,128)S(1)}, f32[128,128]{1,0:T(8,128)S(1)}, u32[]{:S(2)}, u32[]{:S(2)}) collective-permute-start(f32[128,128]{1,0:T(8,128)S(1)} %get-tuple-element.23), channel_id=1, source_target_pairs={{0,8},{2,10},{4,12},{6,14},{8,0},{10,2},{12,4},{14,6},{16,24},{18,... | collective-permute-start | bytes 196616 | tf_op jit(solution)/shard_map/ppermute | solution.py:50
  49.1 21.0 %collective-permute-start.12 = (f32[1152,128]{1,0:T(8,128)S(1)}, f32[1152,128]{1,0:T(8,128)S(1)}, u32[]{:S(2)}, u32[]{:S(2)}) collective-permute-start(f32[1152,128]{1,0:T(8,128)S(1)} %constant_dynamic-update-slice_fusion.8.left_ref.refs_0_), channel_id=1, source_target_pairs={{0,1},{1,0},{2,3},{3,2},{4,5},{5,4},{6,7},{7,6},{8,9},{9,8},{10,11... | collective-permute-start | bytes 1769480 | tf_op jit(solution)/shard_map/ppermute | solution.py:50
  52.7 6.0 %collective-permute-start.18 = (f32[64,128]{1,0:T(8,128)S(1)}, f32[64,128]{1,0:T(8,128)S(1)}, u32[]{:S(2)}, u32[]{:S(2)}) collective-permute-start(f32[64,128]{1,0:T(8,128)S(1)} %constant_dynamic-slice_fusion), channel_id=1, source_target_pairs={{0,16},{2,18},{4,20},{6,22},{8,24},{10,26},{12,28},{14,30},{16,0},... | collective-permute-start | bytes 98312 | tf_op jit(solution)/shard_map/ppermute | solution.py:50
  58.7 4.9 %collective-permute-start.19 = (f32[64,128]{1,0:T(8,128)S(1)}, f32[64,128]{1,0:T(8,128)S(1)}, u32[]{:S(2)}, u32[]{:S(2)}) collective-permute-start(f32[64,128]{1,0:T(8,128)S(1)} %get-tuple-element.15), channel_id=1, source_target_pairs={{0,16},{2,18},{4,20},{6,22},{8,24},{10,26},{12,28},{14,30},{16,0},... | collective-permute-start | bytes 98312 | tf_op jit(solution)/shard_map/ppermute | solution.py:50
  63.6 6.3 %collective-permute-start.22 = (f32[128,128]{1,0:T(8,128)S(1)}, f32[128,128]{1,0:T(8,128)S(1)}, u32[]{:S(2)}, u32[]{:S(2)}) collective-permute-start(f32[128,128]{1,0:T(8,128)S(1)} %constant_dynamic-update-slice_fusion.6), channel_id=1, source_target_pairs={{0,12},{2,14},{4,8},{6,10},{8,4},{10,6},{12,0},{14,2},{16,28},{18,... | collective-permute-start | bytes 196616 | tf_op jit(solution)/shard_map/ppermute | solution.py:50
  64.8 5.1 %collective-permute-start.21 = (f32[128,128]{1,0:T(8,128)S(1)}, f32[128,128]{1,0:T(8,128)S(1)}, u32[]{:S(2)}, u32[]{:S(2)}) collective-permute-start(f32[128,128]{1,0:T(8,128)S(1)} %constant_dynamic-update-slice_fusion.6), channel_id=1, source_target_pairs={{0,8},{2,10},{4,12},{6,14},{8,0},{10,2},{12,4},{14,6},{16,24},{18,... | collective-permute-start | bytes 196616 | tf_op jit(solution)/shard_map/ppermute | solution.py:50
  65.6 4.3 %collective-permute-start.20 = (f32[128,128]{1,0:T(8,128)S(1)}, f32[128,128]{1,0:T(8,128)S(1)}, u32[]{:S(2)}, u32[]{:S(2)}) collective-permute-start(f32[128,128]{1,0:T(8,128)S(1)} %constant_dynamic-update-slice_fusion.6), channel_id=1, source_target_pairs={{0,4},{2,6},{4,0},{6,2},{8,12},{10,14},{12,8},{14,10},{16,20},{18,... | collective-permute-start | bytes 196616 | tf_op jit(solution)/shard_map/ppermute | solution.py:50
  70.0 2.1 %collective-permute-start.23 = (f32[512,128]{1,0:T(8,128)S(1)}, f32[512,128]{1,0:T(8,128)S(1)}, u32[]{:S(2)}, u32[]{:S(2)}) collective-permute-start(f32[512,128]{1,0:T(8,128)S(1)} %constant_dynamic-update-slice_fusion.2), channel_id=1, source_target_pairs={{0,2},{2,0},{4,6},{6,4},{8,10},{10,8},{12,14},{14,12},{16,18},{18,... | collective-permute-start | bytes 786440 | tf_op jit(solution)/shard_map/ppermute | solution.py:50
  70.1 2.0 %copy-start.1 = (bf16[128,1024]{1,0:T(8,128)(2,1)S(1)}, bf16[128,1024]{1,0:T(8,128)(2,1)}, u32[]{:S(2)}) copy-start(bf16[128,1024]{1,0:T(8,128)(2,1)} %grads_ref.3) | copy-start | bytes 786436
where the time goes:
time: 78.2 us; the launch traced here: 77.9 us
  starting transfers between devices  32 us (41%)
  waiting for transfers between devices  24.4 us (31%)
  Pallas kernels  14 us (18%)
  local copies, waits for them, and re-layouts  4.95 us (6%)
  between operations  1.16 us (1%)
  matrix products  1.12 us (1%)
    ppermute x24, starting transfers between devices, shifted(): return lax.ppermute(value, axis, pairs)  32 us
    ppermute x24, waiting for transfers between devices, shifted(): return lax.ppermute(value, axis, pairs)  24.4 us
    pallas_call x1, Pallas kernels, finish(): pl.pallas_call(functools.partial(finish_body, replicas), grid=(rows // ti...  5.82 us
    pallas_call x2, Pallas kernels, inverse_factor(): state = call(state)  4.79 us
    unnamed x8, local copies, waits for them, and re-layouts  4.48 us
    pallas_call x1, Pallas kernels, basis(): pl.pallas_call(basis_body, out_shape=jax.ShapeDtypeStruct((acts.shape[0],...  1.88 us
  transfers between devices with their start and end apart: 24, of which 13 were waited for; matrix products, arithmetic and copies ran while one was open for 5% of the time, Pallas kernels for 9%

commit v1 on v0

--- a/solution.py
+++ b/solution.py
@@ -143,7 +143,7 @@
             out_shape=jax.ShapeDtypeStruct(gram.shape, jnp.float32),
             in_specs=[pl.BlockSpec(memory_space=pltpu.VMEM)],
             out_specs=pl.BlockSpec(memory_space=pltpu.VMEM),
-            compiler_params=grant(4),
+            compiler_params=grant(2),
             cost_estimate=cost(3),
         )
         state = call(state)
@@ -198,7 +198,7 @@
         out_shape=jax.ShapeDtypeStruct((out_grads.shape[0], right_prev.shape[1]), jnp.float32),
         in_specs=vmem(2),
         out_specs=vmem(1)[0],
-        compiler_params=grant(12),
+        compiler_params=grant(4),
         name="project",
     )(out_grads, right_prev)
 
@@ -218,7 +218,7 @@
         out_shape=jax.ShapeDtypeStruct((rows, parts[0].shape[1]), jnp.float32),
         in_specs=[SMEM] + vmem(1 + len(parts)),
         out_specs=vmem(1)[0],
-        compiler_params=grant(12),
+        compiler_params=grant(4),
         name="apply",
     )(place, tall, *parts)
 
@@ -235,7 +235,7 @@
         out_shape=jax.ShapeDtypeStruct((tall.shape[1], left.shape[1]), jnp.float32),
         in_specs=[SMEM] + vmem(2),
         out_specs=vmem(1)[0],
-        compiler_params=grant(12),
+        compiler_params=grant(4),
         name="weigh",
     )(place, tall, left)
 
@@ -259,13 +259,13 @@
         out_shape=jax.ShapeDtypeStruct((acts.shape[0], columns), jnp.bfloat16),
         in_specs=[SMEM] + vmem(2 + len(parts)),
         out_specs=vmem(1)[0],
-        compiler_params=grant(16),
+        compiler_params=grant(8),
         cost_estimate=cost(2),
         name="basis",
     )(places, inverse, acts, *parts)
 
 
-def finish_body(replicas, mine_ref, tall_ref, grads_ref, sum_ref, inverse_ref, update_ref, residual_ref, wide):
+def finish_body(replicas, place_ref, mine_ref, tall_ref, grads_ref, sum_ref, inverse_ref, update_ref, residual_ref, wide):
     step, tile = pl.program_id(0), residual_ref.shape[0]
     tokens, rank = grads_ref.shape[0], inverse_ref.shape[0]
 
@@ -276,16 +276,21 @@
         wide[:tokens, :] = grads_ref[...]
         for index, term in enumerate((top, top, low)):
             wide[tokens + index * rank : tokens + (index + 1) * rank, :] = term
-        update_ref[...] = -jnp.dot(mine_ref[:, tokens:], wide[tokens:, :], preferred_element_type=jnp.float32)
+        my_rows = update_ref.shape[0]
+        mine = pl.ds(pl.multiple_of(place_ref[0] * my_rows, 16), my_rows)
+        left = mine_ref[mine, tokens:] if my_rows % 16 == 0 else mine_ref[:, tokens:]
+        update_ref[...] = -jnp.dot(left, wide[tokens:, :], preferred_element_type=jnp.float32)
 
     rows = pl.ds(pl.multiple_of(step * tile, tile), tile)
     residual = jnp.dot(tall_ref[rows, :], wide[...], preferred_element_type=jnp.float32)
     residual_ref[...] = residual.astype(jnp.bfloat16)
 
 
-def finish(replicas, mine, tall, out_grads, right_sum, inverse):
+def finish(replicas, place, tall, out_grads, right_sum, inverse):
     rows, columns = tall.shape[0], out_grads.shape[1]
-    my_rows = mine.shape[0]
+    my_rows, mine = rows // replicas, tall
+    if my_rows % 16 != 0:
+        mine = lax.dynamic_slice_in_dim(tall, place[0] * my_rows, my_rows, 0)
     tile = next(size for size in (384, 256, 192, 128, 96, 64, 32, 16, 8) if rows % size == 0)
     return pl.pallas_call(
         functools.partial(finish_body, replicas),
@@ -294,15 +299,15 @@
             jax.ShapeDtypeStruct((my_rows, columns), jnp.float32),
             jax.ShapeDtypeStruct((rows, columns), jnp.bfloat16),
         ),
-        in_specs=vmem(5),
+        in_specs=[SMEM] + vmem(5),
         out_specs=(
             pl.BlockSpec((my_rows, columns), lambda i: (0, 0)),
             pl.BlockSpec((tile, columns), lambda i: (i, 0)),
         ),
         scratch_shapes=[pltpu.VMEM((tall.shape[1], columns), jnp.bfloat16)],
-        compiler_params=grant(24, dimension_semantics=("arbitrary",)),
+        compiler_params=grant(12, dimension_semantics=("arbitrary",)),
         name="finish",
-    )(mine, tall, out_grads, right_sum, inverse)
+    )(place, mine, tall, out_grads, right_sum, inverse)
 
 
 def sent_all(value, axis):
@@ -338,9 +343,8 @@
     parts, places = sent_all(left_own, "tp")
     inverse = inverse_factor(gram)
     tall = basis(places, inverse, acts, parts)
-    rows_dev = rows // replicas
-    mine = lax.dynamic_slice_in_dim(tall, lax.axis_index("dp") * rows_dev, rows_dev, 0)
-    return finish(replicas, mine, tall, out_grads, right_sum, inverse)
+    replica = lax.axis_index("dp").astype(jnp.int32).reshape(1)
+    return finish(replicas, replica, tall, out_grads, right_sum, inverse)
 
 
 def solution(mesh):

time: 78.2 us -> 78.2 us (level)
  no operation moved by 1% of the time
where the time goes in v1:
time: 78.2 us; the launch traced here: 77.9 us
  starting transfers between devices  32 us (41%)
  waiting for transfers between devices  24.4 us (31%)
  Pallas kernels  14.1 us (18%)
  local copies, waits for them, and re-layouts  4.93 us (6%)
  between operations  1.15 us (1%)
  matrix products  1.12 us (1%)
    ppermute x24, starting transfers between devices, shifted(): return lax.ppermute(value, axis, pairs)  32 us
    ppermute x24, waiting for transfers between devices, shifted(): return lax.ppermute(value, axis, pairs)  24.4 us
    pallas_call x1, Pallas kernels, finish(): pl.pallas_call(functools.partial(finish_body, replicas), grid=(rows // ti...  5.83 us
    pallas_call x2, Pallas kernels, inverse_factor(): state = call(state)  4.79 us
    unnamed x8, local copies, waits for them, and re-layouts  4.48 us
    pallas_call x1, Pallas kernels, basis(): pl.pallas_call(basis_body, out_shape=jax.ShapeDtypeStruct((acts.shape[0],...  1.89 us
  transfers between devices with their start and end apart: 24, of which 13 were waited for; matrix products, arithmetic and copies ran while one was open for 5% of the time, Pallas kernels for 9%

profile of v1, /device:TPU:0, one launch (start us, length us, event | category | flops | bytes accessed | tf_op | source)
XLA Modules:
  0.0 77.9 jit_solution(14990285226685322964)
XLA Ops:
  0.6 0.0 copy-start
  0.6 0.9 %copy-done = bf16[128,1024]{1,0:T(8,128)(2,1)S(1)} copy-done((bf16[128,1024]{1,0:T(8,128)(2,1)S(1)}, bf16[128,1024]{1,0:T(8,128)(2,1)}, u32[]{:S(2)}) %copy-start) | copy-done | bytes 262168
  1.6 1.0 %copy-done.2 = f32[1024,128]{1,0:T(8,128)S(1)} copy-done((f32[1024,128]{1,0:T(8,128)S(1)}, f32[1024,128]{1,0:T(8,128)}, u32[]{:S(2)}) %copy-start.2) | copy-done | bytes 524312
  2.6 0.4 project.1.refs_0_
  3.0 3.0 %collective-permute-start = (f32[128,128]{1,0:T(8,128)S(1)}, f32[128,128]{1,0:T(8,128)S(1)}, u32[]{:S(2)}, u32[]{:S(2)}) collective-permute-start(f32[128,128]{1,0:T(8,128)S(1)} %project.1.refs_0_), channel_id=1, source_target_pairs={{0,1},{1,0},{2,3},{3,2},{4,5},{5,4},{6,7},{7,6},{8,9},{9,8},{10,11... | collective-permute-start | bytes 196616 | tf_op jit(solution)/shard_map/ppermute | solution.py:50
  6.0 1.1 %copy.6 = bf16[128,1024]{0,1:T(8,128)(2,1)S(1)} copy(bf16[128,1024]{1,0:T(8,128)(2,1)} %grads_ref.3) | data formatting | bytes 524288 | tf_op args[1]
  7.2 1.4 %copy.5 = bf16[128,2304]{0,1:T(8,128)(2,1)S(1)} copy(bf16[128,2304]{1,0:T(8,128)(2,1)} %param.3) | data formatting | bytes 1179648 | tf_op args[0]
  8.6 0.0 collective-permute-done.refs_1_
  8.6 0.4 apply.2
  9.0 0.1 collective-permute-start.1
  9.1 1.5 %collective-permute-done.1 = f32[576,128]{1,0:T(8,128)S(1)} collective-permute-done((f32[576,128]{1,0:T(8,128)S(1)}, f32[576,128]{1,0:T(8,128)S(1)}, u32[]{:S(2)}, u32[]{:S(2)}) %collective-permute-start.1) | collective-permute-done | bytes 294944 | tf_op jit(solution)/shard_map/ppermute | solution.py:50
  10.7 1.8 %collective-permute-start.2 = (f32[144,128]{1,0:T(8,128)S(1)}, f32[144,128]{1,0:T(8,128)S(1)}, u32[]{:S(2)}, u32[]{:S(2)}) collective-permute-start(f32[144,128]{1,0:T(8,128)S(1)} %get-tuple-element.18), channel_id=1, source_target_pairs={{0,4},{2,6},{4,0},{6,2},{8,12},{10,14},{12,8},{14,10},{16,20},{18,... | collective-permute-start | bytes 221192 | tf_op jit(solution)/shard_map/ppermute | solution.py:50
  12.5 1.5 %collective-permute-start.4 = (f32[144,128]{1,0:T(8,128)S(1)}, f32[144,128]{1,0:T(8,128)S(1)}, u32[]{:S(2)}, u32[]{:S(2)}) collective-permute-start(f32[144,128]{1,0:T(8,128)S(1)} %get-tuple-element.19), channel_id=1, source_target_pairs={{0,12},{2,14},{4,8},{6,10},{8,4},{10,6},{12,0},{14,2},{16,28},{18,... | collective-permute-start | bytes 221192 | tf_op jit(solution)/shard_map/ppermute | solution.py:50
  14.1 0.2 collective-permute-start.3
  14.3 1.6 %collective-permute-done.2 = f32[144,128]{1,0:T(8,128)S(1)} collective-permute-done((f32[144,128]{1,0:T(8,128)S(1)}, f32[144,128]{1,0:T(8,128)S(1)}, u32[]{:S(2)}, u32[]{:S(2)}) %collective-permute-start.2) | collective-permute-done | bytes 73760 | tf_op jit(solution)/shard_map/ppermute | solution.py:50
  15.9 2.5 %collective-permute-done.4 = f32[144,128]{1,0:T(8,128)S(1)} collective-permute-done((f32[144,128]{1,0:T(8,128)S(1)}, f32[144,128]{1,0:T(8,128)S(1)}, u32[]{:S(2)}, u32[]{:S(2)}) %collective-permute-start.4) | collective-permute-done | bytes 73760 | tf_op jit(solution)/shard_map/ppermute | solution.py:50
  18.4 0.0 collective-permute-done.3
  18.5 2.7 %collective-permute-start.5 = (f32[72,128]{1,0:T(8,128)S(1)}, f32[72,128]{1,0:T(8,128)S(1)}, u32[]{:S(2)}, u32[]{:S(2)}) collective-permute-start(f32[72,128]{1,0:T(8,128)S(1)} %constant_dynamic-slice_fusion.5), channel_id=1, source_target_pairs={{0,16},{2,18},{4,20},{6,22},{8,24},{10,26},{12,28},{14,30},{16,0},... | collective-permute-start | bytes 110600 | tf_op jit(solution)/shard_map/ppermute | solution.py:50
  21.1 2.3 %collective-permute-done.5 = f32[72,128]{1,0:T(8,128)S(1)} collective-permute-done((f32[72,128]{1,0:T(8,128)S(1)}, f32[72,128]{1,0:T(8,128)S(1)}, u32[]{:S(2)}, u32[]{:S(2)}) %collective-permute-start.5) | collective-permute-done | bytes 36896 | tf_op jit(solution)/shard_map/ppermute | solution.py:50
  23.4 2.8 %collective-permute-start.6 = (f32[72,128]{1,0:T(8,128)S(1)}, f32[72,128]{1,0:T(8,128)S(1)}, u32[]{:S(2)}, u32[]{:S(2)}) collective-permute-start(f32[72,128]{1,0:T(8,128)S(1)} %get-tuple-element.17), channel_id=1, source_target_pairs={{0,16},{2,18},{4,20},{6,22},{8,24},{10,26},{12,28},{14,30},{16,0},... | collective-permute-start | bytes 110600 | tf_op jit(solution)/shard_map/ppermute | solution.py:50
  26.2 2.2 %collective-permute-done.6 = f32[72,128]{1,0:T(8,128)S(1)} collective-permute-done((f32[72,128]{1,0:T(8,128)S(1)}, f32[72,128]{1,0:T(8,128)S(1)}, u32[]{:S(2)}, u32[]{:S(2)}) %collective-permute-start.6) | collective-permute-done | bytes 36896 | tf_op jit(solution)/shard_map/ppermute | solution.py:50
  28.3 2.3 %collective-permute-start.9 = (f32[144,128]{1,0:T(8,128)S(1)}, f32[144,128]{1,0:T(8,128)S(1)}, u32[]{:S(2)}, u32[]{:S(2)}) collective-permute-start(f32[144,128]{1,0:T(8,128)S(1)} %constant_dynamic-update-slice_fusion.14), channel_id=1, source_target_pairs={{0,12},{2,14},{4,8},{6,10},{8,4},{10,6},{12,0},{14,2},{16,28},{18,... | collective-permute-start | bytes 221192 | tf_op jit(solution)/shard_map/ppermute | solution.py:50
  30.6 0.7 collective-permute-start.8
  31.3 0.5 collective-permute-start.7
  31.9 3.8 %collective-permute-done.7 = f32[144,128]{1,0:T(8,128)S(1)} collective-permute-done((f32[144,128]{1,0:T(8,128)S(1)}, f32[144,128]{1,0:T(8,128)S(1)}, u32[]{:S(2)}, u32[]{:S(2)}) %collective-permute-start.7) | collective-permute-done | bytes 73760 | tf_op jit(solution)/shard_map/ppermute | solution.py:50
  35.7 0.0 collective-permute-done.8
  35.7 0.0 collective-permute-done.9
  35.7 0.1 collective-permute-start.10
  35.9 1.5 %collective-permute-done.10 = f32[576,128]{1,0:T(8,128)S(1)} collective-permute-done((f32[576,128]{1,0:T(8,128)S(1)}, f32[576,128]{1,0:T(8,128)S(1)}, u32[]{:S(2)}, u32[]{:S(2)}) %collective-permute-start.10) | collective-permute-done | bytes 294944 | tf_op jit(solution)/shard_map/ppermute | solution.py:50
  37.4 0.4 weigh.1.refs_0_
  37.9 1.6 %collective-permute-start.13 = (f32[128,128]{1,0:T(8,128)S(1)}, f32[128,128]{1,0:T(8,128)S(1)}, u32[]{:S(2)}, u32[]{:S(2)}) collective-permute-start(f32[128,128]{1,0:T(8,128)S(1)} %weigh.1.refs_0_), channel_id=1, source_target_pairs={{0,1},{1,0},{2,3},{3,2},{4,5},{5,4},{6,7},{7,6},{8,9},{9,8},{10,11... | collective-permute-start | bytes 196616 | tf_op jit(solution)/shard_map/ppermute | solution.py:50
  39.4 2.8 %collective-permute-done.13.refs_1_ = f32[128,128]{1,0:T(8,128)S(1)} collective-permute-done((f32[128,128]{1,0:T(8,128)S(1)}, f32[128,128]{1,0:T(8,128)S(1)}, u32[]{:S(2)}, u32[]{:S(2)}) %collective-permute-start.13) | collective-permute-done | bytes 65568 | tf_op jit(solution)/shard_map/ppermute | solution.py:50
  42.2 0.4 apply.3
  42.6 0.1 collective-permute-start.14
  42.7 1.1 %fusion = f32[128,128]{1,0:T(8,128)S(1)} fusion(f32[1152,128]{1,0:T(8,128)S(1)} %constant_dynamic-update-slice_fusion.8.left_ref.refs_0_), kind=kOutput, calls=%fused_computation.33 | convolution fusion | flops 226492416 | bytes 655360 | tf_op jit(solution)/shard_map/dot_general | solution.py:336
  43.8 1.6 %collective-permute-start.11 = (f32[128,128]{1,0:T(8,128)S(1)}, f32[128,128]{1,0:T(8,128)S(1)}, u32[]{:S(2)}, u32[]{:S(2)}) collective-permute-start(f32[128,128]{1,0:T(8,128)S(1)} %fusion), channel_id=1, source_target_pairs={{0,1},{1,0},{2,3},{3,2},{4,5},{5,4},{6,7},{7,6},{8,9},{9,8},{10,11... | collective-permute-start | bytes 196616 | tf_op jit(solution)/shard_map/ppermute | solution.py:50
  45.4 0.0 collective-permute-done.14
  45.5 0.6 collective-permute-start.15
  46.0 2.3 %collective-permute-start.17 = (f32[128,128]{1,0:T(8,128)S(1)}, f32[128,128]{1,0:T(8,128)S(1)}, u32[]{:S(2)}, u32[]{:S(2)}) collective-permute-start(f32[128,128]{1,0:T(8,128)S(1)} %get-tuple-element.22), channel_id=1, source_target_pairs={{0,12},{2,14},{4,8},{6,10},{8,4},{10,6},{12,0},{14,2},{16,28},{18,... | collective-permute-start | bytes 196616 | tf_op jit(solution)/shard_map/ppermute | solution.py:50
  48.3 0.7 collective-permute-start.16
  49.0 0.1 pad_add_fusion.place_ref
  49.1 0.5 collective-permute-start.12
  49.6 0.0 collective-permute-done.11
  49.6 0.9 %collective-permute-done.15 = f32[128,128]{1,0:T(8,128)S(1)} collective-permute-done((f32[128,128]{1,0:T(8,128)S(1)}, f32[128,128]{1,0:T(8,128)S(1)}, u32[]{:S(2)}, u32[]{:S(2)}) %collective-permute-start.15) | collective-permute-done | bytes 65568 | tf_op jit(solution)/shard_map/ppermute | solution.py:50
  50.5 1.3 %collective-permute-done.17 = f32[128,128]{1,0:T(8,128)S(1)} collective-permute-done((f32[128,128]{1,0:T(8,128)S(1)}, f32[128,128]{1,0:T(8,128)S(1)}, u32[]{:S(2)}, u32[]{:S(2)}) %collective-permute-start.17) | collective-permute-done | bytes 65568 | tf_op jit(solution)/shard_map/ppermute | solution.py:50
  51.8 0.8 %collective-permute-done.16 = f32[128,128]{1,0:T(8,128)S(1)} collective-permute-done((f32[128,128]{1,0:T(8,128)S(1)}, f32[128,128]{1,0:T(8,128)S(1)}, u32[]{:S(2)}, u32[]{:S(2)}) %collective-permute-start.16) | collective-permute-done | bytes 65568 | tf_op jit(solution)/shard_map/ppermute | solution.py:50
  52.7 3.4 %collective-permute-start.18 = (f32[64,128]{1,0:T(8,128)S(1)}, f32[64,128]{1,0:T(8,128)S(1)}, u32[]{:S(2)}, u32[]{:S(2)}) collective-permute-start(f32[64,128]{1,0:T(8,128)S(1)} %constant_dynamic-slice_fusion), channel_id=1, source_target_pairs={{0,16},{2,18},{4,20},{6,22},{8,24},{10,26},{12,28},{14,30},{16,0},... | collective-permute-start | bytes 98312 | tf_op jit(solution)/shard_map/ppermute | solution.py:50
  56.0 2.6 %shard_map.50.state_ref = f32[128,128]{1,0:T(8,128)S(1)} custom-call(f32[128,128]{1,0:T(8,128)S(1)} %add.135.state_ref), custom_call_target="tpu_custom_call" | custom-call | flops 3000000000 | bytes 131072 | tf_op jit(solution)/shard_map/pallas_call | solution.py:149
  58.7 0.0 collective-permute-done.18
  58.7 2.2 %collective-permute-start.19 = (f32[64,128]{1,0:T(8,128)S(1)}, f32[64,128]{1,0:T(8,128)S(1)}, u32[]{:S(2)}, u32[]{:S(2)}) collective-permute-start(f32[64,128]{1,0:T(8,128)S(1)} %get-tuple-element.15), channel_id=1, source_target_pairs={{0,16},{2,18},{4,20},{6,22},{8,24},{10,26},{12,28},{14,30},{16,0},... | collective-permute-start | bytes 98312 | tf_op jit(solution)/shard_map/ppermute | solution.py:50
  60.9 2.2 %shard_map.51.inverse_ref = f32[128,128]{1,0:T(8,128)S(1)} custom-call(f32[128,128]{1,0:T(8,128)S(1)} %shard_map.50.state_ref), custom_call_target="tpu_custom_call" | custom-call | flops 3000000000 | bytes 131072 | tf_op jit(solution)/shard_map/pallas_call | solution.py:149
  63.1 0.5 collective-permute-done.19
  63.6 1.2 %collective-permute-start.22 = (f32[128,128]{1,0:T(8,128)S(1)}, f32[128,128]{1,0:T(8,128)S(1)}, u32[]{:S(2)}, u32[]{:S(2)}) collective-permute-start(f32[128,128]{1,0:T(8,128)S(1)} %constant_dynamic-update-slice_fusion.6), channel_id=1, source_target_pairs={{0,12},{2,14},{4,8},{6,10},{8,4},{10,6},{12,0},{14,2},{16,28},{18,... | collective-permute-start | bytes 196616 | tf_op jit(solution)/shard_map/ppermute | solution.py:50
  64.8 0.8 %collective-permute-start.21 = (f32[128,128]{1,0:T(8,128)S(1)}, f32[128,128]{1,0:T(8,128)S(1)}, u32[]{:S(2)}, u32[]{:S(2)}) collective-permute-start(f32[128,128]{1,0:T(8,128)S(1)} %constant_dynamic-update-slice_fusion.6), channel_id=1, source_target_pairs={{0,8},{2,10},{4,12},{6,14},{8,0},{10,2},{12,4},{14,6},{16,24},{18,... | collective-permute-start | bytes 196616 | tf_op jit(solution)/shard_map/ppermute | solution.py:50
  65.6 1.5 %collective-permute-start.20 = (f32[128,128]{1,0:T(8,128)S(1)}, f32[128,128]{1,0:T(8,128)S(1)}, u32[]{:S(2)}, u32[]{:S(2)}) collective-permute-start(f32[128,128]{1,0:T(8,128)S(1)} %constant_dynamic-update-slice_fusion.6), channel_id=1, source_target_pairs={{0,4},{2,6},{4,0},{6,2},{8,12},{10,14},{12,8},{14,10},{16,20},{18,... | collective-permute-start | bytes 196616 | tf_op jit(solution)/shard_map/ppermute | solution.py:50
  67.1 0.0 copy-start.1
  67.1 2.8 %collective-permute-done.20 = f32[128,128]{1,0:T(8,128)S(1)} collective-permute-done((f32[128,128]{1,0:T(8,128)S(1)}, f32[128,128]{1,0:T(8,128)S(1)}, u32[]{:S(2)}, u32[]{:S(2)}) %collective-permute-start.20) | collective-permute-done | bytes 65568 | tf_op jit(solution)/shard_map/ppermute | solution.py:50
  69.9 0.0 collective-permute-done.21
  69.9 0.0 collective-permute-done.22
  70.0 0.1 collective-permute-start.23
  70.1 0.0 collective-permute-done.12.refs_1_
  70.1 1.9 %basis.1.mine_ref.tall_ref = bf16[2304,512]{1,0:T(8,128)(2,1)S(1)} custom-call(s32[2]{0:T(128)S(1)} %pad_add_fusion.place_ref, f32[128,128]{1,0:T(8,128)S(1)} %shard_map.51.inverse_ref, bf16[2304,128]{1,0:T(8,128)(2,1)S(1)} %bitcast.9, f32[1152,128]{1,0:T(8,128)S(1)} %constant_dynamic-update-slice_fusion.8.left_ref.refs_0_, ...), custom_call_target="tpu_custom_call" | custom-call | flops 2000000000 | bytes 131072 | tf_op jit(solution)/shard_map/basis/pallas_call | solution.py:257
  72.0 0.0 collective-permute-done.23
  72.1 5.8 %finish.1 = (f32[144,1024]{1,0:T(8,128)}, bf16[2304,1024]{1,0:T(8,128)(2,1)}) custom-call(s32[1]{0:T(128)} %bitcast.place_ref, bf16[2304,512]{1,0:T(8,128)(2,1)S(1)} %basis.1.mine_ref.tall_ref, bf16[2304,512]{1,0:T(8,128)(2,1)S(1)} %basis.1.mine_ref.tall_ref, bf16[128,1024]{1,0:T(8,128)(2,1)S(1)} %copy-done.1, ...), custom_call_target="tpu_custom_call" | custom-call | tf_op jit(solution)/shard_map/finish/pallas_call | solution.py:295
  (35 shorter events, 0.6 us)
Async XLA Ops:
  0.6 1.0 %copy-start = (bf16[128,1024]{1,0:T(8,128)(2,1)S(1)}, bf16[128,1024]{1,0:T(8,128)(2,1)}, u32[]{:S(2)}) copy-start(bf16[128,1024]{1,0:T(8,128)(2,1)} %grads_ref.3) | copy-start | bytes 786436
  1.6 1.0 %copy-start.2 = (f32[1024,128]{1,0:T(8,128)S(1)}, f32[1024,128]{1,0:T(8,128)}, u32[]{:S(2)}) copy-start(f32[1024,128]{1,0:T(8,128)} %right_ref.1) | copy-start | bytes 1572868
  3.0 5.6 %collective-permute-start = (f32[128,128]{1,0:T(8,128)S(1)}, f32[128,128]{1,0:T(8,128)S(1)}, u32[]{:S(2)}, u32[]{:S(2)}) collective-permute-start(f32[128,128]{1,0:T(8,128)S(1)} %project.1.refs_0_), channel_id=1, source_target_pairs={{0,1},{1,0},{2,3},{3,2},{4,5},{5,4},{6,7},{7,6},{8,9},{9,8},{10,11... | collective-permute-start | bytes 196616 | tf_op jit(solution)/shard_map/ppermute | solution.py:50
  9.0 1.6 %collective-permute-start.1 = (f32[576,128]{1,0:T(8,128)S(1)}, f32[576,128]{1,0:T(8,128)S(1)}, u32[]{:S(2)}, u32[]{:S(2)}) collective-permute-start(f32[576,128]{1,0:T(8,128)S(1)} %constant_dynamic-slice_fusion.9), channel_id=1, source_target_pairs={{0,2},{2,0},{4,6},{6,4},{8,10},{10,8},{12,14},{14,12},{16,18},{18,... | collective-permute-start | bytes 884744 | tf_op jit(solution)/shard_map/ppermute | solution.py:50
  10.7 5.2 %collective-permute-start.2 = (f32[144,128]{1,0:T(8,128)S(1)}, f32[144,128]{1,0:T(8,128)S(1)}, u32[]{:S(2)}, u32[]{:S(2)}) collective-permute-start(f32[144,128]{1,0:T(8,128)S(1)} %get-tuple-element.18), channel_id=1, source_target_pairs={{0,4},{2,6},{4,0},{6,2},{8,12},{10,14},{12,8},{14,10},{16,20},{18,... | collective-permute-start | bytes 221192 | tf_op jit(solution)/shard_map/ppermute | solution.py:50
  12.5 5.9 %collective-permute-start.4 = (f32[144,128]{1,0:T(8,128)S(1)}, f32[144,128]{1,0:T(8,128)S(1)}, u32[]{:S(2)}, u32[]{:S(2)}) collective-permute-start(f32[144,128]{1,0:T(8,128)S(1)} %get-tuple-element.19), channel_id=1, source_target_pairs={{0,12},{2,14},{4,8},{6,10},{8,4},{10,6},{12,0},{14,2},{16,28},{18,... | collective-permute-start | bytes 221192 | tf_op jit(solution)/shard_map/ppermute | solution.py:50
  14.1 4.4 %collective-permute-start.3 = (f32[144,128]{1,0:T(8,128)S(1)}, f32[144,128]{1,0:T(8,128)S(1)}, u32[]{:S(2)}, u32[]{:S(2)}) collective-permute-start(f32[144,128]{1,0:T(8,128)S(1)} %get-tuple-element.20), channel_id=1, source_target_pairs={{0,8},{2,10},{4,12},{6,14},{8,0},{10,2},{12,4},{14,6},{16,24},{18,... | collective-permute-start | bytes 221192 | tf_op jit(solution)/shard_map/ppermute | solution.py:50
  18.5 4.9 %collective-permute-start.5 = (f32[72,128]{1,0:T(8,128)S(1)}, f32[72,128]{1,0:T(8,128)S(1)}, u32[]{:S(2)}, u32[]{:S(2)}) collective-permute-start(f32[72,128]{1,0:T(8,128)S(1)} %constant_dynamic-slice_fusion.5), channel_id=1, source_target_pairs={{0,16},{2,18},{4,20},{6,22},{8,24},{10,26},{12,28},{14,30},{16,0},... | collective-permute-start | bytes 110600 | tf_op jit(solution)/shard_map/ppermute | solution.py:50
  23.4 4.9 %collective-permute-start.6 = (f32[72,128]{1,0:T(8,128)S(1)}, f32[72,128]{1,0:T(8,128)S(1)}, u32[]{:S(2)}, u32[]{:S(2)}) collective-permute-start(f32[72,128]{1,0:T(8,128)S(1)} %get-tuple-element.17), channel_id=1, source_target_pairs={{0,16},{2,18},{4,20},{6,22},{8,24},{10,26},{12,28},{14,30},{16,0},... | collective-permute-start | bytes 110600 | tf_op jit(solution)/shard_map/ppermute | solution.py:50
  28.3 7.4 %collective-permute-start.9 = (f32[144,128]{1,0:T(8,128)S(1)}, f32[144,128]{1,0:T(8,128)S(1)}, u32[]{:S(2)}, u32[]{:S(2)}) collective-permute-start(f32[144,128]{1,0:T(8,128)S(1)} %constant_dynamic-update-slice_fusion.14), channel_id=1, source_target_pairs={{0,12},{2,14},{4,8},{6,10},{8,4},{10,6},{12,0},{14,2},{16,28},{18,... | collective-permute-start | bytes 221192 | tf_op jit(solution)/shard_map/ppermute | solution.py:50
  30.6 5.1 %collective-permute-start.8 = (f32[144,128]{1,0:T(8,128)S(1)}, f32[144,128]{1,0:T(8,128)S(1)}, u32[]{:S(2)}, u32[]{:S(2)}) collective-permute-start(f32[144,128]{1,0:T(8,128)S(1)} %constant_dynamic-update-slice_fusion.14), channel_id=1, source_target_pairs={{0,8},{2,10},{4,12},{6,14},{8,0},{10,2},{12,4},{14,6},{16,24},{18,... | collective-permute-start | bytes 221192 | tf_op jit(solution)/shard_map/ppermute | solution.py:50
  31.3 4.4 %collective-permute-start.7 = (f32[144,128]{1,0:T(8,128)S(1)}, f32[144,128]{1,0:T(8,128)S(1)}, u32[]{:S(2)}, u32[]{:S(2)}) collective-permute-start(f32[144,128]{1,0:T(8,128)S(1)} %constant_dynamic-update-slice_fusion.14), channel_id=1, source_target_pairs={{0,4},{2,6},{4,0},{6,2},{8,12},{10,14},{12,8},{14,10},{16,20},{18,... | collective-permute-start | bytes 221192 | tf_op jit(solution)/shard_map/ppermute | solution.py:50
  35.7 1.6 %collective-permute-start.10 = (f32[576,128]{1,0:T(8,128)S(1)}, f32[576,128]{1,0:T(8,128)S(1)}, u32[]{:S(2)}, u32[]{:S(2)}) collective-permute-start(f32[576,128]{1,0:T(8,128)S(1)} %constant_dynamic-update-slice_fusion.10), channel_id=1, source_target_pairs={{0,2},{2,0},{4,6},{6,4},{8,10},{10,8},{12,14},{14,12},{16,18},{18,... | collective-permute-start | bytes 884744 | tf_op jit(solution)/shard_map/ppermute | solution.py:50
  37.9 4.3 %collective-permute-start.13 = (f32[128,128]{1,0:T(8,128)S(1)}, f32[128,128]{1,0:T(8,128)S(1)}, u32[]{:S(2)}, u32[]{:S(2)}) collective-permute-start(f32[128,128]{1,0:T(8,128)S(1)} %weigh.1.refs_0_), channel_id=1, source_target_pairs={{0,1},{1,0},{2,3},{3,2},{4,5},{5,4},{6,7},{7,6},{8,9},{9,8},{10,11... | collective-permute-start | bytes 196616 | tf_op jit(solution)/shard_map/ppermute | solution.py:50
  42.6 2.8 %collective-permute-start.14 = (f32[512,128]{1,0:T(8,128)S(1)}, f32[512,128]{1,0:T(8,128)S(1)}, u32[]{:S(2)}, u32[]{:S(2)}) collective-permute-start(f32[512,128]{1,0:T(8,128)S(1)} %constant_dynamic-slice_fusion.4), channel_id=1, source_target_pairs={{0,2},{2,0},{4,6},{6,4},{8,10},{10,8},{12,14},{14,12},{16,18},{18,... | collective-permute-start | bytes 786440 | tf_op jit(solution)/shard_map/ppermute | solution.py:50
  43.8 5.8 %collective-permute-start.11 = (f32[128,128]{1,0:T(8,128)S(1)}, f32[128,128]{1,0:T(8,128)S(1)}, u32[]{:S(2)}, u32[]{:S(2)}) collective-permute-start(f32[128,128]{1,0:T(8,128)S(1)} %fusion), channel_id=1, source_target_pairs={{0,1},{1,0},{2,3},{3,2},{4,5},{5,4},{6,7},{7,6},{8,9},{9,8},{10,11... | collective-permute-start | bytes 196616 | tf_op jit(solution)/shard_map/ppermute | solution.py:50
  45.5 5.0 %collective-permute-start.15 = (f32[128,128]{1,0:T(8,128)S(1)}, f32[128,128]{1,0:T(8,128)S(1)}, u32[]{:S(2)}, u32[]{:S(2)}) collective-permute-start(f32[128,128]{1,0:T(8,128)S(1)} %get-tuple-element.21), channel_id=1, source_target_pairs={{0,4},{2,6},{4,0},{6,2},{8,12},{10,14},{12,8},{14,10},{16,20},{18,... | collective-permute-start | bytes 196616 | tf_op jit(solution)/shard_map/ppermute | solution.py:50
  46.0 5.7 %collective-permute-start.17 = (f32[128,128]{1,0:T(8,128)S(1)}, f32[128,128]{1,0:T(8,128)S(1)}, u32[]{:S(2)}, u32[]{:S(2)}) collective-permute-start(f32[128,128]{1,0:T(8,128)S(1)} %get-tuple-element.22), channel_id=1, source_target_pairs={{0,12},{2,14},{4,8},{6,10},{8,4},{10,6},{12,0},{14,2},{16,28},{18,... | collective-permute-start | bytes 196616 | tf_op jit(solution)/shard_map/ppermute | solution.py:50
  48.3 4.3 %collective-permute-start.16 = (f32[128,128]{1,0:T(8,128)S(1)}, f32[128,128]{1,0:T(8,128)S(1)}, u32[]{:S(2)}, u32[]{:S(2)}) collective-permute-start(f32[128,128]{1,0:T(8,128)S(1)} %get-tuple-element.23), channel_id=1, source_target_pairs={{0,8},{2,10},{4,12},{6,14},{8,0},{10,2},{12,4},{14,6},{16,24},{18,... | collective-permute-start | bytes 196616 | tf_op jit(solution)/shard_map/ppermute | solution.py:50
  49.1 21.0 %collective-permute-start.12 = (f32[1152,128]{1,0:T(8,128)S(1)}, f32[1152,128]{1,0:T(8,128)S(1)}, u32[]{:S(2)}, u32[]{:S(2)}) collective-permute-start(f32[1152,128]{1,0:T(8,128)S(1)} %constant_dynamic-update-slice_fusion.8.left_ref.refs_0_), channel_id=1, source_target_pairs={{0,1},{1,0},{2,3},{3,2},{4,5},{5,4},{6,7},{7,6},{8,9},{9,8},{10,11... | collective-permute-start | bytes 1769480 | tf_op jit(solution)/shard_map/ppermute | solution.py:50
  52.7 6.0 %collective-permute-start.18 = (f32[64,128]{1,0:T(8,128)S(1)}, f32[64,128]{1,0:T(8,128)S(1)}, u32[]{:S(2)}, u32[]{:S(2)}) collective-permute-start(f32[64,128]{1,0:T(8,128)S(1)} %constant_dynamic-slice_fusion), channel_id=1, source_target_pairs={{0,16},{2,18},{4,20},{6,22},{8,24},{10,26},{12,28},{14,30},{16,0},... | collective-permute-start | bytes 98312 | tf_op jit(solution)/shard_map/ppermute | solution.py:50
  58.7 4.9 %collective-permute-start.19 = (f32[64,128]{1,0:T(8,128)S(1)}, f32[64,128]{1,0:T(8,128)S(1)}, u32[]{:S(2)}, u32[]{:S(2)}) collective-permute-start(f32[64,128]{1,0:T(8,128)S(1)} %get-tuple-element.15), channel_id=1, source_target_pairs={{0,16},{2,18},{4,20},{6,22},{8,24},{10,26},{12,28},{14,30},{16,0},... | collective-permute-start | bytes 98312 | tf_op jit(solution)/shard_map/ppermute | solution.py:50
  63.6 6.3 %collective-permute-start.22 = (f32[128,128]{1,0:T(8,128)S(1)}, f32[128,128]{1,0:T(8,128)S(1)}, u32[]{:S(2)}, u32[]{:S(2)}) collective-permute-start(f32[128,128]{1,0:T(8,128)S(1)} %constant_dynamic-update-slice_fusion.6), channel_id=1, source_target_pairs={{0,12},{2,14},{4,8},{6,10},{8,4},{10,6},{12,0},{14,2},{16,28},{18,... | collective-permute-start | bytes 196616 | tf_op jit(solution)/shard_map/ppermute | solution.py:50
  64.8 5.1 %collective-permute-start.21 = (f32[128,128]{1,0:T(8,128)S(1)}, f32[128,128]{1,0:T(8,128)S(1)}, u32[]{:S(2)}, u32[]{:S(2)}) collective-permute-start(f32[128,128]{1,0:T(8,128)S(1)} %constant_dynamic-update-slice_fusion.6), channel_id=1, source_target_pairs={{0,8},{2,10},{4,12},{6,14},{8,0},{10,2},{12,4},{14,6},{16,24},{18,... | collective-permute-start | bytes 196616 | tf_op jit(solution)/shard_map/ppermute | solution.py:50
  65.6 4.3 %collective-permute-start.20 = (f32[128,128]{1,0:T(8,128)S(1)}, f32[128,128]{1,0:T(8,128)S(1)}, u32[]{:S(2)}, u32[]{:S(2)}) collective-permute-start(f32[128,128]{1,0:T(8,128)S(1)} %constant_dynamic-update-slice_fusion.6), channel_id=1, source_target_pairs={{0,4},{2,6},{4,0},{6,2},{8,12},{10,14},{12,8},{14,10},{16,20},{18,... | collective-permute-start | bytes 196616 | tf_op jit(solution)/shard_map/ppermute | solution.py:50
  67.1 5.0 %copy-start.1 = (bf16[128,1024]{1,0:T(8,128)(2,1)S(1)}, bf16[128,1024]{1,0:T(8,128)(2,1)}, u32[]{:S(2)}) copy-start(bf16[128,1024]{1,0:T(8,128)(2,1)} %grads_ref.3) | copy-start | bytes 786436
  70.0 2.1 %collective-permute-start.23 = (f32[512,128]{1,0:T(8,128)S(1)}, f32[512,128]{1,0:T(8,128)S(1)}, u32[]{:S(2)}, u32[]{:S(2)}) collective-permute-start(f32[512,128]{1,0:T(8,128)S(1)} %constant_dynamic-update-slice_fusion.2), channel_id=1, source_target_pairs={{0,2},{2,0},{4,6},{6,4},{8,10},{10,8},{12,14},{14,12},{16,18},{18,... | collective-permute-start | bytes 786440 | tf_op jit(solution)/shard_map/ppermute | solution.py:50

commit v2 on v1

--- a/solution.py
+++ b/solution.py
@@ -50,9 +50,9 @@
     return lax.ppermute(value, axis, pairs)
 
 
-def scatter_sum(value, axis):
-    position = lax.axis_index(axis)
-    for radix, stride in stages_of(axis):
+def scatter_sum(value, axis, tied=()):
+    position, stages = lax.axis_index(axis), stages_of(axis)
+    for stage, (radix, stride) in enumerate(stages[:-1]):
         digit = position // stride % radix
         rows = value.shape[0] // radix
         received = []
@@ -62,12 +62,29 @@
         value = lax.dynamic_slice_in_dim(value, digit * rows, rows, 0)
         for block in received:
             value = value + block
-    return value
+        if stage == 0:
+            value, tied = lax.optimization_barrier((value, tied))
+    radix, stride = stages[-1]
+    received = [shifted(value, axis, radix, stride, step) for step in range(1, radix)]
+    digit = position // stride % radix
+    if radix == 2:
+        return value + received[0], tied
+    return ordered_sum([value] + received, digit), tied
+
+
+def ordered_sum(values, digit):
+    radix, total = len(values), None
+    for place in range(radix):
+        term = values[0]
+        for step in range(1, radix):
+            term = jnp.where(source(digit, step, radix) == place, values[step], term)
+        total = term if total is None else total + term
+    return total
 
 
 def gather_rows(value, axis):
     position = lax.axis_index(axis)
-    for radix, stride in reversed(stages_of(axis)):
+    for radix, stride in reversed(stages_of(axis)[:-1]):
         digit = position // stride % radix
         rows = value.shape[0]
         whole = jnp.zeros((radix * rows, value.shape[1]), value.dtype)
@@ -77,6 +94,10 @@
             whole = lax.dynamic_update_slice_in_dim(whole, block, source(digit, step, radix) * rows, 0)
         value = whole
     return value
+
+
+def blocks_of(axis):
+    return lax.axis_size(axis) // stages_of(axis)[-1][0]
 
 
 def padded_rows(value, multiple):
@@ -328,17 +349,20 @@
     acts, grads = lax.optimization_barrier((activations.T, out_grads.T))
 
     projected, _ = sent_all(project(out_grads, right_prev), "tp")
-    left_part = padded_rows(apply(place, acts, my_rows, projected), replicas)
-    left_own = gather_rows(scatter_sum(left_part, "dp"), "dp")[:my_rows]
+    left_part = padded_rows(apply(place, acts, my_rows, projected), blocks_of("dp"))
+    left_own, _ = scatter_sum(left_part, "dp")
+    left_own = gather_rows(left_own, "dp")[:my_rows]
 
     weighted_own, left_own = lax.optimization_barrier((weigh(place, acts, left_own), left_own))
     weighted, _ = sent_all(weighted_own, "tp")
     gram = jnp.dot(left_own.T, left_own, precision=HI)
     grams, _ = sent_all(gram, "tp")
+    left_own, weighted[0] = lax.optimization_barrier((left_own, weighted[0]))
+    right_part = apply(origin, grads, my_columns, weighted)
+    right_part = padded_rows(right_part, blocks_of("dp"))
+    right_sum, grams = scatter_sum(right_part, "dp", tied=grams)
+    right_sum = gather_rows(right_sum, "dp")[:my_columns]
     gram = sum(grams[1:], grams[0])
-    left_own, weighted[0] = lax.optimization_barrier((left_own, weighted[0]))
-    right_part = padded_rows(apply(origin, grads, my_columns, weighted), replicas)
-    right_sum = gather_rows(scatter_sum(right_part, "dp"), "dp")[:my_columns]
 
     parts, places = sent_all(left_own, "tp")
     inverse = inverse_factor(gram)

time: 78.2 us -> 74.9 us (0.958)
  starting transfers between devices: 32 us -> 28.2 us
    ppermute x24 -> x22, starting transfers between devices: 32 us -> 28.2 us  [shifted(): return lax.ppermute(value, axis, pairs)]
    ppermute x24 -> x22, waiting for transfers between devices: 24.4 us -> 25.1 us  [shifted(): return lax.ppermute(value, axis, pairs)]
  transfers between devices with their start and end apart: 24 -> 22, of which waited for: 13 -> 14; matrix products, arithmetic and copies ran while one was open for 5% -> 5% of each run, Pallas kernels for 9% -> 9%
where the time goes in v2:
time: 74.9 us; the launch traced here: 74.6 us
  starting transfers between devices  28.2 us (38%)
  waiting for transfers between devices  25.1 us (34%)
  Pallas kernels  14.1 us (19%)
  local copies, waits for them, and re-layouts  4.84 us (6%)
  matrix products  1.12 us (1%)
  between operations  1.05 us (1%)
    ppermute x22, starting transfers between devices, shifted(): return lax.ppermute(value, axis, pairs)  28.2 us
    ppermute x22, waiting for transfers between devices, shifted(): return lax.ppermute(value, axis, pairs)  25.1 us
    pallas_call x1, Pallas kernels, finish(): pl.pallas_call(functools.partial(finish_body, replicas), grid=(rows // ti...  5.83 us
    pallas_call x2, Pallas kernels, inverse_factor(): state = call(state)  4.79 us
    unnamed x8, local copies, waits for them, and re-layouts  4.48 us
    pallas_call x1, Pallas kernels, basis(): pl.pallas_call(basis_body, out_shape=jax.ShapeDtypeStruct((acts.shape[0],...  1.89 us
  transfers between devices with their start and end apart: 22, of which 14 were waited for; matrix products, arithmetic and copies ran while one was open for 5% of the time, Pallas kernels for 9%

profile of v2, /device:TPU:0, one launch (start us, length us, event | category | flops | bytes accessed | tf_op | source)
XLA Modules:
  0.0 74.6 jit_solution(2029686264294227911)
XLA Ops:
  0.6 0.0 copy-start
  0.6 0.9 %copy-done = bf16[128,1024]{1,0:T(8,128)(2,1)S(1)} copy-done((bf16[128,1024]{1,0:T(8,128)(2,1)S(1)}, bf16[128,1024]{1,0:T(8,128)(2,1)}, u32[]{:S(2)}) %copy-start) | copy-done | bytes 262168
  1.6 0.0 copy-start.2
  1.6 1.0 %copy-done.2 = f32[1024,128]{1,0:T(8,128)S(1)} copy-done((f32[1024,128]{1,0:T(8,128)S(1)}, f32[1024,128]{1,0:T(8,128)}, u32[]{:S(2)}) %copy-start.2) | copy-done | bytes 524312
  2.6 0.4 project.1.refs_0_
  3.0 3.0 %collective-permute-start = (f32[128,128]{1,0:T(8,128)S(1)}, f32[128,128]{1,0:T(8,128)S(1)}, u32[]{:S(2)}, u32[]{:S(2)}) collective-permute-start(f32[128,128]{1,0:T(8,128)S(1)} %project.1.refs_0_), channel_id=1, source_target_pairs={{0,1},{1,0},{2,3},{3,2},{4,5},{5,4},{6,7},{7,6},{8,9},{9,8},{10,11... | collective-permute-start | bytes 196616 | tf_op jit(solution)/shard_map/ppermute | solution.py:50
  6.0 1.1 %copy.6 = bf16[128,1024]{0,1:T(8,128)(2,1)S(1)} copy(bf16[128,1024]{1,0:T(8,128)(2,1)} %grads_ref.3) | data formatting | bytes 524288 | tf_op args[1]
  7.2 1.4 %copy.5 = bf16[128,2304]{0,1:T(8,128)(2,1)S(1)} copy(bf16[128,2304]{1,0:T(8,128)(2,1)} %param.3) | data formatting | bytes 1179648 | tf_op args[0]
  8.6 0.0 collective-permute-done.refs_1_
  8.6 0.4 apply.2
  9.0 0.1 collective-permute-start.1
  9.1 1.5 %collective-permute-done.1 = f32[576,128]{1,0:T(8,128)S(1)} collective-permute-done((f32[576,128]{1,0:T(8,128)S(1)}, f32[576,128]{1,0:T(8,128)S(1)}, u32[]{:S(2)}, u32[]{:S(2)}) %collective-permute-start.1) | collective-permute-done | bytes 294944 | tf_op jit(solution)/shard_map/ppermute | solution.py:50
  10.7 1.8 %collective-permute-start.2 = (f32[144,128]{1,0:T(8,128)S(1)}, f32[144,128]{1,0:T(8,128)S(1)}, u32[]{:S(2)}, u32[]{:S(2)}) collective-permute-start(f32[144,128]{1,0:T(8,128)S(1)} %get-tuple-element.24), channel_id=1, source_target_pairs={{0,4},{2,6},{4,0},{6,2},{8,12},{10,14},{12,8},{14,10},{16,20},{18,... | collective-permute-start | bytes 221192 | tf_op jit(solution)/shard_map/ppermute | solution.py:50
  12.5 1.5 %collective-permute-start.4 = (f32[144,128]{1,0:T(8,128)S(1)}, f32[144,128]{1,0:T(8,128)S(1)}, u32[]{:S(2)}, u32[]{:S(2)}) collective-permute-start(f32[144,128]{1,0:T(8,128)S(1)} %get-tuple-element.25), channel_id=1, source_target_pairs={{0,12},{2,14},{4,8},{6,10},{8,4},{10,6},{12,0},{14,2},{16,28},{18,... | collective-permute-start | bytes 221192 | tf_op jit(solution)/shard_map/ppermute | solution.py:50
  14.1 0.2 collective-permute-start.3
  14.3 1.6 %collective-permute-done.2 = f32[144,128]{1,0:T(8,128)S(1)} collective-permute-done((f32[144,128]{1,0:T(8,128)S(1)}, f32[144,128]{1,0:T(8,128)S(1)}, u32[]{:S(2)}, u32[]{:S(2)}) %collective-permute-start.2) | collective-permute-done | bytes 73760 | tf_op jit(solution)/shard_map/ppermute | solution.py:50
  15.9 2.5 %collective-permute-done.4 = f32[144,128]{1,0:T(8,128)S(1)} collective-permute-done((f32[144,128]{1,0:T(8,128)S(1)}, f32[144,128]{1,0:T(8,128)S(1)}, u32[]{:S(2)}, u32[]{:S(2)}) %collective-permute-start.4) | collective-permute-done | bytes 73760 | tf_op jit(solution)/shard_map/ppermute | solution.py:50
  18.4 0.0 collective-permute-done.3
  18.4 2.7 %collective-permute-start.5 = (f32[144,128]{1,0:T(8,128)S(1)}, f32[144,128]{1,0:T(8,128)S(1)}, u32[]{:S(2)}, u32[]{:S(2)}) collective-permute-start(f32[144,128]{1,0:T(8,128)S(1)} %add_add_fusion), channel_id=1, source_target_pairs={{0,16},{2,18},{4,20},{6,22},{8,24},{10,26},{12,28},{14,30},{16,0},... | collective-permute-start | bytes 221192 | tf_op jit(solution)/shard_map/ppermute | solution.py:50
  21.1 2.7 %collective-permute-done.5 = f32[144,128]{1,0:T(8,128)S(1)} collective-permute-done((f32[144,128]{1,0:T(8,128)S(1)}, f32[144,128]{1,0:T(8,128)S(1)}, u32[]{:S(2)}, u32[]{:S(2)}) %collective-permute-start.5) | collective-permute-done | bytes 73760 | tf_op jit(solution)/shard_map/ppermute | solution.py:50
  23.8 1.6 %collective-permute-start.6 = (f32[144,128]{1,0:T(8,128)S(1)}, f32[144,128]{1,0:T(8,128)S(1)}, u32[]{:S(2)}, u32[]{:S(2)}) collective-permute-start(f32[144,128]{1,0:T(8,128)S(1)} %get-tuple-element.23), channel_id=1, source_target_pairs={{0,4},{2,6},{4,0},{6,2},{8,12},{10,14},{12,8},{14,10},{16,20},{18,... | collective-permute-start | bytes 221192 | tf_op jit(solution)/shard_map/ppermute | solution.py:50
  25.4 1.3 %collective-permute-start.7 = (f32[144,128]{1,0:T(8,128)S(1)}, f32[144,128]{1,0:T(8,128)S(1)}, u32[]{:S(2)}, u32[]{:S(2)}) collective-permute-start(f32[144,128]{1,0:T(8,128)S(1)} %get-tuple-element.23), channel_id=1, source_target_pairs={{0,8},{2,10},{4,12},{6,14},{8,0},{10,2},{12,4},{14,6},{16,24},{18,... | collective-permute-start | bytes 221192 | tf_op jit(solution)/shard_map/ppermute | solution.py:50
  26.8 0.6 collective-permute-start.8
  27.4 1.7 %collective-permute-done.6 = f32[144,128]{1,0:T(8,128)S(1)} collective-permute-done((f32[144,128]{1,0:T(8,128)S(1)}, f32[144,128]{1,0:T(8,128)S(1)}, u32[]{:S(2)}, u32[]{:S(2)}) %collective-permute-start.6) | collective-permute-done | bytes 73760 | tf_op jit(solution)/shard_map/ppermute | solution.py:50
  29.0 0.7 collective-permute-done.7
  29.8 2.2 %collective-permute-done.8 = f32[144,128]{1,0:T(8,128)S(1)} collective-permute-done((f32[144,128]{1,0:T(8,128)S(1)}, f32[144,128]{1,0:T(8,128)S(1)}, u32[]{:S(2)}, u32[]{:S(2)}) %collective-permute-start.8) | collective-permute-done | bytes 73760 | tf_op jit(solution)/shard_map/ppermute | solution.py:50
  32.0 0.1 collective-permute-start.9
  32.2 1.5 %collective-permute-done.9 = f32[576,128]{1,0:T(8,128)S(1)} collective-permute-done((f32[576,128]{1,0:T(8,128)S(1)}, f32[576,128]{1,0:T(8,128)S(1)}, u32[]{:S(2)}, u32[]{:S(2)}) %collective-permute-start.9) | collective-permute-done | bytes 294944 | tf_op jit(solution)/shard_map/ppermute | solution.py:50
  33.7 0.4 weigh.1.refs_0_
  34.1 1.6 %collective-permute-start.10 = (f32[128,128]{1,0:T(8,128)S(1)}, f32[128,128]{1,0:T(8,128)S(1)}, u32[]{:S(2)}, u32[]{:S(2)}) collective-permute-start(f32[128,128]{1,0:T(8,128)S(1)} %weigh.1.refs_0_), channel_id=1, source_target_pairs={{0,1},{1,0},{2,3},{3,2},{4,5},{5,4},{6,7},{7,6},{8,9},{9,8},{10,11... | collective-permute-start | bytes 196616 | tf_op jit(solution)/shard_map/ppermute | solution.py:50
  35.7 2.8 %collective-permute-done.10.refs_1_ = f32[128,128]{1,0:T(8,128)S(1)} collective-permute-done((f32[128,128]{1,0:T(8,128)S(1)}, f32[128,128]{1,0:T(8,128)S(1)}, u32[]{:S(2)}, u32[]{:S(2)}) %collective-permute-start.10) | collective-permute-done | bytes 65568 | tf_op jit(solution)/shard_map/ppermute | solution.py:50
  38.5 0.4 apply.3
  38.9 0.1 collective-permute-start.11
  39.0 1.1 %fusion = f32[128,128]{1,0:T(8,128)S(1)} fusion(f32[1152,128]{1,0:T(8,128)S(1)} %constant_dynamic-update-slice_fusion.6.left_ref.refs_0_), kind=kOutput, calls=%fused_computation.25 | convolution fusion | flops 226492416 | bytes 655360 | tf_op jit(solution)/shard_map/dot_general | solution.py:358
  40.1 1.6 %collective-permute-start.12 = (f32[128,128]{1,0:T(8,128)S(1)}, f32[128,128]{1,0:T(8,128)S(1)}, u32[]{:S(2)}, u32[]{:S(2)}) collective-permute-start(f32[128,128]{1,0:T(8,128)S(1)} %fusion), channel_id=1, source_target_pairs={{0,1},{1,0},{2,3},{3,2},{4,5},{5,4},{6,7},{7,6},{8,9},{9,8},{10,11... | collective-permute-start | bytes 196616 | tf_op jit(solution)/shard_map/ppermute | solution.py:50
  41.6 0.0 collective-permute-done.11
  41.7 2.9 %collective-permute-done.12 = f32[128,128]{1,0:T(8,128)S(1)} collective-permute-done((f32[128,128]{1,0:T(8,128)S(1)}, f32[128,128]{1,0:T(8,128)S(1)}, u32[]{:S(2)}, u32[]{:S(2)}) %collective-permute-start.12) | collective-permute-done | bytes 65568 | tf_op jit(solution)/shard_map/ppermute | solution.py:50
  44.6 0.6 collective-permute-start.14
  45.3 1.6 %collective-permute-start.16 = (f32[128,128]{1,0:T(8,128)S(1)}, f32[128,128]{1,0:T(8,128)S(1)}, u32[]{:S(2)}, u32[]{:S(2)}) collective-permute-start(f32[128,128]{1,0:T(8,128)S(1)} %get-tuple-element.28), channel_id=1, source_target_pairs={{0,12},{2,14},{4,8},{6,10},{8,4},{10,6},{12,0},{14,2},{16,28},{18,... | collective-permute-start | bytes 196616 | tf_op jit(solution)/shard_map/ppermute | solution.py:50
  46.8 1.3 %collective-permute-start.15 = (f32[128,128]{1,0:T(8,128)S(1)}, f32[128,128]{1,0:T(8,128)S(1)}, u32[]{:S(2)}, u32[]{:S(2)}) collective-permute-start(f32[128,128]{1,0:T(8,128)S(1)} %get-tuple-element.29), channel_id=1, source_target_pairs={{0,8},{2,10},{4,12},{6,14},{8,0},{10,2},{12,4},{14,6},{16,24},{18,... | collective-permute-start | bytes 196616 | tf_op jit(solution)/shard_map/ppermute | solution.py:50
  48.2 0.1 pad_add_fusion.place_ref
  48.3 1.5 %collective-permute-start.13 = (f32[1152,128]{1,0:T(8,128)S(1)}, f32[1152,128]{1,0:T(8,128)S(1)}, u32[]{:S(2)}, u32[]{:S(2)}) collective-permute-start(f32[1152,128]{1,0:T(8,128)S(1)} %constant_dynamic-update-slice_fusion.6.left_ref.refs_0_), channel_id=1, source_target_pairs={{0,1},{1,0},{2,3},{3,2},{4,5},{5,4},{6,7},{7,6},{8,9},{9,8},{10,11... | collective-permute-start | bytes 1769480 | tf_op jit(solution)/shard_map/ppermute | solution.py:50
  49.8 0.0 collective-permute-done.14
  49.8 0.7 collective-permute-done.16
  50.4 0.7 collective-permute-done.15
  51.1 3.3 %collective-permute-start.17 = (f32[128,128]{1,0:T(8,128)S(1)}, f32[128,128]{1,0:T(8,128)S(1)}, u32[]{:S(2)}, u32[]{:S(2)}) collective-permute-start(f32[128,128]{1,0:T(8,128)S(1)} %add_add_fusion.1), channel_id=1, source_target_pairs={{0,16},{2,18},{4,20},{6,22},{8,24},{10,26},{12,28},{14,30},{16,0},... | collective-permute-start | bytes 196616 | tf_op jit(solution)/shard_map/ppermute | solution.py:50
  54.5 2.6 %shard_map.50.state_ref = f32[128,128]{1,0:T(8,128)S(1)} custom-call(f32[128,128]{1,0:T(8,128)S(1)} %add.112.state_ref), custom_call_target="tpu_custom_call" | custom-call | flops 3000000000 | bytes 131072 | tf_op jit(solution)/shard_map/pallas_call | solution.py:170
  57.1 0.0 collective-permute-done.17
  57.2 0.8 %collective-permute-start.18 = (f32[128,128]{1,0:T(8,128)S(1)}, f32[128,128]{1,0:T(8,128)S(1)}, u32[]{:S(2)}, u32[]{:S(2)}) collective-permute-start(f32[128,128]{1,0:T(8,128)S(1)} %get-tuple-element.21), channel_id=1, source_target_pairs={{0,4},{2,6},{4,0},{6,2},{8,12},{10,14},{12,8},{14,10},{16,20},{18,... | collective-permute-start | bytes 196616 | tf_op jit(solution)/shard_map/ppermute | solution.py:50
  58.0 2.2 %shard_map.51.inverse_ref = f32[128,128]{1,0:T(8,128)S(1)} custom-call(f32[128,128]{1,0:T(8,128)S(1)} %shard_map.50.state_ref), custom_call_target="tpu_custom_call" | custom-call | flops 3000000000 | bytes 131072 | tf_op jit(solution)/shard_map/pallas_call | solution.py:170
  60.2 0.0 copy-start.1
  60.2 1.3 %collective-permute-start.19 = (f32[128,128]{1,0:T(8,128)S(1)}, f32[128,128]{1,0:T(8,128)S(1)}, u32[]{:S(2)}, u32[]{:S(2)}) collective-permute-start(f32[128,128]{1,0:T(8,128)S(1)} %get-tuple-element.21), channel_id=1, source_target_pairs={{0,8},{2,10},{4,12},{6,14},{8,0},{10,2},{12,4},{14,6},{16,24},{18,... | collective-permute-start | bytes 196616 | tf_op jit(solution)/shard_map/ppermute | solution.py:50
  61.5 1.5 %collective-permute-start.20 = (f32[128,128]{1,0:T(8,128)S(1)}, f32[128,128]{1,0:T(8,128)S(1)}, u32[]{:S(2)}, u32[]{:S(2)}) collective-permute-start(f32[128,128]{1,0:T(8,128)S(1)} %get-tuple-element.21), channel_id=1, source_target_pairs={{0,12},{2,14},{4,8},{6,10},{8,4},{10,6},{12,0},{14,2},{16,28},{18,... | collective-permute-start | bytes 196616 | tf_op jit(solution)/shard_map/ppermute | solution.py:50
  63.0 0.0 collective-permute-done.18
  63.0 1.5 %collective-permute-done.19 = f32[128,128]{1,0:T(8,128)S(1)} collective-permute-done((f32[128,128]{1,0:T(8,128)S(1)}, f32[128,128]{1,0:T(8,128)S(1)}, u32[]{:S(2)}, u32[]{:S(2)}) %collective-permute-start.19) | collective-permute-done | bytes 65568 | tf_op jit(solution)/shard_map/ppermute | solution.py:50
  64.5 2.1 %collective-permute-done.20 = f32[128,128]{1,0:T(8,128)S(1)} collective-permute-done((f32[128,128]{1,0:T(8,128)S(1)}, f32[128,128]{1,0:T(8,128)S(1)}, u32[]{:S(2)}, u32[]{:S(2)}) %collective-permute-start.20) | collective-permute-done | bytes 65568 | tf_op jit(solution)/shard_map/ppermute | solution.py:50
  66.7 0.1 collective-permute-start.21
  66.8 0.0 collective-permute-done.13.refs_1_
  66.8 1.9 %basis.1.mine_ref.tall_ref = bf16[2304,512]{1,0:T(8,128)(2,1)S(1)} custom-call(s32[2]{0:T(128)S(1)} %pad_add_fusion.place_ref, f32[128,128]{1,0:T(8,128)S(1)} %shard_map.51.inverse_ref, bf16[2304,128]{1,0:T(8,128)(2,1)S(1)} %bitcast.9, f32[1152,128]{1,0:T(8,128)S(1)} %constant_dynamic-update-slice_fusion.6.left_ref.refs_0_, ...), custom_call_target="tpu_custom_call" | custom-call | flops 2000000000 | bytes 131072 | tf_op jit(solution)/shard_map/basis/pallas_call | solution.py:278
  68.7 0.0 collective-permute-done.21
  68.8 0.0 copy-done.1
  68.8 5.8 %finish.1 = (f32[144,1024]{1,0:T(8,128)}, bf16[2304,1024]{1,0:T(8,128)(2,1)}) custom-call(s32[1]{0:T(128)} %bitcast.place_ref, bf16[2304,512]{1,0:T(8,128)(2,1)S(1)} %basis.1.mine_ref.tall_ref, bf16[2304,512]{1,0:T(8,128)(2,1)S(1)} %basis.1.mine_ref.tall_ref, bf16[128,1024]{1,0:T(8,128)(2,1)S(1)} %copy-done.1, ...), custom_call_target="tpu_custom_call" | custom-call | tf_op jit(solution)/shard_map/finish/pallas_call | solution.py:316
  (25 shorter events, 0.5 us)
Async XLA Ops:
  0.6 1.0 %copy-start = (bf16[128,1024]{1,0:T(8,128)(2,1)S(1)}, bf16[128,1024]{1,0:T(8,128)(2,1)}, u32[]{:S(2)}) copy-start(bf16[128,1024]{1,0:T(8,128)(2,1)} %grads_ref.3) | copy-start | bytes 786436
  1.6 1.0 %copy-start.2 = (f32[1024,128]{1,0:T(8,128)S(1)}, f32[1024,128]{1,0:T(8,128)}, u32[]{:S(2)}) copy-start(f32[1024,128]{1,0:T(8,128)} %right_ref.1) | copy-start | bytes 1572868
  3.0 5.6 %collective-permute-start = (f32[128,128]{1,0:T(8,128)S(1)}, f32[128,128]{1,0:T(8,128)S(1)}, u32[]{:S(2)}, u32[]{:S(2)}) collective-permute-start(f32[128,128]{1,0:T(8,128)S(1)} %project.1.refs_0_), channel_id=1, source_target_pairs={{0,1},{1,0},{2,3},{3,2},{4,5},{5,4},{6,7},{7,6},{8,9},{9,8},{10,11... | collective-permute-start | bytes 196616 | tf_op jit(solution)/shard_map/ppermute | solution.py:50
  9.0 1.6 %collective-permute-start.1 = (f32[576,128]{1,0:T(8,128)S(1)}, f32[576,128]{1,0:T(8,128)S(1)}, u32[]{:S(2)}, u32[]{:S(2)}) collective-permute-start(f32[576,128]{1,0:T(8,128)S(1)} %constant_dynamic-slice_fusion.7), channel_id=1, source_target_pairs={{0,2},{2,0},{4,6},{6,4},{8,10},{10,8},{12,14},{14,12},{16,18},{18,... | collective-permute-start | bytes 884744 | tf_op jit(solution)/shard_map/ppermute | solution.py:50
  10.7 5.2 %collective-permute-start.2 = (f32[144,128]{1,0:T(8,128)S(1)}, f32[144,128]{1,0:T(8,128)S(1)}, u32[]{:S(2)}, u32[]{:S(2)}) collective-permute-start(f32[144,128]{1,0:T(8,128)S(1)} %get-tuple-element.24), channel_id=1, source_target_pairs={{0,4},{2,6},{4,0},{6,2},{8,12},{10,14},{12,8},{14,10},{16,20},{18,... | collective-permute-start | bytes 221192 | tf_op jit(solution)/shard_map/ppermute | solution.py:50
  12.5 5.9 %collective-permute-start.4 = (f32[144,128]{1,0:T(8,128)S(1)}, f32[144,128]{1,0:T(8,128)S(1)}, u32[]{:S(2)}, u32[]{:S(2)}) collective-permute-start(f32[144,128]{1,0:T(8,128)S(1)} %get-tuple-element.25), channel_id=1, source_target_pairs={{0,12},{2,14},{4,8},{6,10},{8,4},{10,6},{12,0},{14,2},{16,28},{18,... | collective-permute-start | bytes 221192 | tf_op jit(solution)/shard_map/ppermute | solution.py:50
  14.1 4.4 %collective-permute-start.3 = (f32[144,128]{1,0:T(8,128)S(1)}, f32[144,128]{1,0:T(8,128)S(1)}, u32[]{:S(2)}, u32[]{:S(2)}) collective-permute-start(f32[144,128]{1,0:T(8,128)S(1)} %get-tuple-element.26), channel_id=1, source_target_pairs={{0,8},{2,10},{4,12},{6,14},{8,0},{10,2},{12,4},{14,6},{16,24},{18,... | collective-permute-start | bytes 221192 | tf_op jit(solution)/shard_map/ppermute | solution.py:50
  18.4 5.3 %collective-permute-start.5 = (f32[144,128]{1,0:T(8,128)S(1)}, f32[144,128]{1,0:T(8,128)S(1)}, u32[]{:S(2)}, u32[]{:S(2)}) collective-permute-start(f32[144,128]{1,0:T(8,128)S(1)} %add_add_fusion), channel_id=1, source_target_pairs={{0,16},{2,18},{4,20},{6,22},{8,24},{10,26},{12,28},{14,30},{16,0},... | collective-permute-start | bytes 221192 | tf_op jit(solution)/shard_map/ppermute | solution.py:50
  23.8 5.2 %collective-permute-start.6 = (f32[144,128]{1,0:T(8,128)S(1)}, f32[144,128]{1,0:T(8,128)S(1)}, u32[]{:S(2)}, u32[]{:S(2)}) collective-permute-start(f32[144,128]{1,0:T(8,128)S(1)} %get-tuple-element.23), channel_id=1, source_target_pairs={{0,4},{2,6},{4,0},{6,2},{8,12},{10,14},{12,8},{14,10},{16,20},{18,... | collective-permute-start | bytes 221192 | tf_op jit(solution)/shard_map/ppermute | solution.py:50
  25.4 4.4 %collective-permute-start.7 = (f32[144,128]{1,0:T(8,128)S(1)}, f32[144,128]{1,0:T(8,128)S(1)}, u32[]{:S(2)}, u32[]{:S(2)}) collective-permute-start(f32[144,128]{1,0:T(8,128)S(1)} %get-tuple-element.23), channel_id=1, source_target_pairs={{0,8},{2,10},{4,12},{6,14},{8,0},{10,2},{12,4},{14,6},{16,24},{18,... | collective-permute-start | bytes 221192 | tf_op jit(solution)/shard_map/ppermute | solution.py:50
  26.8 5.3 %collective-permute-start.8 = (f32[144,128]{1,0:T(8,128)S(1)}, f32[144,128]{1,0:T(8,128)S(1)}, u32[]{:S(2)}, u32[]{:S(2)}) collective-permute-start(f32[144,128]{1,0:T(8,128)S(1)} %get-tuple-element.23), channel_id=1, source_target_pairs={{0,12},{2,14},{4,8},{6,10},{8,4},{10,6},{12,0},{14,2},{16,28},{18,... | collective-permute-start | bytes 221192 | tf_op jit(solution)/shard_map/ppermute | solution.py:50
  32.0 1.6 %collective-permute-start.9 = (f32[576,128]{1,0:T(8,128)S(1)}, f32[576,128]{1,0:T(8,128)S(1)}, u32[]{:S(2)}, u32[]{:S(2)}) collective-permute-start(f32[576,128]{1,0:T(8,128)S(1)} %constant_dynamic-update-slice_fusion.8), channel_id=1, source_target_pairs={{0,2},{2,0},{4,6},{6,4},{8,10},{10,8},{12,14},{14,12},{16,18},{18,... | collective-permute-start | bytes 884744 | tf_op jit(solution)/shard_map/ppermute | solution.py:50
  34.1 4.3 %collective-permute-start.10 = (f32[128,128]{1,0:T(8,128)S(1)}, f32[128,128]{1,0:T(8,128)S(1)}, u32[]{:S(2)}, u32[]{:S(2)}) collective-permute-start(f32[128,128]{1,0:T(8,128)S(1)} %weigh.1.refs_0_), channel_id=1, source_target_pairs={{0,1},{1,0},{2,3},{3,2},{4,5},{5,4},{6,7},{7,6},{8,9},{9,8},{10,11... | collective-permute-start | bytes 196616 | tf_op jit(solution)/shard_map/ppermute | solution.py:50
  38.9 2.8 %collective-permute-start.11 = (f32[512,128]{1,0:T(8,128)S(1)}, f32[512,128]{1,0:T(8,128)S(1)}, u32[]{:S(2)}, u32[]{:S(2)}) collective-permute-start(f32[512,128]{1,0:T(8,128)S(1)} %constant_dynamic-slice_fusion.3), channel_id=1, source_target_pairs={{0,2},{2,0},{4,6},{6,4},{8,10},{10,8},{12,14},{14,12},{16,18},{18,... | collective-permute-start | bytes 786440 | tf_op jit(solution)/shard_map/ppermute | solution.py:50
  40.1 4.5 %collective-permute-start.12 = (f32[128,128]{1,0:T(8,128)S(1)}, f32[128,128]{1,0:T(8,128)S(1)}, u32[]{:S(2)}, u32[]{:S(2)}) collective-permute-start(f32[128,128]{1,0:T(8,128)S(1)} %fusion), channel_id=1, source_target_pairs={{0,1},{1,0},{2,3},{3,2},{4,5},{5,4},{6,7},{7,6},{8,9},{9,8},{10,11... | collective-permute-start | bytes 196616 | tf_op jit(solution)/shard_map/ppermute | solution.py:50
  44.6 5.1 %collective-permute-start.14 = (f32[128,128]{1,0:T(8,128)S(1)}, f32[128,128]{1,0:T(8,128)S(1)}, u32[]{:S(2)}, u32[]{:S(2)}) collective-permute-start(f32[128,128]{1,0:T(8,128)S(1)} %get-tuple-element.27), channel_id=1, source_target_pairs={{0,4},{2,6},{4,0},{6,2},{8,12},{10,14},{12,8},{14,10},{16,20},{18,... | collective-permute-start | bytes 196616 | tf_op jit(solution)/shard_map/ppermute | solution.py:50
  45.3 5.2 %collective-permute-start.16 = (f32[128,128]{1,0:T(8,128)S(1)}, f32[128,128]{1,0:T(8,128)S(1)}, u32[]{:S(2)}, u32[]{:S(2)}) collective-permute-start(f32[128,128]{1,0:T(8,128)S(1)} %get-tuple-element.28), channel_id=1, source_target_pairs={{0,12},{2,14},{4,8},{6,10},{8,4},{10,6},{12,0},{14,2},{16,28},{18,... | collective-permute-start | bytes 196616 | tf_op jit(solution)/shard_map/ppermute | solution.py:50
  46.8 4.3 %collective-permute-start.15 = (f32[128,128]{1,0:T(8,128)S(1)}, f32[128,128]{1,0:T(8,128)S(1)}, u32[]{:S(2)}, u32[]{:S(2)}) collective-permute-start(f32[128,128]{1,0:T(8,128)S(1)} %get-tuple-element.29), channel_id=1, source_target_pairs={{0,8},{2,10},{4,12},{6,14},{8,0},{10,2},{12,4},{14,6},{16,24},{18,... | collective-permute-start | bytes 196616 | tf_op jit(solution)/shard_map/ppermute | solution.py:50
  48.3 18.6 %collective-permute-start.13 = (f32[1152,128]{1,0:T(8,128)S(1)}, f32[1152,128]{1,0:T(8,128)S(1)}, u32[]{:S(2)}, u32[]{:S(2)}) collective-permute-start(f32[1152,128]{1,0:T(8,128)S(1)} %constant_dynamic-update-slice_fusion.6.left_ref.refs_0_), channel_id=1, source_target_pairs={{0,1},{1,0},{2,3},{3,2},{4,5},{5,4},{6,7},{7,6},{8,9},{9,8},{10,11... | collective-permute-start | bytes 1769480 | tf_op jit(solution)/shard_map/ppermute | solution.py:50
  51.1 6.0 %collective-permute-start.17 = (f32[128,128]{1,0:T(8,128)S(1)}, f32[128,128]{1,0:T(8,128)S(1)}, u32[]{:S(2)}, u32[]{:S(2)}) collective-permute-start(f32[128,128]{1,0:T(8,128)S(1)} %add_add_fusion.1), channel_id=1, source_target_pairs={{0,16},{2,18},{4,20},{6,22},{8,24},{10,26},{12,28},{14,30},{16,0},... | collective-permute-start | bytes 196616 | tf_op jit(solution)/shard_map/ppermute | solution.py:50
  57.2 5.8 %collective-permute-start.18 = (f32[128,128]{1,0:T(8,128)S(1)}, f32[128,128]{1,0:T(8,128)S(1)}, u32[]{:S(2)}, u32[]{:S(2)}) collective-permute-start(f32[128,128]{1,0:T(8,128)S(1)} %get-tuple-element.21), channel_id=1, source_target_pairs={{0,4},{2,6},{4,0},{6,2},{8,12},{10,14},{12,8},{14,10},{16,20},{18,... | collective-permute-start | bytes 196616 | tf_op jit(solution)/shard_map/ppermute | solution.py:50
  60.2 8.6 %copy-start.1 = (bf16[128,1024]{1,0:T(8,128)(2,1)S(1)}, bf16[128,1024]{1,0:T(8,128)(2,1)}, u32[]{:S(2)}) copy-start(bf16[128,1024]{1,0:T(8,128)(2,1)} %grads_ref.3) | copy-start | bytes 786436
  60.2 4.3 %collective-permute-start.19 = (f32[128,128]{1,0:T(8,128)S(1)}, f32[128,128]{1,0:T(8,128)S(1)}, u32[]{:S(2)}, u32[]{:S(2)}) collective-permute-start(f32[128,128]{1,0:T(8,128)S(1)} %get-tuple-element.21), channel_id=1, source_target_pairs={{0,8},{2,10},{4,12},{6,14},{8,0},{10,2},{12,4},{14,6},{16,24},{18,... | collective-permute-start | bytes 196616 | tf_op jit(solution)/shard_map/ppermute | solution.py:50
  61.5 5.2 %collective-permute-start.20 = (f32[128,128]{1,0:T(8,128)S(1)}, f32[128,128]{1,0:T(8,128)S(1)}, u32[]{:S(2)}, u32[]{:S(2)}) collective-permute-start(f32[128,128]{1,0:T(8,128)S(1)} %get-tuple-element.21), channel_id=1, source_target_pairs={{0,12},{2,14},{4,8},{6,10},{8,4},{10,6},{12,0},{14,2},{16,28},{18,... | collective-permute-start | bytes 196616 | tf_op jit(solution)/shard_map/ppermute | solution.py:50
  66.7 2.1 %collective-permute-start.21 = (f32[512,128]{1,0:T(8,128)S(1)}, f32[512,128]{1,0:T(8,128)S(1)}, u32[]{:S(2)}, u32[]{:S(2)}) collective-permute-start(f32[512,128]{1,0:T(8,128)S(1)} %constant_dynamic-update-slice_fusion.2), channel_id=1, source_target_pairs={{0,2},{2,0},{4,6},{6,4},{8,10},{10,8},{12,14},{14,12},{16,18},{18,... | collective-permute-start | bytes 786440 | tf_op jit(solution)/shard_map/ppermute | solution.py:50

commit v3 on v2

--- a/solution.py
+++ b/solution.py
@@ -66,10 +66,14 @@
             value, tied = lax.optimization_barrier((value, tied))
     radix, stride = stages[-1]
     received = [shifted(value, axis, radix, stride, step) for step in range(1, radix)]
-    digit = position // stride % radix
+    return [value] + received, tied
+
+
+def together(values, axis):
+    radix, stride = stages_of(axis)[-1]
     if radix == 2:
-        return value + received[0], tied
-    return ordered_sum([value] + received, digit), tied
+        return values[0] + values[1]
+    return ordered_sum(values, lax.axis_index(axis) // stride % radix)
 
 
 def ordered_sum(values, digit):
@@ -209,19 +213,32 @@
     return lax.dot_general(left, right, dims, precision=HI, preferred_element_type=jnp.float32)
 
 
-def project_body(grads_ref, right_ref, out_ref):
-    out_ref[...] = exact_dot(grads_ref[...], right_ref[...], (1, 0))
+def project_body(grads_ref, right_ref, out_ref, grads, right, arrived):
+    copies = [
+        pltpu.make_async_copy(grads_ref, grads, arrived.at[0]),
+        pltpu.make_async_copy(right_ref, right, arrived.at[1]),
+    ]
+    for copy in copies:
+        copy.start()
+    for copy in copies:
+        copy.wait()
+    out_ref[...] = exact_dot(grads[...], right[...], (1, 0))
 
 
 def project(out_grads, right_prev):
     return pl.pallas_call(
         project_body,
         out_shape=jax.ShapeDtypeStruct((out_grads.shape[0], right_prev.shape[1]), jnp.float32),
-        in_specs=vmem(2),
+        in_specs=[pl.BlockSpec(memory_space=pltpu.HBM)] * 2,
         out_specs=vmem(1)[0],
-        compiler_params=grant(4),
+        scratch_shapes=[
+            pltpu.VMEM(out_grads.shape, out_grads.dtype),
+            pltpu.VMEM(right_prev.shape, right_prev.dtype),
+            pltpu.SemaphoreType.DMA((2,)),
+        ],
+        compiler_params=grant(6),
         name="project",
-    )(out_grads, right_prev)
+    )(*(pltpu.with_memory_space_constraint(array, pltpu.HBM) for array in (out_grads, right_prev)))
 
 
 def apply_body(place_ref, tall_ref, *refs):
@@ -286,47 +303,86 @@
     )(places, inverse, acts, *parts)
 
 
-def finish_body(replicas, place_ref, mine_ref, tall_ref, grads_ref, sum_ref, inverse_ref, update_ref, residual_ref, wide):
-    step, tile = pl.program_id(0), residual_ref.shape[0]
+def blocks_fit(columns, axis):
+    blocks = blocks_of(axis)
+    return columns % blocks == 0 and columns // blocks % 128 == 0
+
+
+def turn_body(replicas, inverse_ref, *refs):
+    total = refs[0][...]
+    for ref in refs[1:-1]:
+        total = total + ref[...]
+    right = nt_dot(total, inverse_ref[...]) * (1.0 / replicas)
+    refs[-1][...] = jnp.transpose(right)
+
+
+def turn(replicas, inverse, parts):
+    rows, rank = parts[0].shape
+    return pl.pallas_call(
+        functools.partial(turn_body, replicas),
+        out_shape=jax.ShapeDtypeStruct((rank, rows), jnp.float32),
+        in_specs=vmem(1 + len(parts)),
+        out_specs=vmem(1)[0],
+        compiler_params=grant(2),
+        name="turn",
+    )(inverse, *parts)
+
+
+def finish_body(replicas, turned, place_ref, mine_ref, tall_ref, grads_ref, sum_ref, inverse_ref, update_ref, residual_ref,
+                wide, tiles, update, sent):
     tokens, rank = grads_ref.shape[0], inverse_ref.shape[0]
-
-    @pl.when(step == 0)
-    def _():
-        right = nt_dot(inverse_ref[...], sum_ref[...]) * (1.0 / replicas)
-        top, low = terms_in_kernel(right, 2)
-        wide[:tokens, :] = grads_ref[...]
+    count, tile = tiles.shape[:2]
+    wide[:tokens, :] = grads_ref[...]
+    width = sum_ref.shape[1] if turned else wide.shape[1]
+    for start in range(0, wide.shape[1], width):
+        if turned:
+            first = start // width * rank
+            top, low = terms_in_kernel(sum_ref[first : first + rank, :], 2)
+        else:
+            right = nt_dot(sum_ref[...], inverse_ref[...]) * (1.0 / replicas)
+            top, low = (jnp.transpose(term) for term in terms_in_kernel(right, 2))
         for index, term in enumerate((top, top, low)):
-            wide[tokens + index * rank : tokens + (index + 1) * rank, :] = term
-        my_rows = update_ref.shape[0]
-        mine = pl.ds(pl.multiple_of(place_ref[0] * my_rows, 16), my_rows)
-        left = mine_ref[mine, tokens:] if my_rows % 16 == 0 else mine_ref[:, tokens:]
-        update_ref[...] = -jnp.dot(left, wide[tokens:, :], preferred_element_type=jnp.float32)
-
-    rows = pl.ds(pl.multiple_of(step * tile, tile), tile)
-    residual = jnp.dot(tall_ref[rows, :], wide[...], preferred_element_type=jnp.float32)
-    residual_ref[...] = residual.astype(jnp.bfloat16)
-
-
-def finish(replicas, place, tall, out_grads, right_sum, inverse):
+            wide[tokens + index * rank : tokens + (index + 1) * rank, start : start + width] = term
+    copies = []
+    for index in range(count):
+        rows = pl.ds(index * tile, tile)
+        residual = jnp.dot(tall_ref[rows, :], wide[...], preferred_element_type=jnp.float32)
+        tiles[index] = residual.astype(jnp.bfloat16)
+        copies.append(pltpu.make_async_copy(tiles.at[index], residual_ref.at[rows, :], sent.at[index]))
+        copies[-1].start()
+        if index == 0:
+            my_rows = update_ref.shape[0]
+            mine = pl.ds(pl.multiple_of(place_ref[0] * my_rows, 16), my_rows)
+            left = mine_ref[mine, tokens:] if my_rows % 16 == 0 else mine_ref[:, tokens:]
+            update[...] = -jnp.dot(left, wide[tokens:, :], preferred_element_type=jnp.float32)
+            copies.append(pltpu.make_async_copy(update, update_ref, sent.at[count]))
+            copies[-1].start()
+    for copy in copies:
+        copy.wait()
+
+
+def finish(replicas, turned, place, tall, out_grads, right_sum, inverse):
     rows, columns = tall.shape[0], out_grads.shape[1]
     my_rows, mine = rows // replicas, tall
     if my_rows % 16 != 0:
         mine = lax.dynamic_slice_in_dim(tall, place[0] * my_rows, my_rows, 0)
-    tile = next(size for size in (384, 256, 192, 128, 96, 64, 32, 16, 8) if rows % size == 0)
-    return pl.pallas_call(
-        functools.partial(finish_body, replicas),
-        grid=(rows // tile,),
+    tile = next(size for size in (256, 192, 128, 96, 64, 32, 16) if rows % size == 0)
+    hbm = pl.BlockSpec(memory_space=pltpu.HBM)
+    return pl.pallas_call(
+        functools.partial(finish_body, replicas, turned),
         out_shape=(
             jax.ShapeDtypeStruct((my_rows, columns), jnp.float32),
             jax.ShapeDtypeStruct((rows, columns), jnp.bfloat16),
         ),
         in_specs=[SMEM] + vmem(5),
-        out_specs=(
-            pl.BlockSpec((my_rows, columns), lambda i: (0, 0)),
-            pl.BlockSpec((tile, columns), lambda i: (i, 0)),
-        ),
-        scratch_shapes=[pltpu.VMEM((tall.shape[1], columns), jnp.bfloat16)],
-        compiler_params=grant(12, dimension_semantics=("arbitrary",)),
+        out_specs=(hbm, hbm),
+        scratch_shapes=[
+            pltpu.VMEM((tall.shape[1], columns), jnp.bfloat16),
+            pltpu.VMEM((rows // tile, tile, columns), jnp.bfloat16),
+            pltpu.VMEM((my_rows, columns), jnp.float32),
+            pltpu.SemaphoreType.DMA((rows // tile + 1,)),
+        ],
+        compiler_params=grant(20),
         name="finish",
     )(place, mine, tall, out_grads, right_sum, inverse)
 
@@ -350,8 +406,8 @@
 
     projected, _ = sent_all(project(out_grads, right_prev), "tp")
     left_part = padded_rows(apply(place, acts, my_rows, projected), blocks_of("dp"))
-    left_own, _ = scatter_sum(left_part, "dp")
-    left_own = gather_rows(left_own, "dp")[:my_rows]
+    left_parts, _ = scatter_sum(left_part, "dp")
+    left_own = gather_rows(together(left_parts, "dp"), "dp")[:my_rows]
 
     weighted_own, left_own = lax.optimization_barrier((weigh(place, acts, left_own), left_own))
     weighted, _ = sent_all(weighted_own, "tp")
@@ -360,15 +416,18 @@
     left_own, weighted[0] = lax.optimization_barrier((left_own, weighted[0]))
     right_part = apply(origin, grads, my_columns, weighted)
     right_part = padded_rows(right_part, blocks_of("dp"))
-    right_sum, grams = scatter_sum(right_part, "dp", tied=grams)
-    right_sum = gather_rows(right_sum, "dp")[:my_columns]
+    right_parts, grams = scatter_sum(right_part, "dp", tied=grams)
     gram = sum(grams[1:], grams[0])
 
     parts, places = sent_all(left_own, "tp")
     inverse = inverse_factor(gram)
+    turned = blocks_fit(my_columns, "dp") and len(right_parts) == 2
+    right_own = turn(replicas, inverse, right_parts) if turned else together(right_parts, "dp")
+    right_sum = gather_rows(right_own, "dp")
+    right_sum = right_sum if turned else right_sum[:my_columns]
     tall = basis(places, inverse, acts, parts)
     replica = lax.axis_index("dp").astype(jnp.int32).reshape(1)
-    return finish(replicas, replica, tall, out_grads, right_sum, inverse)
+    return finish(replicas, turned, replica, tall, out_grads, right_sum, inverse)
 
 
 def solution(mesh):

time: 74.9 us -> 69.3 us (0.925)
  waiting for transfers between devices: 25.1 us -> 23.1 us
  local copies, waits for them, and re-layouts: 4.84 us -> 2.87 us
  starting transfers between devices: 28.2 us -> 27.2 us
    ppermute x22, waiting for transfers between devices: 25.1 us -> 23.1 us  [shifted(): return lax.ppermute(value, axis, pairs)]
    unnamed x8 -> x4, local copies, waits for them, and re-layouts: 4.48 us -> 2.49 us
    pallas_call x1 -> x2, Pallas kernels: 5.83 us -> 4.05 us  [the longest x1 3.71 us: finish(): pl.pallas_call(functools.partial(finish_body, replicas, turned), out_shap...]
    pallas_call x1, Pallas kernels: 0.37 us -> 1.53 us  [project(): pl.pallas_call(project_body, out_shape=jax.ShapeDtypeStruct((out_grads.sh...]
    ppermute x22, starting transfers between devices: 28.2 us -> 27.2 us  [shifted(): return lax.ppermute(value, axis, pairs)]
  transfers between devices with their start and end apart: 22 -> 22, of which waited for: 14 -> 13; matrix products, arithmetic and copies ran while one was open for 5% -> 6% of each run, Pallas kernels for 9% -> 10%
where the time goes in v3:
time: 69.3 us; the launch traced here: 69 us
  starting transfers between devices  27.2 us (39%)
  waiting for transfers between devices  23.1 us (33%)
  Pallas kernels  13.4 us (19%)
  local copies, waits for them, and re-layouts  2.87 us (4%)
  matrix products  1.12 us (2%)
  between operations  1.03 us (1%)
    ppermute x22, starting transfers between devices, shifted(): return lax.ppermute(value, axis, pairs)  27.2 us
    ppermute x22, waiting for transfers between devices, shifted(): return lax.ppermute(value, axis, pairs)  23.1 us
    pallas_call x2, Pallas kernels, inverse_factor(): state = call(state)  4.79 us
    pallas_call x1, Pallas kernels, finish(): pl.pallas_call(functools.partial(finish_body, replicas, turned), out_shap...  3.71 us
    unnamed x4, local copies, waits for them, and re-layouts  2.49 us
    pallas_call x1, Pallas kernels, basis(): pl.pallas_call(basis_body, out_shape=jax.ShapeDtypeStruct((acts.shape[0],...  1.89 us
    pallas_call x1, Pallas kernels, project(): pl.pallas_call(project_body, out_shape=jax.ShapeDtypeStruct((out_grads.sh...  1.53 us
  transfers between devices with their start and end apart: 22, of which 13 were waited for; matrix products, arithmetic and copies ran while one was open for 6% of the time, Pallas kernels for 10%

profile of v3, /device:TPU:0, one launch (start us, length us, event | category | flops | bytes accessed | tf_op | source)
XLA Modules:
  0.0 69.0 jit_solution(7212283380716213140)
XLA Ops:
  0.6 1.5 %project.1.refs_0_ = f32[128,128]{1,0:T(8,128)S(1)} custom-call(bf16[128,1024]{1,0:T(8,128)(2,1)} %grads_ref.3, f32[1024,128]{1,0:T(8,128)} %right_ref.1), custom_call_target="tpu_custom_call" | custom-call | tf_op jit(solution)/shard_map/project/pallas_call | solution.py:229
  2.2 3.0 %collective-permute-start = (f32[128,128]{1,0:T(8,128)S(1)}, f32[128,128]{1,0:T(8,128)S(1)}, u32[]{:S(2)}, u32[]{:S(2)}) collective-permute-start(f32[128,128]{1,0:T(8,128)S(1)} %project.1.refs_0_), channel_id=1, source_target_pairs={{0,1},{1,0},{2,3},{3,2},{4,5},{5,4},{6,7},{7,6},{8,9},{9,8},{10,11... | collective-permute-start | bytes 196616 | tf_op jit(solution)/shard_map/ppermute | solution.py:50
  5.2 1.1 %copy.6 = bf16[128,1024]{0,1:T(8,128)(2,1)S(1)} copy(bf16[128,1024]{1,0:T(8,128)(2,1)} %grads_ref.3) | data formatting | bytes 524288 | tf_op args[1]
  6.3 1.4 %copy.5 = bf16[128,2304]{0,1:T(8,128)(2,1)S(1)} copy(bf16[128,2304]{1,0:T(8,128)(2,1)} %param.3) | data formatting | bytes 1179648 | tf_op args[0]
  7.7 0.0 collective-permute-done.refs_1_
  7.7 0.4 apply.2
  8.1 0.1 collective-permute-start.1
  8.3 1.5 %collective-permute-done.1 = f32[576,128]{1,0:T(8,128)S(1)} collective-permute-done((f32[576,128]{1,0:T(8,128)S(1)}, f32[576,128]{1,0:T(8,128)S(1)}, u32[]{:S(2)}, u32[]{:S(2)}) %collective-permute-start.1) | collective-permute-done | bytes 294944 | tf_op jit(solution)/shard_map/ppermute | solution.py:50
  9.9 1.8 %collective-permute-start.2 = (f32[144,128]{1,0:T(8,128)S(1)}, f32[144,128]{1,0:T(8,128)S(1)}, u32[]{:S(2)}, u32[]{:S(2)}) collective-permute-start(f32[144,128]{1,0:T(8,128)S(1)} %get-tuple-element.22), channel_id=1, source_target_pairs={{0,4},{2,6},{4,0},{6,2},{8,12},{10,14},{12,8},{14,10},{16,20},{18,... | collective-permute-start | bytes 221192 | tf_op jit(solution)/shard_map/ppermute | solution.py:50
  11.7 1.5 %collective-permute-start.4 = (f32[144,128]{1,0:T(8,128)S(1)}, f32[144,128]{1,0:T(8,128)S(1)}, u32[]{:S(2)}, u32[]{:S(2)}) collective-permute-start(f32[144,128]{1,0:T(8,128)S(1)} %get-tuple-element.23), channel_id=1, source_target_pairs={{0,12},{2,14},{4,8},{6,10},{8,4},{10,6},{12,0},{14,2},{16,28},{18,... | collective-permute-start | bytes 221192 | tf_op jit(solution)/shard_map/ppermute | solution.py:50
  13.2 0.2 collective-permute-start.3
  13.4 1.6 %collective-permute-done.2 = f32[144,128]{1,0:T(8,128)S(1)} collective-permute-done((f32[144,128]{1,0:T(8,128)S(1)}, f32[144,128]{1,0:T(8,128)S(1)}, u32[]{:S(2)}, u32[]{:S(2)}) %collective-permute-start.2) | collective-permute-done | bytes 73760 | tf_op jit(solution)/shard_map/ppermute | solution.py:50
  15.1 2.5 %collective-permute-done.4 = f32[144,128]{1,0:T(8,128)S(1)} collective-permute-done((f32[144,128]{1,0:T(8,128)S(1)}, f32[144,128]{1,0:T(8,128)S(1)}, u32[]{:S(2)}, u32[]{:S(2)}) %collective-permute-start.4) | collective-permute-done | bytes 73760 | tf_op jit(solution)/shard_map/ppermute | solution.py:50
  17.6 0.0 collective-permute-done.3
  17.6 2.7 %collective-permute-start.5 = (f32[144,128]{1,0:T(8,128)S(1)}, f32[144,128]{1,0:T(8,128)S(1)}, u32[]{:S(2)}, u32[]{:S(2)}) collective-permute-start(f32[144,128]{1,0:T(8,128)S(1)} %add_add_fusion), channel_id=1, source_target_pairs={{0,16},{2,18},{4,20},{6,22},{8,24},{10,26},{12,28},{14,30},{16,0},... | collective-permute-start | bytes 221192 | tf_op jit(solution)/shard_map/ppermute | solution.py:50
  20.3 2.7 %collective-permute-done.5 = f32[144,128]{1,0:T(8,128)S(1)} collective-permute-done((f32[144,128]{1,0:T(8,128)S(1)}, f32[144,128]{1,0:T(8,128)S(1)}, u32[]{:S(2)}, u32[]{:S(2)}) %collective-permute-start.5) | collective-permute-done | bytes 73760 | tf_op jit(solution)/shard_map/ppermute | solution.py:50
  23.0 1.6 %collective-permute-start.6 = (f32[144,128]{1,0:T(8,128)S(1)}, f32[144,128]{1,0:T(8,128)S(1)}, u32[]{:S(2)}, u32[]{:S(2)}) collective-permute-start(f32[144,128]{1,0:T(8,128)S(1)} %get-tuple-element.21), channel_id=1, source_target_pairs={{0,4},{2,6},{4,0},{6,2},{8,12},{10,14},{12,8},{14,10},{16,20},{18,... | collective-permute-start | bytes 221192 | tf_op jit(solution)/shard_map/ppermute | solution.py:50
  24.6 1.3 %collective-permute-start.7 = (f32[144,128]{1,0:T(8,128)S(1)}, f32[144,128]{1,0:T(8,128)S(1)}, u32[]{:S(2)}, u32[]{:S(2)}) collective-permute-start(f32[144,128]{1,0:T(8,128)S(1)} %get-tuple-element.21), channel_id=1, source_target_pairs={{0,8},{2,10},{4,12},{6,14},{8,0},{10,2},{12,4},{14,6},{16,24},{18,... | collective-permute-start | bytes 221192 | tf_op jit(solution)/shard_map/ppermute | solution.py:50
  25.9 0.6 collective-permute-start.8
  26.5 1.7 %collective-permute-done.6 = f32[144,128]{1,0:T(8,128)S(1)} collective-permute-done((f32[144,128]{1,0:T(8,128)S(1)}, f32[144,128]{1,0:T(8,128)S(1)}, u32[]{:S(2)}, u32[]{:S(2)}) %collective-permute-start.6) | collective-permute-done | bytes 73760 | tf_op jit(solution)/shard_map/ppermute | solution.py:50
  28.2 0.7 %collective-permute-done.7 = f32[144,128]{1,0:T(8,128)S(1)} collective-permute-done((f32[144,128]{1,0:T(8,128)S(1)}, f32[144,128]{1,0:T(8,128)S(1)}, u32[]{:S(2)}, u32[]{:S(2)}) %collective-permute-start.7) | collective-permute-done | bytes 73760 | tf_op jit(solution)/shard_map/ppermute | solution.py:50
  28.9 2.2 %collective-permute-done.8 = f32[144,128]{1,0:T(8,128)S(1)} collective-permute-done((f32[144,128]{1,0:T(8,128)S(1)}, f32[144,128]{1,0:T(8,128)S(1)}, u32[]{:S(2)}, u32[]{:S(2)}) %collective-permute-start.8) | collective-permute-done | bytes 73760 | tf_op jit(solution)/shard_map/ppermute | solution.py:50
  31.2 0.1 collective-permute-start.9
  31.3 1.5 %collective-permute-done.9 = f32[576,128]{1,0:T(8,128)S(1)} collective-permute-done((f32[576,128]{1,0:T(8,128)S(1)}, f32[576,128]{1,0:T(8,128)S(1)}, u32[]{:S(2)}, u32[]{:S(2)}) %collective-permute-start.9) | collective-permute-done | bytes 294944 | tf_op jit(solution)/shard_map/ppermute | solution.py:50
  32.8 0.4 weigh.1.refs_0_
  33.3 1.6 %collective-permute-start.10 = (f32[128,128]{1,0:T(8,128)S(1)}, f32[128,128]{1,0:T(8,128)S(1)}, u32[]{:S(2)}, u32[]{:S(2)}) collective-permute-start(f32[128,128]{1,0:T(8,128)S(1)} %weigh.1.refs_0_), channel_id=1, source_target_pairs={{0,1},{1,0},{2,3},{3,2},{4,5},{5,4},{6,7},{7,6},{8,9},{9,8},{10,11... | collective-permute-start | bytes 196616 | tf_op jit(solution)/shard_map/ppermute | solution.py:50
  34.8 2.8 %collective-permute-done.10.refs_1_ = f32[128,128]{1,0:T(8,128)S(1)} collective-permute-done((f32[128,128]{1,0:T(8,128)S(1)}, f32[128,128]{1,0:T(8,128)S(1)}, u32[]{:S(2)}, u32[]{:S(2)}) %collective-permute-start.10) | collective-permute-done | bytes 65568 | tf_op jit(solution)/shard_map/ppermute | solution.py:50
  37.6 0.4 apply.3
  38.0 0.1 collective-permute-start.11
  38.1 0.1 pad_add_fusion.place_ref
  38.2 1.1 %fusion = f32[128,128]{1,0:T(8,128)S(1)} fusion(f32[1152,128]{1,0:T(8,128)S(1)} %constant_dynamic-update-slice_fusion.6.left_ref.refs_0_), kind=kOutput, calls=%fused_computation.25 | convolution fusion | flops 226492416 | bytes 655360 | tf_op jit(solution)/shard_map/dot_general | solution.py:414
  39.3 1.6 %collective-permute-start.12 = (f32[128,128]{1,0:T(8,128)S(1)}, f32[128,128]{1,0:T(8,128)S(1)}, u32[]{:S(2)}, u32[]{:S(2)}) collective-permute-start(f32[128,128]{1,0:T(8,128)S(1)} %fusion), channel_id=1, source_target_pairs={{0,1},{1,0},{2,3},{3,2},{4,5},{5,4},{6,7},{7,6},{8,9},{9,8},{10,11... | collective-permute-start | bytes 196616 | tf_op jit(solution)/shard_map/ppermute | solution.py:50
  40.8 0.5 collective-permute-start.13
  41.4 0.0 collective-permute-done.11
  41.4 2.6 %collective-permute-done.12 = f32[128,128]{1,0:T(8,128)S(1)} collective-permute-done((f32[128,128]{1,0:T(8,128)S(1)}, f32[128,128]{1,0:T(8,128)S(1)}, u32[]{:S(2)}, u32[]{:S(2)}) %collective-permute-start.12) | collective-permute-done | bytes 65568 | tf_op jit(solution)/shard_map/ppermute | solution.py:50
  44.0 0.7 collective-permute-start.14
  44.7 1.6 %collective-permute-start.16 = (f32[128,128]{1,0:T(8,128)S(1)}, f32[128,128]{1,0:T(8,128)S(1)}, u32[]{:S(2)}, u32[]{:S(2)}) collective-permute-start(f32[128,128]{1,0:T(8,128)S(1)} %get-tuple-element.26), channel_id=1, source_target_pairs={{0,12},{2,14},{4,8},{6,10},{8,4},{10,6},{12,0},{14,2},{16,28},{18,... | collective-permute-start | bytes 196616 | tf_op jit(solution)/shard_map/ppermute | solution.py:50
  46.3 1.3 %collective-permute-start.15 = (f32[128,128]{1,0:T(8,128)S(1)}, f32[128,128]{1,0:T(8,128)S(1)}, u32[]{:S(2)}, u32[]{:S(2)}) collective-permute-start(f32[128,128]{1,0:T(8,128)S(1)} %get-tuple-element.27), channel_id=1, source_target_pairs={{0,8},{2,10},{4,12},{6,14},{8,0},{10,2},{12,4},{14,6},{16,24},{18,... | collective-permute-start | bytes 196616 | tf_op jit(solution)/shard_map/ppermute | solution.py:50
  47.6 2.6 %shard_map.50.state_ref = f32[128,128]{1,0:T(8,128)S(1)} custom-call(f32[128,128]{1,0:T(8,128)S(1)} %add.109.state_ref), custom_call_target="tpu_custom_call" | custom-call | flops 3000000000 | bytes 131072 | tf_op jit(solution)/shard_map/pallas_call | solution.py:174
  50.2 0.0 collective-permute-done.14
  50.3 0.0 collective-permute-done.16
  50.3 0.3 collective-permute-done.15
  50.6 3.4 %collective-permute-start.17 = (f32[128,128]{1,0:T(8,128)S(1)}, f32[128,128]{1,0:T(8,128)S(1)}, u32[]{:S(2)}, u32[]{:S(2)}) collective-permute-start(f32[128,128]{1,0:T(8,128)S(1)} %add_add_fusion.1.refs_0_), channel_id=1, source_target_pairs={{0,16},{2,18},{4,20},{6,22},{8,24},{10,26},{12,28},{14,30},{16,0},... | collective-permute-start | bytes 196616 | tf_op jit(solution)/shard_map/ppermute | solution.py:50
  53.9 2.2 %shard_map.51.inverse_ref = f32[128,128]{1,0:T(8,128)S(1)} custom-call(f32[128,128]{1,0:T(8,128)S(1)} %shard_map.50.state_ref), custom_call_target="tpu_custom_call" | custom-call | flops 3000000000 | bytes 131072 | tf_op jit(solution)/shard_map/pallas_call | solution.py:174
  56.1 0.1 collective-permute-done.17.refs_1_
  56.2 0.3 turn.1
  56.5 1.8 %collective-permute-start.20 = (f32[128,128]{1,0:T(8,128)S(1)}, f32[128,128]{1,0:T(8,128)S(1)}, u32[]{:S(2)}, u32[]{:S(2)}) collective-permute-start(f32[128,128]{1,0:T(8,128)S(1)} %turn.1), channel_id=1, source_target_pairs={{0,12},{2,14},{4,8},{6,10},{8,4},{10,6},{12,0},{14,2},{16,28},{18,... | collective-permute-start | bytes 196616 | tf_op jit(solution)/shard_map/ppermute | solution.py:50
  58.3 0.5 collective-permute-start.19
  58.8 1.3 %collective-permute-start.18 = (f32[128,128]{1,0:T(8,128)S(1)}, f32[128,128]{1,0:T(8,128)S(1)}, u32[]{:S(2)}, u32[]{:S(2)}) collective-permute-start(f32[128,128]{1,0:T(8,128)S(1)} %turn.1), channel_id=1, source_target_pairs={{0,4},{2,6},{4,0},{6,2},{8,12},{10,14},{12,8},{14,10},{16,20},{18,... | collective-permute-start | bytes 196616 | tf_op jit(solution)/shard_map/ppermute | solution.py:50
  60.1 0.0 copy-start
  60.1 3.0 %collective-permute-done.18 = f32[128,128]{1,0:T(8,128)S(1)} collective-permute-done((f32[128,128]{1,0:T(8,128)S(1)}, f32[128,128]{1,0:T(8,128)S(1)}, u32[]{:S(2)}, u32[]{:S(2)}) %collective-permute-start.18) | collective-permute-done | bytes 65568 | tf_op jit(solution)/shard_map/ppermute | solution.py:50
  63.1 0.0 collective-permute-done.19
  63.1 0.0 collective-permute-done.20
  63.2 0.1 collective-permute-start.21
  63.3 0.0 collective-permute-done.13.refs_1_
  63.3 1.9 %basis.1.mine_ref.tall_ref = bf16[2304,512]{1,0:T(8,128)(2,1)S(1)} custom-call(s32[2]{0:T(128)S(1)} %pad_add_fusion.place_ref, f32[128,128]{1,0:T(8,128)S(1)} %shard_map.51.inverse_ref, bf16[2304,128]{1,0:T(8,128)(2,1)S(1)} %bitcast.9, f32[1152,128]{1,0:T(8,128)S(1)} %constant_dynamic-update-slice_fusion.6.left_ref.refs_0_, ...), custom_call_target="tpu_custom_call" | custom-call | flops 2000000000 | bytes 131072 | tf_op jit(solution)/shard_map/basis/pallas_call | solution.py:295
  65.2 0.0 collective-permute-done.21
  65.3 0.0 copy-done
  65.3 3.7 %finish.1 = (f32[144,1024]{1,0:T(8,128)}, bf16[2304,1024]{1,0:T(8,128)(2,1)}) custom-call(s32[1]{0:T(128)} %bitcast.place_ref, bf16[2304,512]{1,0:T(8,128)(2,1)S(1)} %basis.1.mine_ref.tall_ref, bf16[2304,512]{1,0:T(8,128)(2,1)S(1)} %basis.1.mine_ref.tall_ref, bf16[128,1024]{1,0:T(8,128)(2,1)S(1)} %copy-done, ...), custom_call_target="tpu_custom_call" | custom-call | tf_op jit(solution)/shard_map/finish/pallas_call | solution.py:371
  (25 shorter events, 0.5 us)
Async XLA Ops:
  2.2 5.5 %collective-permute-start = (f32[128,128]{1,0:T(8,128)S(1)}, f32[128,128]{1,0:T(8,128)S(1)}, u32[]{:S(2)}, u32[]{:S(2)}) collective-permute-start(f32[128,128]{1,0:T(8,128)S(1)} %project.1.refs_0_), channel_id=1, source_target_pairs={{0,1},{1,0},{2,3},{3,2},{4,5},{5,4},{6,7},{7,6},{8,9},{9,8},{10,11... | collective-permute-start | bytes 196616 | tf_op jit(solution)/shard_map/ppermute | solution.py:50
  8.1 1.6 %collective-permute-start.1 = (f32[576,128]{1,0:T(8,128)S(1)}, f32[576,128]{1,0:T(8,128)S(1)}, u32[]{:S(2)}, u32[]{:S(2)}) collective-permute-start(f32[576,128]{1,0:T(8,128)S(1)} %constant_dynamic-slice_fusion.7), channel_id=1, source_target_pairs={{0,2},{2,0},{4,6},{6,4},{8,10},{10,8},{12,14},{14,12},{16,18},{18,... | collective-permute-start | bytes 884744 | tf_op jit(solution)/shard_map/ppermute | solution.py:50
  9.9 5.2 %collective-permute-start.2 = (f32[144,128]{1,0:T(8,128)S(1)}, f32[144,128]{1,0:T(8,128)S(1)}, u32[]{:S(2)}, u32[]{:S(2)}) collective-permute-start(f32[144,128]{1,0:T(8,128)S(1)} %get-tuple-element.22), channel_id=1, source_target_pairs={{0,4},{2,6},{4,0},{6,2},{8,12},{10,14},{12,8},{14,10},{16,20},{18,... | collective-permute-start | bytes 221192 | tf_op jit(solution)/shard_map/ppermute | solution.py:50
  11.7 5.9 %collective-permute-start.4 = (f32[144,128]{1,0:T(8,128)S(1)}, f32[144,128]{1,0:T(8,128)S(1)}, u32[]{:S(2)}, u32[]{:S(2)}) collective-permute-start(f32[144,128]{1,0:T(8,128)S(1)} %get-tuple-element.23), channel_id=1, source_target_pairs={{0,12},{2,14},{4,8},{6,10},{8,4},{10,6},{12,0},{14,2},{16,28},{18,... | collective-permute-start | bytes 221192 | tf_op jit(solution)/shard_map/ppermute | solution.py:50
  13.2 4.4 %collective-permute-start.3 = (f32[144,128]{1,0:T(8,128)S(1)}, f32[144,128]{1,0:T(8,128)S(1)}, u32[]{:S(2)}, u32[]{:S(2)}) collective-permute-start(f32[144,128]{1,0:T(8,128)S(1)} %get-tuple-element.24), channel_id=1, source_target_pairs={{0,8},{2,10},{4,12},{6,14},{8,0},{10,2},{12,4},{14,6},{16,24},{18,... | collective-permute-start | bytes 221192 | tf_op jit(solution)/shard_map/ppermute | solution.py:50
  17.6 5.3 %collective-permute-start.5 = (f32[144,128]{1,0:T(8,128)S(1)}, f32[144,128]{1,0:T(8,128)S(1)}, u32[]{:S(2)}, u32[]{:S(2)}) collective-permute-start(f32[144,128]{1,0:T(8,128)S(1)} %add_add_fusion), channel_id=1, source_target_pairs={{0,16},{2,18},{4,20},{6,22},{8,24},{10,26},{12,28},{14,30},{16,0},... | collective-permute-start | bytes 221192 | tf_op jit(solution)/shard_map/ppermute | solution.py:50
  23.0 5.2 %collective-permute-start.6 = (f32[144,128]{1,0:T(8,128)S(1)}, f32[144,128]{1,0:T(8,128)S(1)}, u32[]{:S(2)}, u32[]{:S(2)}) collective-permute-start(f32[144,128]{1,0:T(8,128)S(1)} %get-tuple-element.21), channel_id=1, source_target_pairs={{0,4},{2,6},{4,0},{6,2},{8,12},{10,14},{12,8},{14,10},{16,20},{18,... | collective-permute-start | bytes 221192 | tf_op jit(solution)/shard_map/ppermute | solution.py:50
  24.6 4.4 %collective-permute-start.7 = (f32[144,128]{1,0:T(8,128)S(1)}, f32[144,128]{1,0:T(8,128)S(1)}, u32[]{:S(2)}, u32[]{:S(2)}) collective-permute-start(f32[144,128]{1,0:T(8,128)S(1)} %get-tuple-element.21), channel_id=1, source_target_pairs={{0,8},{2,10},{4,12},{6,14},{8,0},{10,2},{12,4},{14,6},{16,24},{18,... | collective-permute-start | bytes 221192 | tf_op jit(solution)/shard_map/ppermute | solution.py:50
  25.9 5.3 %collective-permute-start.8 = (f32[144,128]{1,0:T(8,128)S(1)}, f32[144,128]{1,0:T(8,128)S(1)}, u32[]{:S(2)}, u32[]{:S(2)}) collective-permute-start(f32[144,128]{1,0:T(8,128)S(1)} %get-tuple-element.21), channel_id=1, source_target_pairs={{0,12},{2,14},{4,8},{6,10},{8,4},{10,6},{12,0},{14,2},{16,28},{18,... | collective-permute-start | bytes 221192 | tf_op jit(solution)/shard_map/ppermute | solution.py:50
  31.2 1.6 %collective-permute-start.9 = (f32[576,128]{1,0:T(8,128)S(1)}, f32[576,128]{1,0:T(8,128)S(1)}, u32[]{:S(2)}, u32[]{:S(2)}) collective-permute-start(f32[576,128]{1,0:T(8,128)S(1)} %constant_dynamic-update-slice_fusion.8), channel_id=1, source_target_pairs={{0,2},{2,0},{4,6},{6,4},{8,10},{10,8},{12,14},{14,12},{16,18},{18,... | collective-permute-start | bytes 884744 | tf_op jit(solution)/shard_map/ppermute | solution.py:50
  33.3 4.3 %collective-permute-start.10 = (f32[128,128]{1,0:T(8,128)S(1)}, f32[128,128]{1,0:T(8,128)S(1)}, u32[]{:S(2)}, u32[]{:S(2)}) collective-permute-start(f32[128,128]{1,0:T(8,128)S(1)} %weigh.1.refs_0_), channel_id=1, source_target_pairs={{0,1},{1,0},{2,3},{3,2},{4,5},{5,4},{6,7},{7,6},{8,9},{9,8},{10,11... | collective-permute-start | bytes 196616 | tf_op jit(solution)/shard_map/ppermute | solution.py:50
  38.0 3.4 %collective-permute-start.11 = (f32[512,128]{1,0:T(8,128)S(1)}, f32[512,128]{1,0:T(8,128)S(1)}, u32[]{:S(2)}, u32[]{:S(2)}) collective-permute-start(f32[512,128]{1,0:T(8,128)S(1)} %constant_dynamic-slice_fusion.3), channel_id=1, source_target_pairs={{0,2},{2,0},{4,6},{6,4},{8,10},{10,8},{12,14},{14,12},{16,18},{18,... | collective-permute-start | bytes 786440 | tf_op jit(solution)/shard_map/ppermute | solution.py:50
  39.3 4.7 %collective-permute-start.12 = (f32[128,128]{1,0:T(8,128)S(1)}, f32[128,128]{1,0:T(8,128)S(1)}, u32[]{:S(2)}, u32[]{:S(2)}) collective-permute-start(f32[128,128]{1,0:T(8,128)S(1)} %fusion), channel_id=1, source_target_pairs={{0,1},{1,0},{2,3},{3,2},{4,5},{5,4},{6,7},{7,6},{8,9},{9,8},{10,11... | collective-permute-start | bytes 196616 | tf_op jit(solution)/shard_map/ppermute | solution.py:50
  40.8 22.5 %collective-permute-start.13 = (f32[1152,128]{1,0:T(8,128)S(1)}, f32[1152,128]{1,0:T(8,128)S(1)}, u32[]{:S(2)}, u32[]{:S(2)}) collective-permute-start(f32[1152,128]{1,0:T(8,128)S(1)} %constant_dynamic-update-slice_fusion.6.left_ref.refs_0_), channel_id=1, source_target_pairs={{0,1},{1,0},{2,3},{3,2},{4,5},{5,4},{6,7},{7,6},{8,9},{9,8},{10,11... | collective-permute-start | bytes 1769480 | tf_op jit(solution)/shard_map/ppermute | solution.py:50
  44.0 6.2 %collective-permute-start.14 = (f32[128,128]{1,0:T(8,128)S(1)}, f32[128,128]{1,0:T(8,128)S(1)}, u32[]{:S(2)}, u32[]{:S(2)}) collective-permute-start(f32[128,128]{1,0:T(8,128)S(1)} %get-tuple-element.25), channel_id=1, source_target_pairs={{0,4},{2,6},{4,0},{6,2},{8,12},{10,14},{12,8},{14,10},{16,20},{18,... | collective-permute-start | bytes 196616 | tf_op jit(solution)/shard_map/ppermute | solution.py:50
  44.7 5.6 %collective-permute-start.16 = (f32[128,128]{1,0:T(8,128)S(1)}, f32[128,128]{1,0:T(8,128)S(1)}, u32[]{:S(2)}, u32[]{:S(2)}) collective-permute-start(f32[128,128]{1,0:T(8,128)S(1)} %get-tuple-element.26), channel_id=1, source_target_pairs={{0,12},{2,14},{4,8},{6,10},{8,4},{10,6},{12,0},{14,2},{16,28},{18,... | collective-permute-start | bytes 196616 | tf_op jit(solution)/shard_map/ppermute | solution.py:50
  46.3 4.3 %collective-permute-start.15 = (f32[128,128]{1,0:T(8,128)S(1)}, f32[128,128]{1,0:T(8,128)S(1)}, u32[]{:S(2)}, u32[]{:S(2)}) collective-permute-start(f32[128,128]{1,0:T(8,128)S(1)} %get-tuple-element.27), channel_id=1, source_target_pairs={{0,8},{2,10},{4,12},{6,14},{8,0},{10,2},{12,4},{14,6},{16,24},{18,... | collective-permute-start | bytes 196616 | tf_op jit(solution)/shard_map/ppermute | solution.py:50
  50.6 5.6 %collective-permute-start.17 = (f32[128,128]{1,0:T(8,128)S(1)}, f32[128,128]{1,0:T(8,128)S(1)}, u32[]{:S(2)}, u32[]{:S(2)}) collective-permute-start(f32[128,128]{1,0:T(8,128)S(1)} %add_add_fusion.1.refs_0_), channel_id=1, source_target_pairs={{0,16},{2,18},{4,20},{6,22},{8,24},{10,26},{12,28},{14,30},{16,0},... | collective-permute-start | bytes 196616 | tf_op jit(solution)/shard_map/ppermute | solution.py:50
  56.5 6.6 %collective-permute-start.20 = (f32[128,128]{1,0:T(8,128)S(1)}, f32[128,128]{1,0:T(8,128)S(1)}, u32[]{:S(2)}, u32[]{:S(2)}) collective-permute-start(f32[128,128]{1,0:T(8,128)S(1)} %turn.1), channel_id=1, source_target_pairs={{0,12},{2,14},{4,8},{6,10},{8,4},{10,6},{12,0},{14,2},{16,28},{18,... | collective-permute-start | bytes 196616 | tf_op jit(solution)/shard_map/ppermute | solution.py:50
  58.3 4.8 %collective-permute-start.19 = (f32[128,128]{1,0:T(8,128)S(1)}, f32[128,128]{1,0:T(8,128)S(1)}, u32[]{:S(2)}, u32[]{:S(2)}) collective-permute-start(f32[128,128]{1,0:T(8,128)S(1)} %turn.1), channel_id=1, source_target_pairs={{0,8},{2,10},{4,12},{6,14},{8,0},{10,2},{12,4},{14,6},{16,24},{18,... | collective-permute-start | bytes 196616 | tf_op jit(solution)/shard_map/ppermute | solution.py:50
  58.8 4.3 %collective-permute-start.18 = (f32[128,128]{1,0:T(8,128)S(1)}, f32[128,128]{1,0:T(8,128)S(1)}, u32[]{:S(2)}, u32[]{:S(2)}) collective-permute-start(f32[128,128]{1,0:T(8,128)S(1)} %turn.1), channel_id=1, source_target_pairs={{0,4},{2,6},{4,0},{6,2},{8,12},{10,14},{12,8},{14,10},{16,20},{18,... | collective-permute-start | bytes 196616 | tf_op jit(solution)/shard_map/ppermute | solution.py:50
  60.1 5.2 %copy-start = (bf16[128,1024]{1,0:T(8,128)(2,1)S(1)}, bf16[128,1024]{1,0:T(8,128)(2,1)}, u32[]{:S(2)}) copy-start(bf16[128,1024]{1,0:T(8,128)(2,1)} %grads_ref.3) | copy-start | bytes 786436
  63.2 2.1 %collective-permute-start.21 = (f32[512,128]{1,0:T(8,128)S(1)}, f32[512,128]{1,0:T(8,128)S(1)}, u32[]{:S(2)}, u32[]{:S(2)}) collective-permute-start(f32[512,128]{1,0:T(8,128)S(1)} %constant_dynamic-update-slice_fusion.2), channel_id=1, source_target_pairs={{0,2},{2,0},{4,6},{6,4},{8,10},{10,8},{12,14},{14,12},{16,18},{18,... | collective-permute-start | bytes 786440 | tf_op jit(solution)/shard_map/ppermute | solution.py:50

commit v4 on v3

--- a/solution.py
+++ b/solution.py
@@ -214,15 +214,23 @@
 
 
 def project_body(grads_ref, right_ref, out_ref, grads, right, arrived):
-    copies = [
-        pltpu.make_async_copy(grads_ref, grads, arrived.at[0]),
-        pltpu.make_async_copy(right_ref, right, arrived.at[1]),
-    ]
-    for copy in copies:
-        copy.start()
-    for copy in copies:
+    depth = right_ref.shape[0]
+    step = depth // 4 if depth % 512 == 0 else depth
+    starts = range(0, depth, step)
+    whole = pltpu.make_async_copy(grads_ref, grads, arrived.at[0])
+    whole.start()
+    copies = []
+    for index, start in enumerate(starts):
+        rows = pl.ds(start, step)
+        copies.append(pltpu.make_async_copy(right_ref.at[rows, :], right.at[rows, :], arrived.at[1 + index]))
+        copies[-1].start()
+    whole.wait()
+    total = None
+    for copy, start in zip(copies, starts):
         copy.wait()
-    out_ref[...] = exact_dot(grads[...], right[...], (1, 0))
+        part = exact_dot(grads[:, start : start + step], right[start : start + step, :], (1, 0))
+        total = part if total is None else total + part
+    out_ref[...] = total
 
 
 def project(out_grads, right_prev):
@@ -234,7 +242,7 @@
         scratch_shapes=[
             pltpu.VMEM(out_grads.shape, out_grads.dtype),
             pltpu.VMEM(right_prev.shape, right_prev.dtype),
-            pltpu.SemaphoreType.DMA((2,)),
+            pltpu.SemaphoreType.DMA((5,)),
         ],
         compiler_params=grant(6),
         name="project",
@@ -402,10 +410,12 @@
     my_rows = rows // columns
     place = lax.axis_index("tp").astype(jnp.int32).reshape(1)
     origin = jnp.zeros((1,), jnp.int32)
-    acts, grads = lax.optimization_barrier((activations.T, out_grads.T))
+    acts = lax.optimization_barrier(activations.T)
 
     projected, _ = sent_all(project(out_grads, right_prev), "tp")
     left_part = padded_rows(apply(place, acts, my_rows, projected), blocks_of("dp"))
+    grads_late, left_part = lax.optimization_barrier((out_grads, left_part))
+    grads = lax.optimization_barrier(grads_late.T)
     left_parts, _ = scatter_sum(left_part, "dp")
     left_own = gather_rows(together(left_parts, "dp"), "dp")[:my_rows]
 

time: 69.3 us -> 70.4 us (1.016)
  waiting for transfers between devices: 23.1 us -> 25.4 us
  local copies, waits for them, and re-layouts: 2.87 us -> 1.91 us
    ppermute x22, waiting for transfers between devices: 23.1 us -> 25.4 us  [shifted(): return lax.ppermute(value, axis, pairs)]
    unnamed x4 -> x3, local copies, waits for them, and re-layouts: 2.49 us -> 1.37 us
  transfers between devices with their start and end apart: 22 -> 22, of which waited for: 13 -> 14; matrix products, arithmetic and copies ran while one was open for 6% -> 4% of each run, Pallas kernels for 10% -> 10%
where the time goes in v4:
time: 70.4 us; the launch traced here: 70.2 us
  starting transfers between devices  26.6 us (38%)
  waiting for transfers between devices  25.4 us (36%)
  Pallas kernels  13.9 us (20%)
  local copies, waits for them, and re-layouts  1.91 us (3%)
  matrix products  1.12 us (2%)
  between operations  1 us (1%)
    ppermute x22, starting transfers between devices, shifted(): return lax.ppermute(value, axis, pairs)  26.6 us
    ppermute x22, waiting for transfers between devices, shifted(): return lax.ppermute(value, axis, pairs)  25.4 us
    pallas_call x2, Pallas kernels, inverse_factor(): state = call(state)  4.79 us
    pallas_call x1, Pallas kernels, finish(): pl.pallas_call(functools.partial(finish_body, replicas, turned), out_shap...  3.71 us
    pallas_call x1, Pallas kernels, project(): pl.pallas_call(project_body, out_shape=jax.ShapeDtypeStruct((out_grads.sh...  1.96 us
    pallas_call x1, Pallas kernels, basis(): pl.pallas_call(basis_body, out_shape=jax.ShapeDtypeStruct((acts.shape[0],...  1.89 us
  transfers between devices with their start and end apart: 22, of which 14 were waited for; matrix products, arithmetic and copies ran while one was open for 4% of the time, Pallas kernels for 10%

profile of v4, /device:TPU:0, one launch (start us, length us, event | category | flops | bytes accessed | tf_op | source)
XLA Modules:
  0.0 70.2 jit_solution(2992516844003633912)
XLA Ops:
  0.6 0.0 copy-start
  0.6 2.0 %project.1.refs_0_ = f32[128,128]{1,0:T(8,128)S(1)} custom-call(bf16[128,1024]{1,0:T(8,128)(2,1)} %grads_ref.3, f32[1024,128]{1,0:T(8,128)} %right_ref.1), custom_call_target="tpu_custom_call" | custom-call | tf_op jit(solution)/shard_map/project/pallas_call | solution.py:237
  2.6 3.0 %collective-permute-start = (f32[128,128]{1,0:T(8,128)S(1)}, f32[128,128]{1,0:T(8,128)S(1)}, u32[]{:S(2)}, u32[]{:S(2)}) collective-permute-start(f32[128,128]{1,0:T(8,128)S(1)} %project.1.refs_0_), channel_id=1, source_target_pairs={{0,1},{1,0},{2,3},{3,2},{4,5},{5,4},{6,7},{7,6},{8,9},{9,8},{10,11... | collective-permute-start | bytes 196616 | tf_op jit(solution)/shard_map/ppermute | solution.py:50
  5.6 1.4 %copy.5 = bf16[128,2304]{0,1:T(8,128)(2,1)S(1)} copy(bf16[128,2304]{1,0:T(8,128)(2,1)} %param.3) | data formatting | bytes 1179648 | tf_op args[0]
  7.0 0.9 %collective-permute-done.refs_1_ = f32[128,128]{1,0:T(8,128)S(1)} collective-permute-done((f32[128,128]{1,0:T(8,128)S(1)}, f32[128,128]{1,0:T(8,128)S(1)}, u32[]{:S(2)}, u32[]{:S(2)}) %collective-permute-start) | collective-permute-done | bytes 65568 | tf_op jit(solution)/shard_map/ppermute | solution.py:50
  7.9 0.4 apply.2
  8.3 0.1 collective-permute-start.1
  8.5 1.5 %collective-permute-done.1 = f32[576,128]{1,0:T(8,128)S(1)} collective-permute-done((f32[576,128]{1,0:T(8,128)S(1)}, f32[576,128]{1,0:T(8,128)S(1)}, u32[]{:S(2)}, u32[]{:S(2)}) %collective-permute-start.1) | collective-permute-done | bytes 294944 | tf_op jit(solution)/shard_map/ppermute | solution.py:50
  10.0 2.1 %collective-permute-start.2 = (f32[144,128]{1,0:T(8,128)S(1)}, f32[144,128]{1,0:T(8,128)S(1)}, u32[]{:S(2)}, u32[]{:S(2)}) collective-permute-start(f32[144,128]{1,0:T(8,128)S(1)} %get-tuple-element.22), channel_id=1, source_target_pairs={{0,4},{2,6},{4,0},{6,2},{8,12},{10,14},{12,8},{14,10},{16,20},{18,... | collective-permute-start | bytes 221192 | tf_op jit(solution)/shard_map/ppermute | solution.py:50
  12.2 1.5 %collective-permute-start.4 = (f32[144,128]{1,0:T(8,128)S(1)}, f32[144,128]{1,0:T(8,128)S(1)}, u32[]{:S(2)}, u32[]{:S(2)}) collective-permute-start(f32[144,128]{1,0:T(8,128)S(1)} %get-tuple-element.23), channel_id=1, source_target_pairs={{0,12},{2,14},{4,8},{6,10},{8,4},{10,6},{12,0},{14,2},{16,28},{18,... | collective-permute-start | bytes 221192 | tf_op jit(solution)/shard_map/ppermute | solution.py:50
  13.7 0.1 collective-permute-start.3
  13.7 1.9 %collective-permute-done.2 = f32[144,128]{1,0:T(8,128)S(1)} collective-permute-done((f32[144,128]{1,0:T(8,128)S(1)}, f32[144,128]{1,0:T(8,128)S(1)}, u32[]{:S(2)}, u32[]{:S(2)}) %collective-permute-start.2) | collective-permute-done | bytes 73760 | tf_op jit(solution)/shard_map/ppermute | solution.py:50
  15.6 2.4 %collective-permute-done.4 = f32[144,128]{1,0:T(8,128)S(1)} collective-permute-done((f32[144,128]{1,0:T(8,128)S(1)}, f32[144,128]{1,0:T(8,128)S(1)}, u32[]{:S(2)}, u32[]{:S(2)}) %collective-permute-start.4) | collective-permute-done | bytes 73760 | tf_op jit(solution)/shard_map/ppermute | solution.py:50
  18.0 0.0 collective-permute-done.3
  18.0 2.7 %collective-permute-start.5 = (f32[144,128]{1,0:T(8,128)S(1)}, f32[144,128]{1,0:T(8,128)S(1)}, u32[]{:S(2)}, u32[]{:S(2)}) collective-permute-start(f32[144,128]{1,0:T(8,128)S(1)} %add_add_fusion), channel_id=1, source_target_pairs={{0,16},{2,18},{4,20},{6,22},{8,24},{10,26},{12,28},{14,30},{16,0},... | collective-permute-start | bytes 221192 | tf_op jit(solution)/shard_map/ppermute | solution.py:50
  20.7 2.7 %collective-permute-done.5 = f32[144,128]{1,0:T(8,128)S(1)} collective-permute-done((f32[144,128]{1,0:T(8,128)S(1)}, f32[144,128]{1,0:T(8,128)S(1)}, u32[]{:S(2)}, u32[]{:S(2)}) %collective-permute-start.5) | collective-permute-done | bytes 73760 | tf_op jit(solution)/shard_map/ppermute | solution.py:50
  23.4 2.4 %collective-permute-start.6 = (f32[144,128]{1,0:T(8,128)S(1)}, f32[144,128]{1,0:T(8,128)S(1)}, u32[]{:S(2)}, u32[]{:S(2)}) collective-permute-start(f32[144,128]{1,0:T(8,128)S(1)} %get-tuple-element.21), channel_id=1, source_target_pairs={{0,4},{2,6},{4,0},{6,2},{8,12},{10,14},{12,8},{14,10},{16,20},{18,... | collective-permute-start | bytes 221192 | tf_op jit(solution)/shard_map/ppermute | solution.py:50
  25.8 0.6 collective-permute-start.7
  26.4 1.0 %collective-permute-start.8 = (f32[144,128]{1,0:T(8,128)S(1)}, f32[144,128]{1,0:T(8,128)S(1)}, u32[]{:S(2)}, u32[]{:S(2)}) collective-permute-start(f32[144,128]{1,0:T(8,128)S(1)} %get-tuple-element.21), channel_id=1, source_target_pairs={{0,12},{2,14},{4,8},{6,10},{8,4},{10,6},{12,0},{14,2},{16,28},{18,... | collective-permute-start | bytes 221192 | tf_op jit(solution)/shard_map/ppermute | solution.py:50
  27.3 1.6 %collective-permute-done.6 = f32[144,128]{1,0:T(8,128)S(1)} collective-permute-done((f32[144,128]{1,0:T(8,128)S(1)}, f32[144,128]{1,0:T(8,128)S(1)}, u32[]{:S(2)}, u32[]{:S(2)}) %collective-permute-start.6) | collective-permute-done | bytes 73760 | tf_op jit(solution)/shard_map/ppermute | solution.py:50
  28.9 1.2 %collective-permute-done.7 = f32[144,128]{1,0:T(8,128)S(1)} collective-permute-done((f32[144,128]{1,0:T(8,128)S(1)}, f32[144,128]{1,0:T(8,128)S(1)}, u32[]{:S(2)}, u32[]{:S(2)}) %collective-permute-start.7) | collective-permute-done | bytes 73760 | tf_op jit(solution)/shard_map/ppermute | solution.py:50
  30.2 1.4 %collective-permute-done.8 = f32[144,128]{1,0:T(8,128)S(1)} collective-permute-done((f32[144,128]{1,0:T(8,128)S(1)}, f32[144,128]{1,0:T(8,128)S(1)}, u32[]{:S(2)}, u32[]{:S(2)}) %collective-permute-start.8) | collective-permute-done | bytes 73760 | tf_op jit(solution)/shard_map/ppermute | solution.py:50
  31.6 0.1 collective-permute-start.9
  31.8 1.5 %collective-permute-done.9 = f32[576,128]{1,0:T(8,128)S(1)} collective-permute-done((f32[576,128]{1,0:T(8,128)S(1)}, f32[576,128]{1,0:T(8,128)S(1)}, u32[]{:S(2)}, u32[]{:S(2)}) %collective-permute-start.9) | collective-permute-done | bytes 294944 | tf_op jit(solution)/shard_map/ppermute | solution.py:50
  33.3 0.4 weigh.1.refs_0_
  33.7 1.6 %collective-permute-start.10 = (f32[128,128]{1,0:T(8,128)S(1)}, f32[128,128]{1,0:T(8,128)S(1)}, u32[]{:S(2)}, u32[]{:S(2)}) collective-permute-start(f32[128,128]{1,0:T(8,128)S(1)} %weigh.1.refs_0_), channel_id=1, source_target_pairs={{0,1},{1,0},{2,3},{3,2},{4,5},{5,4},{6,7},{7,6},{8,9},{9,8},{10,11... | collective-permute-start | bytes 196616 | tf_op jit(solution)/shard_map/ppermute | solution.py:50
  35.3 0.0 copy-done
  35.3 0.2 copy.6
  35.5 2.6 %collective-permute-done.10.refs_1_ = f32[128,128]{1,0:T(8,128)S(1)} collective-permute-done((f32[128,128]{1,0:T(8,128)S(1)}, f32[128,128]{1,0:T(8,128)S(1)}, u32[]{:S(2)}, u32[]{:S(2)}) %collective-permute-start.10) | collective-permute-done | bytes 65568 | tf_op jit(solution)/shard_map/ppermute | solution.py:50
  38.1 0.4 apply.3
  38.5 0.1 collective-permute-start.11
  38.5 0.1 pad_add_fusion.place_ref
  38.6 1.1 %fusion = f32[128,128]{1,0:T(8,128)S(1)} fusion(f32[1152,128]{1,0:T(8,128)S(1)} %constant_dynamic-update-slice_fusion.6.left_ref.refs_0_), kind=kOutput, calls=%fused_computation.25 | convolution fusion | flops 226492416 | bytes 655360 | tf_op jit(solution)/shard_map/dot_general | solution.py:424
  39.7 1.6 %collective-permute-start.12 = (f32[128,128]{1,0:T(8,128)S(1)}, f32[128,128]{1,0:T(8,128)S(1)}, u32[]{:S(2)}, u32[]{:S(2)}) collective-permute-start(f32[128,128]{1,0:T(8,128)S(1)} %fusion), channel_id=1, source_target_pairs={{0,1},{1,0},{2,3},{3,2},{4,5},{5,4},{6,7},{7,6},{8,9},{9,8},{10,11... | collective-permute-start | bytes 196616 | tf_op jit(solution)/shard_map/ppermute | solution.py:50
  41.3 0.5 collective-permute-start.13
  41.8 0.0 collective-permute-done.11
  41.9 2.6 %collective-permute-done.12 = f32[128,128]{1,0:T(8,128)S(1)} collective-permute-done((f32[128,128]{1,0:T(8,128)S(1)}, f32[128,128]{1,0:T(8,128)S(1)}, u32[]{:S(2)}, u32[]{:S(2)}) %collective-permute-start.12) | collective-permute-done | bytes 65568 | tf_op jit(solution)/shard_map/ppermute | solution.py:50
  44.5 1.1 %collective-permute-start.14 = (f32[128,128]{1,0:T(8,128)S(1)}, f32[128,128]{1,0:T(8,128)S(1)}, u32[]{:S(2)}, u32[]{:S(2)}) collective-permute-start(f32[128,128]{1,0:T(8,128)S(1)} %get-tuple-element.25), channel_id=1, source_target_pairs={{0,4},{2,6},{4,0},{6,2},{8,12},{10,14},{12,8},{14,10},{16,20},{18,... | collective-permute-start | bytes 196616 | tf_op jit(solution)/shard_map/ppermute | solution.py:50
  45.6 2.2 %collective-permute-start.16 = (f32[128,128]{1,0:T(8,128)S(1)}, f32[128,128]{1,0:T(8,128)S(1)}, u32[]{:S(2)}, u32[]{:S(2)}) collective-permute-start(f32[128,128]{1,0:T(8,128)S(1)} %get-tuple-element.26), channel_id=1, source_target_pairs={{0,12},{2,14},{4,8},{6,10},{8,4},{10,6},{12,0},{14,2},{16,28},{18,... | collective-permute-start | bytes 196616 | tf_op jit(solution)/shard_map/ppermute | solution.py:50
  47.8 0.3 collective-permute-start.15
  48.1 2.6 %shard_map.50.state_ref = f32[128,128]{1,0:T(8,128)S(1)} custom-call(f32[128,128]{1,0:T(8,128)S(1)} %add.109.state_ref), custom_call_target="tpu_custom_call" | custom-call | flops 3000000000 | bytes 131072 | tf_op jit(solution)/shard_map/pallas_call | solution.py:174
  50.7 0.0 collective-permute-done.14
  50.7 0.0 collective-permute-done.16
  50.7 1.3 %collective-permute-done.15 = f32[128,128]{1,0:T(8,128)S(1)} collective-permute-done((f32[128,128]{1,0:T(8,128)S(1)}, f32[128,128]{1,0:T(8,128)S(1)}, u32[]{:S(2)}, u32[]{:S(2)}) %collective-permute-start.15) | collective-permute-done | bytes 65568 | tf_op jit(solution)/shard_map/ppermute | solution.py:50
  52.1 2.3 %collective-permute-start.17 = (f32[128,128]{1,0:T(8,128)S(1)}, f32[128,128]{1,0:T(8,128)S(1)}, u32[]{:S(2)}, u32[]{:S(2)}) collective-permute-start(f32[128,128]{1,0:T(8,128)S(1)} %add_add_fusion.1.refs_0_), channel_id=1, source_target_pairs={{0,16},{2,18},{4,20},{6,22},{8,24},{10,26},{12,28},{14,30},{16,0},... | collective-permute-start | bytes 196616 | tf_op jit(solution)/shard_map/ppermute | solution.py:50
  54.4 2.2 %shard_map.51.inverse_ref = f32[128,128]{1,0:T(8,128)S(1)} custom-call(f32[128,128]{1,0:T(8,128)S(1)} %shard_map.50.state_ref), custom_call_target="tpu_custom_call" | custom-call | flops 3000000000 | bytes 131072 | tf_op jit(solution)/shard_map/pallas_call | solution.py:174
  56.5 1.5 %collective-permute-done.17.refs_1_ = f32[128,128]{1,0:T(8,128)S(1)} collective-permute-done((f32[128,128]{1,0:T(8,128)S(1)}, f32[128,128]{1,0:T(8,128)S(1)}, u32[]{:S(2)}, u32[]{:S(2)}) %collective-permute-start.17) | collective-permute-done | bytes 65568 | tf_op jit(solution)/shard_map/ppermute | solution.py:50
  58.0 0.3 turn.1
  58.3 0.4 collective-permute-start.20
  58.7 0.5 collective-permute-start.19
  59.2 2.7 %collective-permute-start.18 = (f32[128,128]{1,0:T(8,128)S(1)}, f32[128,128]{1,0:T(8,128)S(1)}, u32[]{:S(2)}, u32[]{:S(2)}) collective-permute-start(f32[128,128]{1,0:T(8,128)S(1)} %turn.1), channel_id=1, source_target_pairs={{0,4},{2,6},{4,0},{6,2},{8,12},{10,14},{12,8},{14,10},{16,20},{18,... | collective-permute-start | bytes 196616 | tf_op jit(solution)/shard_map/ppermute | solution.py:50
  61.9 2.3 %collective-permute-done.18 = f32[128,128]{1,0:T(8,128)S(1)} collective-permute-done((f32[128,128]{1,0:T(8,128)S(1)}, f32[128,128]{1,0:T(8,128)S(1)}, u32[]{:S(2)}, u32[]{:S(2)}) %collective-permute-start.18) | collective-permute-done | bytes 65568 | tf_op jit(solution)/shard_map/ppermute | solution.py:50
  64.3 0.0 collective-permute-done.19
  64.3 0.0 collective-permute-done.20
  64.4 0.1 collective-permute-start.21
  64.5 0.0 collective-permute-done.13.refs_1_
  64.5 1.9 %basis.1.mine_ref.tall_ref = bf16[2304,512]{1,0:T(8,128)(2,1)S(1)} custom-call(s32[2]{0:T(128)S(1)} %pad_add_fusion.place_ref, f32[128,128]{1,0:T(8,128)S(1)} %shard_map.51.inverse_ref, bf16[2304,128]{1,0:T(8,128)(2,1)S(1)} %bitcast.9, f32[1152,128]{1,0:T(8,128)S(1)} %constant_dynamic-update-slice_fusion.6.left_ref.refs_0_, ...), custom_call_target="tpu_custom_call" | custom-call | flops 2000000000 | bytes 131072 | tf_op jit(solution)/shard_map/basis/pallas_call | solution.py:303
  66.4 0.0 collective-permute-done.21
  66.5 3.7 %finish.1 = (f32[144,1024]{1,0:T(8,128)}, bf16[2304,1024]{1,0:T(8,128)(2,1)}) custom-call(s32[1]{0:T(128)} %bitcast.place_ref, bf16[2304,512]{1,0:T(8,128)(2,1)S(1)} %basis.1.mine_ref.tall_ref, bf16[2304,512]{1,0:T(8,128)(2,1)S(1)} %basis.1.mine_ref.tall_ref, bf16[128,1024]{1,0:T(8,128)(2,1)S(1)} %copy-done, ...), custom_call_target="tpu_custom_call" | custom-call | tf_op jit(solution)/shard_map/finish/pallas_call | solution.py:379
  (25 shorter events, 0.5 us)
Async XLA Ops:
  0.6 34.7 %copy-start = (bf16[128,1024]{1,0:T(8,128)(2,1)S(1)}, bf16[128,1024]{1,0:T(8,128)(2,1)}, u32[]{:S(2)}) copy-start(bf16[128,1024]{1,0:T(8,128)(2,1)} %grads_ref.3) | copy-start | bytes 786436
  2.6 5.3 %collective-permute-start = (f32[128,128]{1,0:T(8,128)S(1)}, f32[128,128]{1,0:T(8,128)S(1)}, u32[]{:S(2)}, u32[]{:S(2)}) collective-permute-start(f32[128,128]{1,0:T(8,128)S(1)} %project.1.refs_0_), channel_id=1, source_target_pairs={{0,1},{1,0},{2,3},{3,2},{4,5},{5,4},{6,7},{7,6},{8,9},{9,8},{10,11... | collective-permute-start | bytes 196616 | tf_op jit(solution)/shard_map/ppermute | solution.py:50
  8.3 1.6 %collective-permute-start.1 = (f32[576,128]{1,0:T(8,128)S(1)}, f32[576,128]{1,0:T(8,128)S(1)}, u32[]{:S(2)}, u32[]{:S(2)}) collective-permute-start(f32[576,128]{1,0:T(8,128)S(1)} %constant_dynamic-slice_fusion.7), channel_id=1, source_target_pairs={{0,2},{2,0},{4,6},{6,4},{8,10},{10,8},{12,14},{14,12},{16,18},{18,... | collective-permute-start | bytes 884744 | tf_op jit(solution)/shard_map/ppermute | solution.py:50
  10.0 5.6 %collective-permute-start.2 = (f32[144,128]{1,0:T(8,128)S(1)}, f32[144,128]{1,0:T(8,128)S(1)}, u32[]{:S(2)}, u32[]{:S(2)}) collective-permute-start(f32[144,128]{1,0:T(8,128)S(1)} %get-tuple-element.22), channel_id=1, source_target_pairs={{0,4},{2,6},{4,0},{6,2},{8,12},{10,14},{12,8},{14,10},{16,20},{18,... | collective-permute-start | bytes 221192 | tf_op jit(solution)/shard_map/ppermute | solution.py:50
  12.2 5.9 %collective-permute-start.4 = (f32[144,128]{1,0:T(8,128)S(1)}, f32[144,128]{1,0:T(8,128)S(1)}, u32[]{:S(2)}, u32[]{:S(2)}) collective-permute-start(f32[144,128]{1,0:T(8,128)S(1)} %get-tuple-element.23), channel_id=1, source_target_pairs={{0,12},{2,14},{4,8},{6,10},{8,4},{10,6},{12,0},{14,2},{16,28},{18,... | collective-permute-start | bytes 221192 | tf_op jit(solution)/shard_map/ppermute | solution.py:50
  13.7 4.4 %collective-permute-start.3 = (f32[144,128]{1,0:T(8,128)S(1)}, f32[144,128]{1,0:T(8,128)S(1)}, u32[]{:S(2)}, u32[]{:S(2)}) collective-permute-start(f32[144,128]{1,0:T(8,128)S(1)} %get-tuple-element.24), channel_id=1, source_target_pairs={{0,8},{2,10},{4,12},{6,14},{8,0},{10,2},{12,4},{14,6},{16,24},{18,... | collective-permute-start | bytes 221192 | tf_op jit(solution)/shard_map/ppermute | solution.py:50
  18.0 5.3 %collective-permute-start.5 = (f32[144,128]{1,0:T(8,128)S(1)}, f32[144,128]{1,0:T(8,128)S(1)}, u32[]{:S(2)}, u32[]{:S(2)}) collective-permute-start(f32[144,128]{1,0:T(8,128)S(1)} %add_add_fusion), channel_id=1, source_target_pairs={{0,16},{2,18},{4,20},{6,22},{8,24},{10,26},{12,28},{14,30},{16,0},... | collective-permute-start | bytes 221192 | tf_op jit(solution)/shard_map/ppermute | solution.py:50
  23.4 5.5 %collective-permute-start.6 = (f32[144,128]{1,0:T(8,128)S(1)}, f32[144,128]{1,0:T(8,128)S(1)}, u32[]{:S(2)}, u32[]{:S(2)}) collective-permute-start(f32[144,128]{1,0:T(8,128)S(1)} %get-tuple-element.21), channel_id=1, source_target_pairs={{0,4},{2,6},{4,0},{6,2},{8,12},{10,14},{12,8},{14,10},{16,20},{18,... | collective-permute-start | bytes 221192 | tf_op jit(solution)/shard_map/ppermute | solution.py:50
  25.8 4.4 %collective-permute-start.7 = (f32[144,128]{1,0:T(8,128)S(1)}, f32[144,128]{1,0:T(8,128)S(1)}, u32[]{:S(2)}, u32[]{:S(2)}) collective-permute-start(f32[144,128]{1,0:T(8,128)S(1)} %get-tuple-element.21), channel_id=1, source_target_pairs={{0,8},{2,10},{4,12},{6,14},{8,0},{10,2},{12,4},{14,6},{16,24},{18,... | collective-permute-start | bytes 221192 | tf_op jit(solution)/shard_map/ppermute | solution.py:50
  26.4 5.3 %collective-permute-start.8 = (f32[144,128]{1,0:T(8,128)S(1)}, f32[144,128]{1,0:T(8,128)S(1)}, u32[]{:S(2)}, u32[]{:S(2)}) collective-permute-start(f32[144,128]{1,0:T(8,128)S(1)} %get-tuple-element.21), channel_id=1, source_target_pairs={{0,12},{2,14},{4,8},{6,10},{8,4},{10,6},{12,0},{14,2},{16,28},{18,... | collective-permute-start | bytes 221192 | tf_op jit(solution)/shard_map/ppermute | solution.py:50
  31.6 1.6 %collective-permute-start.9 = (f32[576,128]{1,0:T(8,128)S(1)}, f32[576,128]{1,0:T(8,128)S(1)}, u32[]{:S(2)}, u32[]{:S(2)}) collective-permute-start(f32[576,128]{1,0:T(8,128)S(1)} %constant_dynamic-update-slice_fusion.8), channel_id=1, source_target_pairs={{0,2},{2,0},{4,6},{6,4},{8,10},{10,8},{12,14},{14,12},{16,18},{18,... | collective-permute-start | bytes 884744 | tf_op jit(solution)/shard_map/ppermute | solution.py:50
  33.7 4.3 %collective-permute-start.10 = (f32[128,128]{1,0:T(8,128)S(1)}, f32[128,128]{1,0:T(8,128)S(1)}, u32[]{:S(2)}, u32[]{:S(2)}) collective-permute-start(f32[128,128]{1,0:T(8,128)S(1)} %weigh.1.refs_0_), channel_id=1, source_target_pairs={{0,1},{1,0},{2,3},{3,2},{4,5},{5,4},{6,7},{7,6},{8,9},{9,8},{10,11... | collective-permute-start | bytes 196616 | tf_op jit(solution)/shard_map/ppermute | solution.py:50
  38.5 3.4 %collective-permute-start.11 = (f32[512,128]{1,0:T(8,128)S(1)}, f32[512,128]{1,0:T(8,128)S(1)}, u32[]{:S(2)}, u32[]{:S(2)}) collective-permute-start(f32[512,128]{1,0:T(8,128)S(1)} %constant_dynamic-slice_fusion.3), channel_id=1, source_target_pairs={{0,2},{2,0},{4,6},{6,4},{8,10},{10,8},{12,14},{14,12},{16,18},{18,... | collective-permute-start | bytes 786440 | tf_op jit(solution)/shard_map/ppermute | solution.py:50
  39.7 4.7 %collective-permute-start.12 = (f32[128,128]{1,0:T(8,128)S(1)}, f32[128,128]{1,0:T(8,128)S(1)}, u32[]{:S(2)}, u32[]{:S(2)}) collective-permute-start(f32[128,128]{1,0:T(8,128)S(1)} %fusion), channel_id=1, source_target_pairs={{0,1},{1,0},{2,3},{3,2},{4,5},{5,4},{6,7},{7,6},{8,9},{9,8},{10,11... | collective-permute-start | bytes 196616 | tf_op jit(solution)/shard_map/ppermute | solution.py:50
  41.3 23.2 %collective-permute-start.13 = (f32[1152,128]{1,0:T(8,128)S(1)}, f32[1152,128]{1,0:T(8,128)S(1)}, u32[]{:S(2)}, u32[]{:S(2)}) collective-permute-start(f32[1152,128]{1,0:T(8,128)S(1)} %constant_dynamic-update-slice_fusion.6.left_ref.refs_0_), channel_id=1, source_target_pairs={{0,1},{1,0},{2,3},{3,2},{4,5},{5,4},{6,7},{7,6},{8,9},{9,8},{10,11... | collective-permute-start | bytes 1769480 | tf_op jit(solution)/shard_map/ppermute | solution.py:50
  44.5 6.2 %collective-permute-start.14 = (f32[128,128]{1,0:T(8,128)S(1)}, f32[128,128]{1,0:T(8,128)S(1)}, u32[]{:S(2)}, u32[]{:S(2)}) collective-permute-start(f32[128,128]{1,0:T(8,128)S(1)} %get-tuple-element.25), channel_id=1, source_target_pairs={{0,4},{2,6},{4,0},{6,2},{8,12},{10,14},{12,8},{14,10},{16,20},{18,... | collective-permute-start | bytes 196616 | tf_op jit(solution)/shard_map/ppermute | solution.py:50
  45.6 5.2 %collective-permute-start.16 = (f32[128,128]{1,0:T(8,128)S(1)}, f32[128,128]{1,0:T(8,128)S(1)}, u32[]{:S(2)}, u32[]{:S(2)}) collective-permute-start(f32[128,128]{1,0:T(8,128)S(1)} %get-tuple-element.26), channel_id=1, source_target_pairs={{0,12},{2,14},{4,8},{6,10},{8,4},{10,6},{12,0},{14,2},{16,28},{18,... | collective-permute-start | bytes 196616 | tf_op jit(solution)/shard_map/ppermute | solution.py:50
  47.8 4.3 %collective-permute-start.15 = (f32[128,128]{1,0:T(8,128)S(1)}, f32[128,128]{1,0:T(8,128)S(1)}, u32[]{:S(2)}, u32[]{:S(2)}) collective-permute-start(f32[128,128]{1,0:T(8,128)S(1)} %get-tuple-element.27), channel_id=1, source_target_pairs={{0,8},{2,10},{4,12},{6,14},{8,0},{10,2},{12,4},{14,6},{16,24},{18,... | collective-permute-start | bytes 196616 | tf_op jit(solution)/shard_map/ppermute | solution.py:50
  52.1 5.9 %collective-permute-start.17 = (f32[128,128]{1,0:T(8,128)S(1)}, f32[128,128]{1,0:T(8,128)S(1)}, u32[]{:S(2)}, u32[]{:S(2)}) collective-permute-start(f32[128,128]{1,0:T(8,128)S(1)} %add_add_fusion.1.refs_0_), channel_id=1, source_target_pairs={{0,16},{2,18},{4,20},{6,22},{8,24},{10,26},{12,28},{14,30},{16,0},... | collective-permute-start | bytes 196616 | tf_op jit(solution)/shard_map/ppermute | solution.py:50
  58.3 6.0 %collective-permute-start.20 = (f32[128,128]{1,0:T(8,128)S(1)}, f32[128,128]{1,0:T(8,128)S(1)}, u32[]{:S(2)}, u32[]{:S(2)}) collective-permute-start(f32[128,128]{1,0:T(8,128)S(1)} %turn.1), channel_id=1, source_target_pairs={{0,12},{2,14},{4,8},{6,10},{8,4},{10,6},{12,0},{14,2},{16,28},{18,... | collective-permute-start | bytes 196616 | tf_op jit(solution)/shard_map/ppermute | solution.py:50
  58.7 5.6 %collective-permute-start.19 = (f32[128,128]{1,0:T(8,128)S(1)}, f32[128,128]{1,0:T(8,128)S(1)}, u32[]{:S(2)}, u32[]{:S(2)}) collective-permute-start(f32[128,128]{1,0:T(8,128)S(1)} %turn.1), channel_id=1, source_target_pairs={{0,8},{2,10},{4,12},{6,14},{8,0},{10,2},{12,4},{14,6},{16,24},{18,... | collective-permute-start | bytes 196616 | tf_op jit(solution)/shard_map/ppermute | solution.py:50
  59.2 5.0 %collective-permute-start.18 = (f32[128,128]{1,0:T(8,128)S(1)}, f32[128,128]{1,0:T(8,128)S(1)}, u32[]{:S(2)}, u32[]{:S(2)}) collective-permute-start(f32[128,128]{1,0:T(8,128)S(1)} %turn.1), channel_id=1, source_target_pairs={{0,4},{2,6},{4,0},{6,2},{8,12},{10,14},{12,8},{14,10},{16,20},{18,... | collective-permute-start | bytes 196616 | tf_op jit(solution)/shard_map/ppermute | solution.py:50
  64.4 2.1 %collective-permute-start.21 = (f32[512,128]{1,0:T(8,128)S(1)}, f32[512,128]{1,0:T(8,128)S(1)}, u32[]{:S(2)}, u32[]{:S(2)}) collective-permute-start(f32[512,128]{1,0:T(8,128)S(1)} %constant_dynamic-update-slice_fusion.2), channel_id=1, source_target_pairs={{0,2},{2,0},{4,6},{6,4},{8,10},{10,8},{12,14},{14,12},{16,18},{18,... | collective-permute-start | bytes 786440 | tf_op jit(solution)/shard_map/ppermute | solution.py:50
